TPU v7x, 256 devices: a whole 4x4x8 slice. The times are simulated.
256 devices in a mesh: task: 128 (over x, y, z), shard: 2 (over core).
Axes of the slice: x: 4, y: 4, z: 8, core: 2. Of those that a mesh axis runs over, the one named last changes fastest.
Arguments:
- tokens: bfloat16 [128, 512, 1024], P('task'), may hold values from -6 to 6
- targets: bfloat16 [128, 512, 1024], P('task'), may hold values from -6 to 6
- meta_tokens: bfloat16 [128, 512, 1024], P('task'), may hold values from -6 to 6
- meta_targets: bfloat16 [128, 512, 1024], P('task'), may hold values from -6 to 6
- gate_weight: bfloat16 [128, 1024, 1536], P('task', None, 'shard'), may hold values from -0.1875 to 0.1875
- up_weight: bfloat16 [128, 1024, 1536], P('task', None, 'shard'), may hold values from -0.1875 to 0.1875
- down_weight: bfloat16 [128, 1536, 1024], P('task', 'shard'), may hold values from -0.15625 to 0.15625
- task_step: int32 [128], P('task'), may hold values from 0 to 9999
- hidden_state: float32 [128, 3, 512], P('task'), may hold values from -3 to 3
- cell_state: float32 [128, 3, 512], P('task'), may hold values from -6 to 6
- recurrent_weight: float32 [512, 2048], P('task'), may hold values from -0.25 to 0.25
- input_weight: float32 [3, 2048], replicated, may hold values from -3.5 to 3.5
- lstm_bias: float32 [2048], replicated, may hold values from -3 to 3
- context_weight: float32 [512, 5], replicated, may hold values from -0.25 to 0.25
- mlp_weight: float32 [3, 4], replicated, may hold values from -4 to 4
Outputs:
- gate_update: bfloat16 [128, 1024, 1536], P('task', None, 'shard')
- up_update: bfloat16 [128, 1024, 1536], P('task', None, 'shard')
- down_update: bfloat16 [128, 1536, 1024], P('task', 'shard')
- new_hidden: float32 [128, 3, 512], P('task')
- new_cell: float32 [128, 3, 512], P('task')
- meta_loss: float32 [], replicated
All inputs are finite; a program needn't handle non-finite values.
Results may differ from a plain program's by a relative error of at most 0.0056.
Values sent between devices are 32-bit elements; how exact they have to be, the bound alone decides.
No kernel may reach another device: no remote copies, remote signals or barrier semaphores. Data moves between devices by JAX's collectives and lax.ppermute only.
A program may use at most 128 MiB of HBM per device.

v0:
```python
import functools

import jax
import jax.numpy as jnp
from jax import lax
from jax.sharding import Mesh
from jax.sharding import PartitionSpec as P

STEPS = 10000
TASK = ("task_0", "task_1", "task_2")


highest = lax.Precision.HIGHEST
epsilon = 1e-06
rate_factor = 0.1


def sent_to_all(array, axis):
    length = lax.axis_size(axis)
    return lax.all_to_all(
        jnp.broadcast_to(array[None], (length, *array.shape)), axis, 0, 0, tiled=True
    )


def taken_together(array, axis):
    everything = sent_to_all(array, axis)
    return jnp.sum(everything, axis=0)


def joined_along(parts, dim):
    parts = jnp.moveaxis(parts, 0, dim)
    lengths = parts.shape
    return parts.reshape(*lengths[:dim], lengths[dim] * lengths[dim + 1], *lengths[dim + 2 :])


def gather_in_order(array, axes, order):
    parts = array[None]
    for k in order:
        parts = lax.all_gather(parts, axes[k], axis=0, tiled=True)
    held = [lax.axis_size(axes[k]) for k in reversed(order)]
    parts = parts.reshape(*held, *array.shape)
    turned = sorted(range(len(order)), key=lambda place: order[len(order) - 1 - place])
    return parts.transpose(*turned, *range(len(order), parts.ndim)).reshape(-1, *array.shape)


def gathered_by_axis(array, axes, order, dim):
    return joined_along(gather_in_order(array, axes, order), dim)


def one_axis_at_a_time(array, axes):
    return functools.reduce(lax.psum, axes, array)


def block_forward(inputs, w_gate, w_up, w_down):
    gate_pre = jnp.dot(inputs, w_gate, preferred_element_type=jnp.float32)
    up_pre = jnp.dot(inputs, w_up, preferred_element_type=jnp.float32)
    sigmoid_gate = jax.nn.sigmoid(gate_pre)
    activated = (gate_pre * sigmoid_gate * up_pre).astype(jnp.bfloat16)
    output = jnp.dot(activated, w_down, preferred_element_type=jnp.float32)
    return (gate_pre, up_pre, sigmoid_gate, activated, output)


def block_grads(inputs, w_down, gate_pre, up_pre, sigmoid_gate, activated, d_out):
    d_act = lax.dot_general(
        d_out, w_down, (((1,), (1,)), ((), ())), preferred_element_type=jnp.float32
    )
    d_gate = (d_act * up_pre * sigmoid_gate * (1.0 + gate_pre * (1.0 - sigmoid_gate))).astype(
        jnp.bfloat16
    )
    d_up = (d_act * gate_pre * sigmoid_gate).astype(jnp.bfloat16)
    grad_gate = lax.dot_general(
        inputs, d_gate, (((0,), (0,)), ((), ())), preferred_element_type=jnp.float32
    )
    grad_up = lax.dot_general(
        inputs, d_up, (((0,), (0,)), ((), ())), preferred_element_type=jnp.float32
    )
    grad_down = lax.dot_general(
        activated, d_out, (((0,), (0,)), ((), ())), preferred_element_type=jnp.float32
    )
    return (grad_gate, grad_up, grad_down)


def lstm_step(features, recurrent_term, cell_old, input_weight, lstm_bias, context_weight):
    state_width = cell_old.shape[-1]
    lstm_in = jnp.dot(features, input_weight, precision=highest) + recurrent_term + lstm_bias
    in_gate = jax.nn.sigmoid(lstm_in[:, :state_width])
    forget_gate = jax.nn.sigmoid(lstm_in[:, state_width : 2 * state_width])
    candidate = jnp.tanh(lstm_in[:, 2 * state_width : 3 * state_width])
    out_gate = jax.nn.sigmoid(lstm_in[:, 3 * state_width :])
    cell_new = forget_gate * cell_old + in_gate * candidate
    hidden_new = out_gate * jnp.tanh(cell_new)
    context = jnp.dot(hidden_new, context_weight, precision=highest)
    return (hidden_new, cell_new, context)


def param_update(param, gradient, rms_param, rms_grad, context_row, mlp_weight):
    p_norm = param.astype(jnp.float32) / rms_param
    g_norm = gradient / rms_grad
    summed = jnp.zeros(param.shape, jnp.float32)
    for hidden_unit in range(mlp_weight.shape[1]):
        inner = (
            mlp_weight[0, hidden_unit] * p_norm
            + mlp_weight[1, hidden_unit] * g_norm
            + context_row[hidden_unit]
        )
        summed = summed + mlp_weight[2, hidden_unit] * jax.nn.relu(inner)
    update = jnp.exp(context_row[-1]) * summed
    new_param = (param.astype(jnp.float32) - rate_factor * rms_param * update).astype(jnp.bfloat16)
    return (update.astype(jnp.bfloat16), new_param)


def local(
    tokens,
    targets,
    meta_tokens,
    meta_targets,
    gate_weight,
    up_weight,
    down_weight,
    task_step,
    hidden_state,
    cell_state,
    recurrent_weight,
    input_weight,
    lstm_bias,
    context_weight,
    mlp_weight,
):
    inputs = tokens[0]
    wanted = targets[0]
    meta_in = meta_tokens[0]
    meta_want = meta_targets[0]
    params = (gate_weight[0], up_weight[0], down_weight[0])
    gate_pre, up_pre, sigmoid_gate, activated, partial_out = block_forward(
        inputs, params[0], params[1], params[2]
    )
    output = taken_together(partial_out, "shard")
    d_out = (output - wanted.astype(jnp.float32)).astype(jnp.bfloat16)
    gradients = block_grads(inputs, params[2], gate_pre, up_pre, sigmoid_gate, activated, d_out)
    grad_sq = jnp.stack([jnp.sum(grad_piece * grad_piece) for grad_piece in gradients])
    param_sq = jnp.stack(
        [jnp.sum(jnp.square(param_piece.astype(jnp.float32))) for param_piece in params]
    )
    tensor_sums = lax.psum(jnp.stack([grad_sq, param_sq]), "shard")
    entries = float(params[0].size * lax.axis_size("shard"))
    rms_grad = jnp.sqrt(tensor_sums[0] / entries + epsilon)
    rms_param = jnp.sqrt(tensor_sums[1] / entries + epsilon)
    fraction = jnp.full((3,), task_step[0].astype(jnp.float32) / STEPS, jnp.float32)
    features = jnp.stack([jnp.log(rms_grad), jnp.log(rms_param), fraction], axis=1)
    hidden_old = hidden_state[0]
    recurrent_term = jnp.dot(
        hidden_old, gathered_by_axis(recurrent_weight, TASK, (0, 1, 2), 0), precision=highest
    )
    hidden_new, cell_new, context = lstm_step(
        features, recurrent_term, cell_state[0], input_weight, lstm_bias, context_weight
    )
    results = [
        param_update(
            params[tensor_id],
            gradients[tensor_id],
            rms_param[tensor_id],
            rms_grad[tensor_id],
            context[tensor_id],
            mlp_weight,
        )
        for tensor_id in range(3)
    ]
    meta_partial = block_forward(meta_in, results[0][1], results[1][1], results[2][1])[4]
    loss_scale = 0.5 / (meta_want.shape[0] * meta_want.shape[1])
    meta_out = taken_together(meta_partial, "shard")
    meta_part = loss_scale * jnp.sum(jnp.square(meta_out - meta_want.astype(jnp.float32)))
    summed = one_axis_at_a_time(meta_part, TASK)
    meta_loss = summed / lax.axis_size(TASK)
    return (
        results[0][0][None],
        results[1][0][None],
        results[2][0][None],
        hidden_new[None],
        cell_new[None],
        meta_loss,
    )


def solution(mesh):
    finer = Mesh(
        mesh.devices.reshape(4, 4, 8, mesh.shape["shard"]), ("task_0", "task_1", "task_2", "shard")
    )
    return jax.shard_map(
        local,
        mesh=finer,
        in_specs=(
            P(TASK, None, None),
            P(TASK, None, None),
            P(TASK, None, None),
            P(TASK, None, None),
            P(TASK, None, "shard"),
            P(TASK, None, "shard"),
            P(TASK, "shard", None),
            P(TASK),
            P(TASK, None, None),
            P(TASK, None, None),
            P(TASK, None),
            P(),
            P(),
            P(),
            P(),
        ),
        out_specs=(
            P(TASK, None, "shard"),
            P(TASK, None, "shard"),
            P(TASK, "shard", None),
            P(TASK, None, None),
            P(TASK, None, None),
            P(),
        ),
        check_vma=False,
    )
```

profile of v0, /device:TPU:32, one launch (start us, length us, event | category | flops | bytes accessed | tf_op | source)
XLA Modules:
  0.0 232.8 jit_solution(13789234758017045377)
XLA Ops:
  7.2 12.7 %all-gather.1 = f32[4,4,2048]{2,1,0:T(4,128)S(1)} all-gather(f32[1,4,2048]{2,1,0:T(4,128)} %bitcast.281), channel_id=2, replica_groups=mesh['task_0'=4,'task_1'=4,'task_2'=8,'shard'=2] {'task_0'}, dimensions={0}, use_global_device_ids=true | all-gather | bytes 163840 | tf_op jit(solution)/shard_map/all_gather | solution.py:39
  19.9 14.4 %all_gather.10 = f32[16,4,2048]{2,1,0:T(4,128)} all-gather(f32[4,4,2048]{2,1,0:T(4,128)S(1)} %all-gather.1), channel_id=1, replica_groups=mesh['task_0'=4,'task_1'=4,'task_2'=8,'shard'=2] {'task_1'}, dimensions={0}, use_global_device_ids=true | all-gather | bytes 655360 | tf_op jit(solution)/shard_map/all_gather | solution.py:39
  34.3 2.5 %fusion.52 = f32[512,768]{1,0:T(8,128)S(1)} fusion(bf16[1,1024,768]{2,1,0:T(8,128)(2,1)} %param.19, bf16[1,512,1024]{2,1,0:T(8,128)(2,1)S(1)} %copy-done), kind=kOutput, calls=%fused_computation.75 | convolution fusion | flops 805306368 | bytes 4194304 | tf_op jit(solution)/shard_map/dot_general | solution.py:55
  36.9 2.2 multiply_convert_fusion.2
  40.1 2.5 %broadcast_in_dim.31 = f32[2,512,1024]{2,1,0:T(8,128)} broadcast(f32[512,1024]{1,0:T(8,128)S(1)} %fusion.61), dimensions={1,2} | broadcast | bytes 6291456 | tf_op jit(solution)/shard_map/broadcast_in_dim | solution.py:21
  42.5 5.7 %all-to-all-start = ((f32[2,512,1024]{2,1,0:T(8,128)}), f32[2,512,1024]{2,1,0:T(8,128)}, u32[]{:S(2)}, u32[]{:S(2)}) async-start(f32[2,512,1024]{2,1,0:T(8,128)} %broadcast_in_dim.31), calls=%async_computation | async-start | bytes 8388608 | tf_op jit(solution)/shard_map/all_to_all | solution.py:20
  48.3 1.6 copy.45
  49.9 1.7 copy.46
  52.7 4.2 %reduce_sum.83 = f32[512,1024]{1,0:T(8,128)} reduce(f32[2,512,1024]{2,1,0:T(8,128)} %all-to-all-done, f32[]{:T(128)} %constant.31.clone.1), dimensions={0}, to_apply=%region_0.0 | reduce | flops 524288 | bytes 6291460 | tf_op jit(solution)/shard_map/reduce_sum | solution.py:27
  56.9 3.0 %fusion.4 = f32[]{:T(128)} fusion(bf16[1,768,1024]{2,1,0:T(8,128)(2,1)} %param.21), kind=kLoop, calls=%fused_computation.14 | loop fusion | flops 2359295 | bytes 1572868 | tf_op jit(solution)/shard_map/reduce_sum | solution.py:142
  60.0 2.9 %fusion = f32[]{:T(128)} fusion(bf16[1,1024,768]{1,2,0:T(8,128)(2,1)} %copy.45), kind=kLoop, calls=%fused_computation.10 | loop fusion | flops 2359295 | bytes 1572868 | tf_op jit(solution)/shard_map/reduce_sum | solution.py:142
  65.3 3.4 %multiply_reduce_fusion = (f32[]{:T(128)}, f32[768,1024]{1,0:T(8,128)}) fusion(bf16[512,768]{1,0:T(8,128)(2,1)S(1)} %get-tuple-element.75, f32[512,1024]{1,0:T(8,128)S(1)} %copy-done.3, bf16[1,512,1024]{2,1,0:T(8,128)(2,1)S(1)} %copy-done.9), kind=kOutput, calls=%fused_computation.57 | convolution fusion | flops 808452096 | bytes 7077892 | tf_op jit(solution)/shard_map/dot_general | solution.py:77
  68.7 3.3 %multiply_reduce_fusion.1 = (f32[]{:T(128)}, f32[768,1024]{1,0:T(8,128)}) fusion(bf16[1,512,1024]{2,1,0:T(8,128)(2,1)S(1)} %copy-done, f32[512,768]{1,0:T(8,128)S(1)} %fusion.59, f32[512,768]{1,0:T(8,128)S(1)} %copy-done.23), kind=kOutput, calls=%fused_computation.58 | convolution fusion | flops 809238528 | bytes 7340036 | tf_op jit(solution)/shard_map/dot_general | solution.py:74
  72.0 3.7 %multiply_reduce_fusion.2 = (f32[]{:T(128)}, f32[768,1024]{1,0:T(8,128)}) fusion(bf16[1,512,1024]{2,1,0:T(8,128)(2,1)S(1)} %copy-done, f32[512,768]{1,0:T(8,128)S(1)} %copy-done.23, f32[512,768]{1,0:T(8,128)S(1)} %fusion.59, f32[512,768]{1,0:T(8,128)S(1)} %copy-done.24), kind=kOutput, calls=%fused_computation.59 | convolution fusion | flops 810811392 | bytes 8912900 | tf_op jit(solution)/shard_map/dot_general | solution.py:71
  75.7 3.8 %maximum_bitcast_fusion = (f32[1,3]{1,0:T(1,128)S(1)}, f32[1,3]{1,0:T(1,128)S(1)}) fusion(f32[1]{0:T(128)} %bitcast.9, f32[1]{0:T(128)} %bitcast.7, f32[1]{0:T(128)} %bitcast.6, f32[1]{0:T(128)} %bitcast.13, f32[1]{0:T(128)} %bitcast.12, f32[1]{0:T(128)} %bitcast.11), kind=kLoop, calls=%fused_computation.136 | loop fusion | flops 12 | bytes 48 | tf_op jit(solution)/shard_map/stack | solution.py:144
  79.5 2.7 %psum.28 = f32[2,3]{1,0:T(2,128)S(1)} all-reduce(f32[2,3]{1,0:T(2,128)S(1)} %pad_maximum_fusion), channel_id=1, replica_groups=mesh['task_0'=4,'task_1'=4,'task_2'=8,'shard'=2] {'shard'}, use_global_device_ids=true, to_apply=%region_7.0 | all-reduce | flops 6 | bytes 48 | tf_op jit(solution)/shard_map/psum | solution.py:144
  88.4 4.8 %copy.65 = f32[8,4,4,4,2048]{4,3,0,1,2:T(4,128)} copy(f32[8,4,4,4,2048]{4,3,2,1,0:T(4,128)} %bitcast.279) | data formatting | bytes 8388608 | tf_op jit(solution)/shard_map/reshape | solution.py:41
  93.1 5.3 %reshape_reshape.3 = f32[512,2048]{1,0:T(8,128)} reshape(f32[4,4,8,4,2048]{4,3,2,1,0:T(4,128)} %bitcast.278) | data formatting | bytes 8388608 | tf_op jit(solution)/shard_map/reshape;reshape | solution.py:33
  98.5 4.4 %fusion.38 = f32[3,2048]{1,0:T(4,128)S(1)} fusion(f32[3,2048]{1,0:T(4,128)S(1)} %fusion.99, f32[512,2048]{1,0:T(8,128)} %reshape_reshape.3, f32[2048]{0:T(1024)S(1)} %copy-done.20, f32[1,3,512]{2,0,1:T(1,128)S(1)} %copy-done.19), kind=kOutput, calls=%fused_computation.63 | convolution fusion | flops 37761024 | bytes 4257792 | tf_op jit(solution)/shard_map/dot_general | solution.py:151
  106.4 15.6 %convert_bitcast_fusion.2 = (bf16[1,1024,768]{1,2,0:T(8,128)(2,1)}, f32[1024,768]{0,1:T(8,128)S(1)}) fusion(f32[]{:T(128)} %bitcast.55, f32[]{:T(128)} %bitcast.41, f32[]{:T(128)} %bitcast.40, f32[]{:T(128)} %bitcast.39, f32[]{:T(128)} %bitcast.53, f32[]{:T(128)} %bitcast.36, f32[]{:T(128)} %bitcast.35, f32[]{:T(128)} %bitcast.34, f32[]{:T(128)} %bitcast.51, ...), kind=kLoop, calls=%fused_computation.95 | loop fusion | flops 25165824 | bytes 9437260 | tf_op jit(solution)/shard_map/broadcast_in_dim | solution.py:176
  122.0 2.2 fusion.46
  124.9 16.5 %convert_bitcast_fusion.1 = (bf16[1,768,1024]{2,1,0:T(8,128)(2,1)}, f32[768,1024]{1,0:T(8,128)}) fusion(f32[]{:T(128)} %bitcast.63, f32[]{:T(128)} %bitcast.41, f32[]{:T(128)} %bitcast.40, f32[]{:T(128)} %bitcast.39, f32[]{:T(128)} %bitcast.62, f32[]{:T(128)} %bitcast.36, f32[]{:T(128)} %bitcast.35, f32[]{:T(128)} %bitcast.34, f32[]{:T(128)} %bitcast.61, ...), kind=kLoop, calls=%fused_computation.94 | loop fusion | flops 25165824 | bytes 9437260 | tf_op jit(solution)/shard_map/broadcast_in_dim | solution.py:177
  141.4 16.0 %convert_bitcast_fusion.3 = (bf16[1,1024,768]{1,2,0:T(8,128)(2,1)}, f32[1024,768]{0,1:T(8,128)}) fusion(f32[]{:T(128)} %bitcast.43, f32[]{:T(128)} %bitcast.41, f32[]{:T(128)} %bitcast.40, f32[]{:T(128)} %bitcast.39, f32[]{:T(128)} %bitcast.38, f32[]{:T(128)} %bitcast.36, f32[]{:T(128)} %bitcast.35, f32[]{:T(128)} %bitcast.34, f32[]{:T(128)} %bitcast.33, ...), kind=kLoop, calls=%fused_computation.96 | loop fusion | flops 25165824 | bytes 9437260 | tf_op jit(solution)/shard_map/broadcast_in_dim | solution.py:175
  157.5 7.5 %fusion.44 = f32[512,1024]{1,0:T(8,128)} fusion(f32[768,1024]{1,0:T(8,128)} %get-tuple-element.31, bf16[1,768,1024]{2,1,0:T(8,128)(2,1)} %param.21, f32[]{:T(128)S(6)} %mul.395, f32[768,512]{0,1:T(8,128)} %fusion.46, bf16[1,512,1024]{2,1,0:T(8,128)(2,1)S(1)} %copy-done.15, f32[1024,768]{0,1:T(8,128)} %get-tuple-element.35, ...), kind=kOutput, calls=%fused_computation.70 | convolution fusion | flops 1619263488 | bytes 14155784 | tf_op jit(solution)/shard_map/dot_general | solution.py:59
  165.0 2.3 broadcast_in_dim.38
  167.3 8.2 %all_to_all.10 = f32[2,512,1024]{2,1,0:T(8,128)} all-to-all(f32[2,512,1024]{2,1,0:T(8,128)S(1)} %broadcast_in_dim.38), channel_id=1, replica_groups=mesh['task_0'=4,'task_1'=4,'task_2'=8,'shard'=2] {'shard'}, dimensions={0} | all-to-all | bytes 8388608 | tf_op jit(solution)/shard_map/all_to_all | solution.py:20
  175.5 2.9 %reduce_sum.91 = f32[512,1024]{1,0:T(8,128)S(1)} reduce(f32[2,512,1024]{2,1,0:T(8,128)} %all_to_all.10, f32[]{:T(128)} %constant.31.clone.1), dimensions={0}, to_apply=%region_8.9 | reduce | flops 524288 | bytes 6291460 | tf_op jit(solution)/shard_map/reduce_sum | solution.py:27
  180.9 10.9 %psum.29 = f32[]{:T(128)} all-reduce(f32[]{:T(128)S(6)} %mul_shard_map.3), channel_id=1, replica_groups=mesh['task_0'=4,'task_1'=4,'task_2'=8,'shard'=2] {'task_0'}, use_global_device_ids=true, to_apply=%region_10.11 | all-reduce | flops 1 | bytes 8 | tf_op jit(solution)/shard_map/psum | solution.py:51
  191.8 2.7 %copy.51 = bf16[1,1024,768]{2,1,0:T(8,128)(2,1)} copy(bf16[1,1024,768]{1,2,0:T(8,128)(2,1)} %get-tuple-element.32) | data formatting | bytes 3145728
  194.5 11.1 %psum.30 = f32[]{:T(128)} all-reduce(f32[]{:T(128)} %psum.29), channel_id=1, replica_groups=mesh['task_0'=4,'task_1'=4,'task_2'=8,'shard'=2] {'task_1'}, use_global_device_ids=true, to_apply=%region_11.12 | all-reduce | flops 1 | bytes 8 | tf_op jit(solution)/shard_map/psum | solution.py:51
  205.6 1.6 copy.50
  207.1 17.0 %psum.31 = f32[]{:T(128)} all-reduce(f32[]{:T(128)} %psum.30), channel_id=1, replica_groups=mesh['task_0'=4,'task_1'=4,'task_2'=8,'shard'=2] {'task_2'}, use_global_device_ids=true, to_apply=%region_12.13 | all-reduce | flops 1 | bytes 8 | tf_op jit(solution)/shard_map/psum | solution.py:51
  (70 shorter events, 12.4 us)
Async XLA Ops:
  7.2 27.2 %copy-start = (bf16[1,512,1024]{2,1,0:T(8,128)(2,1)S(1)}, bf16[1,512,1024]{2,1,0:T(8,128)(2,1)}, u32[]{:S(2)}) copy-start(bf16[1,512,1024]{2,1,0:T(8,128)(2,1)} %param.15) | copy-start | bytes 3145732
  7.2 81.2 %all-gather.4.cloned.1.call-start = ((), (), s32[]{:S(2)}) async-start(), calls=%async_computation.2 | async-start | bytes 4718592 | tf_op jit(solution)/shard_map/all_gather | solution.py:39
  34.3 2.5 %copy-start.13 = (bf16[1,1024,768]{2,1,0:T(8,128)(2,1)S(1)}, bf16[1,1024,768]{2,1,0:T(8,128)(2,1)}, u32[]{:S(2)}) copy-start(bf16[1,1024,768]{2,1,0:T(8,128)(2,1)} %param.20) | copy-start | bytes 4718596
  36.9 2.2 copy-start.22
  36.9 2.2 copy-start.5
  42.5 5.7 %copy-start.12 = (bf16[1,1024,768]{2,1,0:T(8,128)(2,1)S(1)}, bf16[1,1024,768]{2,1,0:T(8,128)(2,1)}, u32[]{:S(2)}) copy-start(bf16[1,1024,768]{2,1,0:T(8,128)(2,1)} %param.19) | copy-start | bytes 4718596
  42.5 10.2 %all-to-all-start = ((f32[2,512,1024]{2,1,0:T(8,128)}), f32[2,512,1024]{2,1,0:T(8,128)}, u32[]{:S(2)}, u32[]{:S(2)}) async-start(f32[2,512,1024]{2,1,0:T(8,128)} %broadcast_in_dim.31), calls=%async_computation | async-start | bytes 8388608 | tf_op jit(solution)/shard_map/all_to_all | solution.py:20
  56.9 7.3 %copy-start.3 = (f32[512,1024]{1,0:T(8,128)S(1)}, f32[512,1024]{1,0:T(8,128)}, u32[]{:S(2)}) copy-start(f32[512,1024]{1,0:T(8,128)} %reduce_sum.83) | copy-start | bytes 6291460
  56.9 7.3 %copy-start.6 = (bf16[1,768,1024]{2,1,0:T(8,128)(2,1)S(1)}, bf16[1,768,1024]{2,1,0:T(8,128)(2,1)}, u32[]{:S(2)}) copy-start(bf16[1,768,1024]{2,1,0:T(8,128)(2,1)} %param.21) | copy-start | bytes 4718596
  56.9 7.3 %copy-start.9 = (bf16[1,512,1024]{2,1,0:T(8,128)(2,1)S(1)}, bf16[1,512,1024]{2,1,0:T(8,128)(2,1)}, u32[]{:S(2)}) copy-start(bf16[1,512,1024]{2,1,0:T(8,128)(2,1)} %param.16) | copy-start | bytes 3145732
  65.3 3.4 %copy-start.23 = (f32[512,768]{1,0:T(8,128)S(1)}, f32[512,768]{1,0:T(8,128)}, u32[]{:S(2)}) copy-start(f32[512,768]{1,0:T(8,128)} %copy-done.22) | copy-start | bytes 4718596
  68.7 3.3 %copy-start.24 = (f32[512,768]{1,0:T(8,128)S(1)}, f32[512,768]{1,0:T(8,128)}, u32[]{:S(2)}) copy-start(f32[512,768]{1,0:T(8,128)} %get-tuple-element.76) | copy-start | bytes 4718596
  72.0 14.0 %copy-start.17 = (f32[3,4]{1,0:T(4,128)S(1)}, f32[3,4]{1,0:T(4,128)}, u32[]{:S(2)}) copy-start(f32[3,4]{1,0:T(4,128)} %param.29) | copy-start | bytes 148
  72.0 14.7 %copy-start.16 = (f32[3,2048]{1,0:T(4,128)S(1)}, f32[3,2048]{1,0:T(4,128)}, u32[]{:S(2)}) copy-start(f32[3,2048]{1,0:T(4,128)} %param.26) | copy-start | bytes 73732
  93.1 5.3 %copy-start.19 = (f32[1,3,512]{2,0,1:T(1,128)S(1)}, f32[1,3,512]{2,0,1:T(1,128)}, u32[]{:S(2)}) copy-start(f32[1,3,512]{2,0,1:T(1,128)} %param.23) | copy-start | bytes 18436
  93.1 5.3 %copy-start.20 = (f32[2048]{0:T(1024)S(1)}, f32[2048]{0:T(1024)}, u32[]{:S(2)}) copy-start(f32[2048]{0:T(1024)} %param.27) | copy-start | bytes 24580
  98.4 4.4 %copy-start.21 = (f32[1,3,512]{2,0,1:T(1,128)S(1)}, f32[1,3,512]{2,0,1:T(1,128)}, u32[]{:S(2)}) copy-start(f32[1,3,512]{2,0,1:T(1,128)} %param.24) | copy-start | bytes 18436
  98.5 5.1 %copy-start.18 = (f32[512,5]{0,1:T(8,128)S(1)}, f32[512,5]{0,1:T(8,128)}, u32[]{:S(2)}) copy-start(f32[512,5]{0,1:T(8,128)} %param.28) | copy-start | bytes 30724
  98.5 7.9 %copy-start.11 = (f32[768,1024]{1,0:T(8,128)S(1)}, f32[768,1024]{1,0:T(8,128)}, u32[]{:S(2)}) copy-start(f32[768,1024]{1,0:T(8,128)} %get-tuple-element.80) | copy-start | bytes 9437188
  106.4 15.6 %copy-start.15 = (bf16[1,512,1024]{2,1,0:T(8,128)(2,1)S(1)}, bf16[1,512,1024]{2,1,0:T(8,128)(2,1)}, u32[]{:S(2)}) copy-start(bf16[1,512,1024]{2,1,0:T(8,128)(2,1)} %param.17) | copy-start | bytes 3145732
  122.0 2.3 copy-start.2
  122.0 2.9 %copy-start.7 = (bf16[1,768,1024]{2,1,0:T(8,128)(2,1)S(1)}, bf16[1,768,1024]{2,1,0:T(8,128)(2,1)}, u32[]{:S(2)}) copy-start(bf16[1,768,1024]{2,1,0:T(8,128)(2,1)} %param.21) | copy-start | bytes 4718596
  124.9 16.5 %copy-start.4 = (bf16[1,1024,768]{1,2,0:T(8,128)(2,1)S(1)}, bf16[1,1024,768]{1,2,0:T(8,128)(2,1)}, u32[]{:S(2)}) copy-start(bf16[1,1024,768]{1,2,0:T(8,128)(2,1)} %copy.45) | copy-start | bytes 4718596
  124.9 16.5 %copy-start.10 = (f32[768,1024]{1,0:T(8,128)S(1)}, f32[768,1024]{1,0:T(8,128)}, u32[]{:S(2)}) copy-start(f32[768,1024]{1,0:T(8,128)} %get-tuple-element.82) | copy-start | bytes 9437188
  175.5 2.9 %copy-start.14 = (bf16[1,512,1024]{2,1,0:T(8,128)(2,1)S(1)}, bf16[1,512,1024]{2,1,0:T(8,128)(2,1)}, u32[]{:S(2)}) copy-start(bf16[1,512,1024]{2,1,0:T(8,128)(2,1)} %param.18) | copy-start | bytes 3145732
  179.5 26.0 %copy-start.8 = (bf16[1,1024,768]{1,2,0:T(8,128)(2,1)S(1)}, bf16[1,1024,768]{1,2,0:T(8,128)(2,1)}, u32[]{:S(2)}) copy-start(bf16[1,1024,768]{1,2,0:T(8,128)(2,1)} %get-tuple-element.34) | copy-start | bytes 4718596
  191.8 33.0 %copy-start.1 = (bf16[1,512,1024]{2,1,0:T(8,128)(2,1)S(1)}, bf16[1,512,1024]{2,1,0:T(8,128)(2,1)}, u32[]{:S(2)}) copy-start(bf16[1,512,1024]{2,1,0:T(8,128)(2,1)} %param.15) | copy-start | bytes 3145732
Sparse Core Ops, SparseCore 0:
  34.4 53.8 all-gather.3
where the time goes:
time: 234 us; the launch traced here: 233 us
  blocking collectives  76.9 us (33%)
  other arithmetic  67.5 us (29%)
  matrix products  31.7 us (14%)
  local copies, waits for them, and re-layouts  27.2 us (12%)
  between operations  21.3 us (9%)
  starting transfers between devices  5.75 us (2%)
  waiting for transfers between devices  2.43 us (1%)
    psum x3, blocking collectives, one_axis_at_a_time(): return functools.reduce(lax.psum, axes, array)  39 us
    all_gather x2, blocking collectives, gather_in_order(): parts = lax.all_gather(parts, axes[k], axis=0, tiled=True)  27.1 us
    broadcast_in_dim x1, other arithmetic, local(): results[2][0][None]  16.5 us
    broadcast_in_dim x1, other arithmetic, local(): results[0][0][None]  16 us
    broadcast_in_dim x1, other arithmetic, local(): results[1][0][None]  15.6 us
    unnamed x56, local copies, waits for them, and re-layouts  9.55 us
    dot_general x2, matrix products, block_forward(): output = jnp.dot(activated, w_down, preferred_element_type=jnp.float32)  8.5 us
    all_to_all x1, blocking collectives, sent_to_all(): lax.all_to_all(jnp.broadcast_to(array[None], (length, *array.shape)), axi...  8.16 us
  transfers between devices with their start and end apart: 2, of which 2 were waited for; matrix products, arithmetic and copies ran while one was open for 17% of the time, Pallas kernels for 0%

commit v1 on v0

v1 whole, which is shorter than its diff:
```python
import functools

import jax
import jax.numpy as jnp
from jax import lax
from jax.experimental import pallas as pl
from jax.experimental.pallas import tpu as pltpu
from jax.sharding import Mesh
from jax.sharding import PartitionSpec as P


STEPS = 10000
X, Y, Z, SHARD = "task_0", "task_1", "task_2", "shard"
TASK = (X, Y, Z)

f32, bf16 = jnp.float32, jnp.bfloat16
highest = lax.Precision.HIGHEST
epsilon = 1e-06
rate_factor = 0.1
CHUNK = 256
MIB = 1 << 20


def dot(a, b):
    return jnp.dot(a, b, preferred_element_type=f32)


def dot_t(a, b):
    return lax.dot_general(a, b, (((1,), (1,)), ((), ())), preferred_element_type=f32)


def lane_sums(value):
    sums = jnp.sum(value, axis=0, keepdims=True)
    total = sums[:, :128]
    for start in range(128, sums.shape[1], 128):
        total = total + sums[:, start : start + 128]
    return total


def squares(value):
    value = value.astype(f32)
    return lane_sums(value * value)


def vmem(*shapes):
    return [pltpu.VMEM(shape, kind) for shape, kind in shapes]


IN_VMEM = pl.BlockSpec(memory_space=pltpu.VMEM)
IN_HBM = pl.BlockSpec(memory_space=pltpu.HBM)
IN_SMEM = pl.BlockSpec(memory_space=pltpu.SMEM)


def call(body, operands, specs, outs, out_specs, scratch=(), limit=8, flops=0):
    held = [pltpu.with_memory_space_constraint(a, pltpu.HBM) if spec is IN_HBM else a for a, spec in zip(operands, specs)]
    return pl.pallas_call(
        body,
        in_specs=specs,
        out_specs=out_specs,
        out_shape=outs,
        scratch_shapes=scratch,
        compiler_params=pltpu.CompilerParams(vmem_limit_bytes=limit * MIB),
        cost_estimate=pl.CostEstimate(flops=flops, transcendentals=0, bytes_accessed=0) if flops else None,
    )(*held)


def piece(j):
    return pl.ds(pl.multiple_of(j * CHUNK, CHUNK), CHUNK)


def forward_kernel(
    place_ref, x_hbm, wg_hbm, wu_hbm, wd_hbm, want_hbm, meta_hbm, meta_want_hbm,
    wg_ref, wu_ref, wd_ref, want_ref, meta_ref, meta_want_ref, out_ref, p_ref, q_ref, act_t_ref, x_t_ref, sq_ref,
    x_ref, sem_x, sem_w, sem_late,
):
    count = wg_ref.shape[1] // CHUNK
    half = meta_want_ref.shape[0]

    def weights(j):
        at = piece(j)
        return (
            pltpu.make_async_copy(wg_hbm.at[:, at], wg_ref.at[:, at], sem_w.at[0, j]),
            pltpu.make_async_copy(wu_hbm.at[:, at], wu_ref.at[:, at], sem_w.at[1, j]),
            pltpu.make_async_copy(wd_hbm.at[at, :], wd_ref.at[at, :], sem_w.at[2, j]),
        )

    mine = pl.ds(pl.multiple_of(place_ref[3] * half, half), half)
    late = (
        pltpu.make_async_copy(want_hbm, want_ref, sem_late.at[0]),
        pltpu.make_async_copy(meta_hbm, meta_ref, sem_late.at[1]),
        pltpu.make_async_copy(meta_want_hbm.at[mine, :], meta_want_ref, sem_late.at[2]),
    )
    first = pltpu.make_async_copy(x_hbm, x_ref, sem_x)
    first.start()
    for j in range(count):
        for copy in weights(j):
            copy.start()
    for copy in late:
        copy.start()
    sq_ref[...] = jnp.zeros_like(sq_ref)
    first.wait()

    def body(j, carry):
        at = piece(j)
        copies = weights(j)
        copies[0].wait()
        copies[1].wait()
        x = x_ref[...]
        gate = dot(x, wg_ref[:, at])
        up = dot(x, wu_ref[:, at])
        sig = jax.nn.sigmoid(gate)
        silu = gate * sig
        q_ref[:, at] = silu
        p_ref[:, at] = up * sig * (1.0 + gate * (1.0 - sig))
        act = (silu * up).astype(bf16)
        act_t_ref[at, :] = act.T
        copies[2].wait()
        part = dot(act, wd_ref[at, :])

        @pl.when(j == 0)
        def _():
            out_ref[...] = part
            x_t_ref[...] = x_ref[...].T

        @pl.when(j > 0)
        def _():
            out_ref[...] += part

        sq_ref[0:1, :] += squares(wg_ref[:, at])
        sq_ref[1:2, :] += squares(wu_ref[:, at])
        sq_ref[2:3, :] += squares(wd_ref[at, :])
        return carry

    lax.fori_loop(0, count, body, 0)
    for copy in late:
        copy.wait()


def forward(place, x, wg, wu, wd, want, meta, meta_want):
    tok, width = x.shape
    hid = wg.shape[1]
    outs = vmem(
        (wg.shape, bf16), (wu.shape, bf16), (wd.shape, bf16), (want.shape, bf16), (meta.shape, bf16),
        ((tok // 2, width), bf16), ((tok, width), f32), ((tok, hid), f32), ((tok, hid), f32),
        ((hid, tok), bf16), ((width, tok), bf16), ((8, 128), f32),
    )
    scratch = [
        pltpu.VMEM((tok, width), bf16),
        pltpu.SemaphoreType.DMA,
        pltpu.SemaphoreType.DMA((3, hid // CHUNK)),
        pltpu.SemaphoreType.DMA((3,)),
    ]
    return call(
        forward_kernel, (place, x, wg, wu, wd, want, meta, meta_want), [IN_SMEM] + [IN_HBM] * 7,
        outs, [IN_VMEM] * len(outs), scratch, 12, 6 * tok * width * hid,
    )


def backward_kernel(
    own_ref, recv_ref, want_ref, wd_ref, p_ref, q_ref, act_t_ref, x_t_ref, psq_ref, gg_ref, gu_ref, gd_ref, sq_ref, d_out_ref
):
    sq_ref[0:8, :] = jnp.zeros_like(psq_ref)
    sq_ref[8:16, :] = psq_ref[...]
    d_out_ref[...] = (own_ref[...] + recv_ref[...] - want_ref[...].astype(f32)).astype(bf16)

    def body(j, carry):
        at = piece(j)
        d_out = d_out_ref[...]
        d_act = dot_t(d_out, wd_ref[at, :])
        dg = (d_act * p_ref[:, at]).astype(bf16)
        du = (d_act * q_ref[:, at]).astype(bf16)
        x_t = x_t_ref[...]
        grad = dot(x_t, dg)
        gg_ref[:, at] = grad
        sq_ref[0:1, :] += squares(grad)
        grad = dot(x_t, du)
        gu_ref[:, at] = grad
        sq_ref[1:2, :] += squares(grad)
        grad = dot(act_t_ref[at, :], d_out)
        gd_ref[at, :] = grad
        sq_ref[2:3, :] += squares(grad)
        return carry

    lax.fori_loop(0, wd_ref.shape[0] // CHUNK, body, 0)


def backward(own, recv, want, wd, p, q, act_t, x_t, param_sq):
    tok, width = own.shape
    hid = wd.shape[0]
    outs = vmem(((width, hid), f32), ((width, hid), f32), ((hid, width), f32), ((16, 128), f32))
    return call(
        backward_kernel, (own, recv, want, wd, p, q, act_t, x_t, param_sq), [IN_VMEM] * 9,
        outs, [IN_VMEM] * 4, [pltpu.VMEM((tok, width), bf16)], 12, 8 * tok * width * hid,
    )


def recurrent_kernel(place_ref, own, h0, h1, h2, h3, r0, r1, r2, r3, o0, o1, o2, o3, stack):
    px, py, pz, core = place_ref[0], place_ref[1], place_ref[2], place_ref[3]
    state = own.shape[2]
    stack[...] = jnp.zeros_like(stack)
    for j in range(own.shape[0]):
        stack[j : j + 1, :] = jnp.where(core == 0, own[j], h0[j])
        stack[8 + j : 9 + j, :] = h1[j]
        stack[16 + j : 17 + j, :] = h2[j]
        stack[24 + j : 25 + j, :] = h3[j]
    shape = (state, 128)
    row = lax.broadcasted_iota(jnp.int32, shape, 0)
    col = lax.broadcasted_iota(jnp.int32, shape, 1)
    step, block, inner = col >> 4, (col >> 2) & 3, col & 3
    pick = (((px + block) & 3) << 7) + (((py + step) & 3) << 5) + (pz << 2) + inner
    chosen = (row == pick).astype(f32)
    hidden = jnp.dot(stack[...], chosen, precision=highest, preferred_element_type=f32)
    total = None
    for k, r_ref in enumerate((r0, r1, r2, r3)):
        term = jnp.dot(hidden[:, 16 * k : 16 * k + 16], r_ref[...], precision=highest, preferred_element_type=f32)
        total = term if total is None else total + term
    for k, out_ref in enumerate((o0, o1, o2, o3)):
        out_ref[...] = total[8 * k : 8 * k + 3]


def shifted(array, axis, shift):
    size = lax.axis_size(axis)
    return lax.ppermute(array, axis, [((i + shift) % size, i) for i in range(size)])


def swapped(array):
    return lax.ppermute(array, SHARD, [(0, 1), (1, 0)])


HOPS = ((None, 4), (1, -2), (-1, 3), (2, -3))


def hop(array, index, back):
    size = lax.axis_size(Z)
    pairs = []
    for core in range(2):
        by = HOPS[index][core]
        if by is None:
            continue
        for i in range(size):
            there = (i + by) % size
            pairs.append((there * 2 + core, i * 2 + core) if back else (i * 2 + core, there * 2 + core))
    return lax.ppermute(array, (Z, SHARD), pairs)


def line_kernel(r0, r1, r2, r3, out_ref):
    for k, r_ref in enumerate((r0, r1, r2, r3)):
        out_ref[4 * k : 4 * k + 4, :] = r_ref[...]


def sum_kernel(place_ref, own, m0, m1, m2, m3, out_ref):
    out_ref[...] = (jnp.where(place_ref[3] == 0, own[...], m0[...]) + m1[...]) + (m2[...] + m3[...])


def recurrent_line(weight):
    others = [shifted(weight, X, k) for k in (1, 2, 3)]
    shape = (4 * weight.shape[0], weight.shape[1])
    return call(line_kernel, (weight, *others), [IN_VMEM] * 4, vmem((shape, f32)), [IN_VMEM], (), 1, 1 << 16)[0]


def recurrent(hidden, hids, line, place):
    plane = [line] + [shifted(line, Y, k) for k in (1, 2, 3)]
    out = (hidden.shape[0], line.shape[1])
    parts = call(
        recurrent_kernel, (place, hidden, *hids, *plane), [IN_SMEM] + [IN_VMEM] * 9,
        vmem(*[(out, f32)] * 4), [IN_VMEM] * 4, [pltpu.VMEM((32, hidden.shape[2]), f32)], 4, 1 << 22,
    )
    moved = [hop(part, k, False) for k, part in enumerate(parts)]
    return call(
        sum_kernel, (place, parts[0], *moved), [IN_SMEM] + [IN_VMEM] * 5,
        vmem((out, f32)), [IN_VMEM], (), 1, 1 << 16,
    )[0]


def update_kernel(
    place_ref,
    mine_ref, theirs_ref, sq_ref, sq_recv_ref, in_w_ref, bias_ref, cell_ref, ctx_w_ref, mlp_ref,
    wg_ref, wu_ref, wd_ref, gg_ref, gu_ref, gd_ref, meta_ref,
    up_g_hbm, up_u_hbm, up_d_hbm, hidden_ref, new_cell_ref, send_ref, keep_ref,
    cell_old, table, table_s, order, sem, sem_out, out_g, out_u, out_d, new_g, new_u, new_d, acc,
):
    count = wg_ref.shape[1] // CHUNK
    units = mlp_ref.shape[1]
    entries = 2.0 * wg_ref.shape[0] * wg_ref.shape[1]

    sums = sq_ref[...] + sq_recv_ref[...]
    total = jnp.sum(sums, axis=1, keepdims=True)
    rms = jnp.sqrt(total / entries + epsilon)
    rms_g, rms_p = rms[0:3], rms[8:11]
    logs = jnp.log(rms)
    fraction = place_ref[4].astype(f32) / STEPS
    in_w = in_w_ref[...]
    lstm_in = (
        (logs[0:3] * in_w[0:1] + logs[8:11] * in_w[1:2] + fraction * in_w[2:3])
        + (mine_ref[...] + theirs_ref[...])
        + bias_ref[...]
    )
    width = cell_ref.shape[2]
    for j in range(3):
        cell_old[j : j + 1, :] = cell_ref[j]
    in_gate = jax.nn.sigmoid(lstm_in[:, :width])
    forget_gate = jax.nn.sigmoid(lstm_in[:, width : 2 * width])
    candidate = jnp.tanh(lstm_in[:, 2 * width : 3 * width])
    out_gate = jax.nn.sigmoid(lstm_in[:, 3 * width :])
    cell = forget_gate * cell_old[0:3, :] + in_gate * candidate
    hidden = out_gate * jnp.tanh(cell)
    for j in range(3):
        new_cell_ref[j] = cell[j : j + 1]
        hidden_ref[j] = hidden[j : j + 1]
    context = lax.dot_general(
        hidden, ctx_w_ref[...], (((1,), (1,)), ((), ())), precision=highest, preferred_element_type=f32
    )
    mlp = mlp_ref[...]
    out_w = mlp[2:3]
    table[0:3, :units] = out_w * mlp[0:1] / rms_p
    table[8:11, :units] = out_w * mlp[1:2] / rms_g
    table[16:19, :units] = -(out_w * context[:, :units])
    table[24:27, : units + 1] = jnp.exp(context)
    table[32:35, 0:1] = rate_factor * rms_p
    table[40:41, :units] = out_w
    copy = pltpu.make_async_copy(table, table_s, sem)
    copy.start()
    copy.wait()

    positive = jnp.int32(0)
    for k in range(units):
        positive = positive + (table_s[40, k] >= 0).astype(jnp.int32)
    above, below = jnp.int32(0), positive
    for k in range(units):
        is_above = table_s[40, k] >= 0
        spot = jnp.where(is_above, above, below)
        for j in range(3):
            for group in range(3):
                order[group * 12 + j * 4 + spot] = table_s[group * 8 + j, k]
        above = above + is_above.astype(jnp.int32)
        below = below + 1 - is_above.astype(jnp.int32)

    def change(which, j, w_ref, grad_ref, out_ref, new_ref, by_rows, strip):
        scale = table_s[24 + which, units]
        rate = table_s[32 + which, 0]
        a = [order[which * 4 + k] for k in range(units)]
        b = [order[12 + which * 4 + k] for k in range(units)]
        edge = [order[24 + which * 4 + k] for k in range(units)]
        offset = -functools.reduce(lambda s, e: s + e, edge)

        def variant(top):
            def body(i, carry):
                here = pl.ds(pl.multiple_of(i * strip, strip), strip)
                if by_rows:
                    there, lanes = pl.ds(pl.multiple_of(j * CHUNK + i * strip, strip), strip), slice(None)
                else:
                    there, lanes = here, piece(j)
                p = w_ref[there, lanes].astype(f32)
                g = grad_ref[there, lanes]
                total = None
                for k in range(units):
                    term = a[k] * p + b[k] * g
                    term = jnp.maximum(term, edge[k]) if k < top else jnp.minimum(term, edge[k])
                    total = term if total is None else total + term
                upd = scale * (total + offset)
                out_ref[there, lanes] = upd.astype(bf16)
                new_ref[here, :] = (p - rate * upd).astype(bf16)
                return carry

            lax.fori_loop(0, new_ref.shape[0] // strip, body, 0)

        for top in range(units + 1):
            pl.when(positive == top)(functools.partial(variant, top))

    def results(j):
        at = piece(j)
        return (
            pltpu.make_async_copy(out_g.at[:, at], up_g_hbm.at[:, at], sem_out.at[0, j]),
            pltpu.make_async_copy(out_u.at[:, at], up_u_hbm.at[:, at], sem_out.at[1, j]),
            pltpu.make_async_copy(out_d.at[at, :], up_d_hbm.at[at, :], sem_out.at[2, j]),
        )

    def body(j, carry):
        copies = results(j)
        change(0, j, wg_ref, gg_ref, out_g, new_g, False, STRIP)
        copies[0].start()
        change(1, j, wu_ref, gu_ref, out_u, new_u, False, STRIP)
        copies[1].start()
        change(2, j, wd_ref, gd_ref, out_d, new_d, True, STRIP // 4)
        copies[2].start()
        meta = meta_ref[...]
        gate = dot(meta, new_g[...])
        up = dot(meta, new_u[...])
        act = (gate * jax.nn.sigmoid(gate) * up).astype(bf16)
        part = dot(act, new_d[...])

        @pl.when(j == 0)
        def _():
            acc[...] = part

        @pl.when(j > 0)
        def _():
            acc[...] += part

        return carry

    lax.fori_loop(0, count, body, 0)
    half = acc.shape[0] // 2
    core = place_ref[3]
    keep_ref[...] = acc[pl.ds(pl.multiple_of(core * half, half), half), :]
    send_ref[...] = acc[pl.ds(pl.multiple_of((1 - core) * half, half), half), :]
    for j in range(count):
        for copy in results(j):
            copy.wait()


STRIP = 64


def update(place, mine, theirs, sums, sums_recv, in_w, bias, cell, ctx_w, mlp, wg, wu, wd, gg, gu, gd, meta):
    tok, width = meta.shape
    hid = wg.shape[1]
    outs = [pltpu.HBM(wg.shape, bf16), pltpu.HBM(wu.shape, bf16), pltpu.HBM(wd.shape, bf16)]
    outs += vmem((cell.shape, f32), (cell.shape, f32), ((tok // 2, width), f32), ((tok // 2, width), f32))
    scratch = [
        pltpu.VMEM((8, cell.shape[2]), f32),
        pltpu.VMEM((48, 128), f32),
        pltpu.SMEM((48, 128), f32),
        pltpu.SMEM((48,), f32),
        pltpu.SemaphoreType.DMA,
        pltpu.SemaphoreType.DMA((3, hid // CHUNK)),
        pltpu.VMEM(wg.shape, bf16),
        pltpu.VMEM(wu.shape, bf16),
        pltpu.VMEM(wd.shape, bf16),
        pltpu.VMEM((width, CHUNK), bf16),
        pltpu.VMEM((width, CHUNK), bf16),
        pltpu.VMEM((CHUNK, width), bf16),
        pltpu.VMEM((tok, width), f32),
    ]
    operands = (place, mine, theirs, sums, sums_recv, in_w, bias, cell, ctx_w, mlp, wg, wu, wd, gg, gu, gd, meta)
    return call(
        update_kernel, operands, [IN_SMEM] + [IN_VMEM] * 16,
        outs, [IN_HBM] * 3 + [IN_VMEM] * 4, scratch, 20, 6 * tok * width * hid,
    )


def loss_kernel(scale, keep_ref, recv_ref, want_ref, out_ref):
    error = keep_ref[...] + recv_ref[...] - want_ref[...].astype(f32)
    total = jnp.sum(jnp.sum(error * error, axis=0, keepdims=True), axis=1, keepdims=True)
    out_ref[...] = jnp.broadcast_to(scale * total, out_ref.shape)


def loss_part(keep, recv, want, count):
    scale = 0.25 / (want.shape[0] * want.shape[1]) / count
    return call(
        functools.partial(loss_kernel, scale), (keep, recv, want), [IN_VMEM] * 3,
        vmem(((1, 128), f32)), [IN_VMEM], (), 8,
    )[0]


def local(
    tokens, targets, meta_tokens, meta_targets, gate_weight, up_weight, down_weight, task_step,
    hidden_state, cell_state, recurrent_weight, input_weight, lstm_bias, context_weight, mlp_weight,
):
    core = lax.axis_index(SHARD)
    place = jnp.stack([lax.axis_index(X), lax.axis_index(Y), lax.axis_index(Z), core, task_step[0]]).astype(jnp.int32)
    hidden = hidden_state.transpose(1, 0, 2)
    line = recurrent_line(recurrent_weight)
    hids = [hop(hidden, k, True) for k in range(4)]
    wg, wu, wd, want, meta, meta_want, own, p, q, act_t, x_t, param_sq = forward(
        place, tokens[0], gate_weight[0], up_weight[0], down_weight[0], targets[0], meta_tokens[0], meta_targets[0]
    )
    recv = swapped(own)
    mine = recurrent(hidden, hids, line, place)
    gg, gu, gd, sums = backward(own, recv, want, wd, p, q, act_t, x_t, param_sq)
    up_g, up_u, up_d, new_hidden, new_cell, send, keep = update(
        place, mine, swapped(mine), sums, swapped(sums), input_weight, lstm_bias[None], cell_state.transpose(1, 0, 2),
        context_weight.T, mlp_weight, wg, wu, wd, gg, gu, gd, meta,
    )
    count = lax.axis_size(TASK)
    part = loss_part(keep, swapped(send), meta_want, count)
    part = part + swapped(part)
    everyone = lax.all_to_all(part.reshape(count), TASK, 0, 0, tiled=True)
    meta_loss = jnp.sum(everyone)
    return (
        up_g[None], up_u[None], up_d[None], new_hidden.transpose(1, 0, 2), new_cell.transpose(1, 0, 2), meta_loss
    )


def solution(mesh):
    finer = Mesh(mesh.devices.reshape(4, 4, 8, mesh.shape["shard"]), (X, Y, Z, SHARD))
    return jax.shard_map(
        local,
        mesh=finer,
        in_specs=(
            P(TASK, None, None), P(TASK, None, None), P(TASK, None, None), P(TASK, None, None),
            P(TASK, None, "shard"), P(TASK, None, "shard"), P(TASK, "shard", None), P(TASK),
            P(TASK, None, None), P(TASK, None, None), P(TASK, None), P(), P(), P(), P(),
        ),
        out_specs=(
            P(TASK, None, "shard"), P(TASK, None, "shard"), P(TASK, "shard", None),
            P(TASK, None, None), P(TASK, None, None), P(),
        ),
        check_vma=False,
    )
```

time: 234 us -> 114 us (0.49)
  blocking collectives: 76.9 us -> 0 us
  other arithmetic: 67.5 us -> 0.74 us
  starting transfers between devices: 5.75 us -> 44.4 us
  Pallas kernels: 0 us -> 32.7 us
  matrix products: 31.7 us -> 0 us
  waiting for transfers between devices: 2.43 us -> 31.1 us
  local copies, waits for them, and re-layouts: 27.2 us -> 2.03 us
  between operations: 21.3 us -> 1.43 us
    broadcast_in_dim x3 -> x0, other arithmetic: 48.1 us -> none  [the longest x1 16.5 us: local(): results[2][0][None]]
    psum x4 -> x0, blocking collectives: 41.6 us -> none  [the longest x3 39 us: one_axis_at_a_time(): return functools.reduce(lax.psum, axes, array)]
    ppermute x0 -> x19, starting transfers between devices: none -> 36.3 us  [the longest x5 14.4 us: swapped(): return lax.ppermute(array, SHARD, [(0, 1), (1, 0)])]
    pallas_call x0 -> x7, Pallas kernels: none -> 32.7 us  [call(): pl.pallas_call(body, in_specs=specs, out_specs=out_specs, out_shape=outs,...]
    dot_general x12 -> x0, matrix products: 31.7 us -> none  [the longest x2 8.5 us: block_forward(): output = jnp.dot(activated, w_down, preferred_element_type=jnp.float32)]
    all_gather x2 -> x0, blocking collectives: 27.1 us -> none  [gather_in_order(): parts = lax.all_gather(parts, axes[k], axis=0, tiled=True)]
    ppermute x0 -> x19, waiting for transfers between devices: none -> 21.1 us  [the longest x8 12.3 us: hop(): return lax.ppermute(array, (Z, SHARD), pairs)]
    reduce_sum x6 -> x1, other arithmetic: 15.5 us -> 0.74 us  [local(): meta_loss = jnp.sum(everyone)]
  transfers between devices with their start and end apart: 2 -> 20, of which waited for: 2 -> 11; matrix products, arithmetic and copies ran while one was open for 17% -> 1% of each run, Pallas kernels for 0% -> 8%
where the time goes in v1:
time: 114 us; the launch traced here: 112 us
  starting transfers between devices  44.4 us (39%)
  Pallas kernels  32.7 us (29%)
  waiting for transfers between devices  31.1 us (27%)
  local copies, waits for them, and re-layouts  2.03 us (2%)
  between operations  1.43 us (1%)
    pallas_call x7, Pallas kernels, call(): pl.pallas_call(body, in_specs=specs, out_specs=out_specs, out_shape=outs,...  32.7 us
    ppermute x5, starting transfers between devices, swapped(): return lax.ppermute(array, SHARD, [(0, 1), (1, 0)])  14.4 us
    ppermute x8, starting transfers between devices, hop(): return lax.ppermute(array, (Z, SHARD), pairs)  12.7 us
    ppermute x8, waiting for transfers between devices, hop(): return lax.ppermute(array, (Z, SHARD), pairs)  12.3 us
    all_to_all x1, waiting for transfers between devices, local(): everyone = lax.all_to_all(part.reshape(count), TASK, 0, 0, tiled=True)  9.95 us
    ppermute x6, starting transfers between devices, shifted(): lax.ppermute(array, axis, [((i + shift) % size, i) for i in range(size)])  9.22 us
    all_to_all x1, starting transfers between devices, local(): everyone = lax.all_to_all(part.reshape(count), TASK, 0, 0, tiled=True)  8.08 us
    ppermute x5, waiting for transfers between devices, swapped(): return lax.ppermute(array, SHARD, [(0, 1), (1, 0)])  4.63 us
  transfers between devices with their start and end apart: 20, of which 11 were waited for; matrix products, arithmetic and copies ran while one was open for 1% of the time, Pallas kernels for 8%

profile of v1, /device:TPU:32, one launch (start us, length us, event | category | flops | bytes accessed | tf_op | source)
XLA Modules:
  0.0 112.3 jit_solution(1321489372652539505)
XLA Ops:
  1.4 9.2 %shard_map.193 = (bf16[1024,768]{1,0:T(8,128)(2,1)S(1)}, bf16[1024,768]{1,0:T(8,128)(2,1)S(1)}, bf16[768,1024]{1,0:T(8,128)(2,1)S(1)}, bf16[512,1024]{1,0:T(8,12...) custom-call(s32[5]{0:T(128)S(1)} %stack.19.place_ref, ...), custom_call_target="tpu_custom_call" | custom-call | flops 2415919104 | tf_op jit(solution)/shard_map/pallas_call | solution.py:56
  10.7 2.8 %collective-permute-start.4 = (f32[4,2048]{1,0:T(4,128)S(1)}, f32[4,2048]{1,0:T(4,128)S(1)}, u32[]{:S(2)}, u32[]{:S(2)}) collective-permute-start(f32[4,2048]{1,0:T(4,128)S(1)} %copy-done.1), channel_id=1, source_target_pairs={{64,0},{128,64},{192,128},{0,192},{65,1},{129,65},{193,129},{1,193... | collective-permute-start | bytes 98312 | tf_op jit(solution)/shard_map/ppermute | solution.py:223
  13.5 0.8 collective-permute-start.5
  14.3 0.9 collective-permute-start.6
  15.2 3.7 %collective-permute-done.5.r2 = f32[4,2048]{1,0:T(4,128)S(1)} collective-permute-done((f32[4,2048]{1,0:T(4,128)S(1)}, f32[4,2048]{1,0:T(4,128)S(1)}, u32[]{:S(2)}, u32[]{:S(2)}) %collective-permute-start.5) | collective-permute-done | bytes 32800 | tf_op jit(solution)/shard_map/ppermute | solution.py:223
  19.4 3.1 %collective-permute-start.7 = (f32[16,2048]{1,0:T(8,128)S(1)}, f32[16,2048]{1,0:T(8,128)S(1)}, u32[]{:S(2)}, u32[]{:S(2)}) collective-permute-start(f32[16,2048]{1,0:T(8,128)S(1)} %shard_map.190.r0), channel_id=1, source_target_pairs={{16,0},{32,16},{48,32},{0,48},{17,1},{33,17},{49,33},{1,49},{18,2}... | collective-permute-start | bytes 393224 | tf_op jit(solution)/shard_map/ppermute | solution.py:223
  22.5 0.6 collective-permute-start.8
  23.2 1.0 collective-permute-start.9
  24.2 0.7 collective-permute-start
  25.0 3.5 %collective-permute-done.1.h1 = f32[3,1,512]{2,1,0:T(1,128)S(1)} collective-permute-done((f32[3,1,512]{2,1,0:T(1,128)S(1)}, f32[3,1,512]{2,1,0:T(1,128)S(1)}, u32[]{:S(2)}, u32[]{:S(2)}) %collective-permute-start.1) | collective-permute-done | bytes 6176 | tf_op jit(solution)/shard_map/ppermute | solution.py:243
  28.5 1.9 %collective-permute-start.2 = (f32[3,1,512]{2,1,0:T(1,128)S(1)}, f32[3,1,512]{2,1,0:T(1,128)S(1)}, u32[]{:S(2)}, u32[]{:S(2)}) collective-permute-start(f32[3,1,512]{2,1,0:T(1,128)S(1)} %bitcast.28), channel_id=1, source_target_pairs={{14,0},{0,2},{2,4},{4,6},{6,8},{8,10},{10,12},{12,14},{7,1},{9,3},... | collective-permute-start | bytes 18440 | tf_op jit(solution)/shard_map/ppermute | solution.py:243
  30.4 3.4 %collective-permute-done.2.h2 = f32[3,1,512]{2,1,0:T(1,128)S(1)} collective-permute-done((f32[3,1,512]{2,1,0:T(1,128)S(1)}, f32[3,1,512]{2,1,0:T(1,128)S(1)}, u32[]{:S(2)}, u32[]{:S(2)}) %collective-permute-start.2) | collective-permute-done | bytes 6176 | tf_op jit(solution)/shard_map/ppermute | solution.py:243
  33.8 5.0 %collective-permute-start.3 = (f32[3,1,512]{2,1,0:T(1,128)S(1)}, f32[3,1,512]{2,1,0:T(1,128)S(1)}, u32[]{:S(2)}, u32[]{:S(2)}) collective-permute-start(f32[3,1,512]{2,1,0:T(1,128)S(1)} %bitcast.29), channel_id=1, source_target_pairs={{4,0},{6,2},{8,4},{10,6},{12,8},{14,10},{0,12},{2,14},{11,1},{13,3... | collective-permute-start | bytes 18440 | tf_op jit(solution)/shard_map/ppermute | solution.py:243
  38.8 1.3 %collective-permute-done.3.h3 = f32[3,1,512]{2,1,0:T(1,128)S(1)} collective-permute-done((f32[3,1,512]{2,1,0:T(1,128)S(1)}, f32[3,1,512]{2,1,0:T(1,128)S(1)}, u32[]{:S(2)}, u32[]{:S(2)}) %collective-permute-start.3) | collective-permute-done | bytes 6176 | tf_op jit(solution)/shard_map/ppermute | solution.py:243
  40.1 1.8 %shard_map.191 = (f32[3,2048]{1,0:T(4,128)S(1)}, f32[3,2048]{1,0:T(4,128)S(1)}, f32[3,2048]{1,0:T(4,128)S(1)}, f32[3,2048]{1,0:T(4,128)S(1)}) custom-call(s32[5]{0:T(128)S(1)} %stack.19.place_ref, f32[3,1,512]{2,1,0:T(1,128)S(1)} %bitcast.30, f32[3,1,512]{2,1,0:T(1,128)S(1)} %collective-permute-done.h0, f32[3,1,512]{2,1,0:T(1,128)S(1)} %collective-permute-done.1.h1, ...), custom_call_target="tpu_custom_call" | custom-call | flops 4194304 | tf_op jit(solution)/shard_map/pallas_call | solution.py:56
  41.9 0.7 collective-permute-start.10
  42.6 1.3 %collective-permute-start.11 = (f32[3,2048]{1,0:T(4,128)S(1)}, f32[3,2048]{1,0:T(4,128)S(1)}, u32[]{:S(2)}, u32[]{:S(2)}) collective-permute-start(f32[3,2048]{1,0:T(4,128)S(1)} %get-tuple-element.34), channel_id=1, source_target_pairs={{0,2},{2,4},{4,6},{6,8},{8,10},{10,12},{12,14},{14,0},{1,13},{3,15... | collective-permute-start | bytes 73736 | tf_op jit(solution)/shard_map/ppermute | solution.py:243
  44.0 0.8 collective-permute-start.12
  44.7 2.3 %collective-permute-start.13 = (f32[3,2048]{1,0:T(4,128)S(1)}, f32[3,2048]{1,0:T(4,128)S(1)}, u32[]{:S(2)}, u32[]{:S(2)}) collective-permute-start(f32[3,2048]{1,0:T(4,128)S(1)} %get-tuple-element.36), channel_id=1, source_target_pairs={{0,4},{2,6},{4,8},{6,10},{8,12},{10,14},{12,0},{14,2},{1,11},{3,13... | collective-permute-start | bytes 73736 | tf_op jit(solution)/shard_map/ppermute | solution.py:243
  47.0 0.9 collective-permute-done.12.m2
  47.9 3.1 %collective-permute-done.13.m3 = f32[3,2048]{1,0:T(4,128)S(1)} collective-permute-done((f32[3,2048]{1,0:T(4,128)S(1)}, f32[3,2048]{1,0:T(4,128)S(1)}, u32[]{:S(2)}, u32[]{:S(2)}) %collective-permute-start.13) | collective-permute-done | bytes 24608 | tf_op jit(solution)/shard_map/ppermute | solution.py:243
  51.6 13.7 %collective-permute-start.14 = (f32[3,2048]{1,0:T(4,128)S(1)}, f32[3,2048]{1,0:T(4,128)S(1)}, u32[]{:S(2)}, u32[]{:S(2)}) collective-permute-start(f32[3,2048]{1,0:T(4,128)S(1)} %shard_map.192.mine_ref), channel_id=1, source_target_pairs={{0,1},{1,0},{2,3},{3,2},{4,5},{5,4},{6,7},{7,6},{8,9},{9,8},{10,11... | collective-permute-start | bytes 73736 | tf_op jit(solution)/shard_map/ppermute | solution.py:227
  65.3 6.1 %shard_map.194 = (f32[1024,768]{1,0:T(8,128)S(1)}, f32[1024,768]{1,0:T(8,128)S(1)}, f32[768,1024]{1,0:T(8,128)S(1)}, f32[16,128]{1,0:T(8,128)S(1)}) custom-call(f32[512,1024]{1,0:T(8,128)S(1)} %get-tuple-element.37.own_ref, f32[512,1024]{1,0:T(8,128)S(1)} %collective-permute-done.15.recv_ref, bf16[512,1024]{1,0:T(8,128)(2,1)S(1)} %get-tuple-element.38.want_ref, ...), custom_call_target="tpu_custom_call" | custom-call | flops 3221225472 | tf_op jit(solution)/shard_map/pallas_call | solution.py:56
  71.6 1.1 %collective-permute-done.16.sq_recv_ref = f32[16,128]{1,0:T(8,128)S(1)} collective-permute-done((f32[16,128]{1,0:T(8,128)S(1)}, f32[16,128]{1,0:T(8,128)S(1)}, u32[]{:S(2)}, u32[]{:S(2)}) %collective-permute-start.16) | collective-permute-done | bytes 8224 | tf_op jit(solution)/shard_map/ppermute | solution.py:227
  72.7 14.5 %shard_map.195 = (bf16[1024,768]{1,0:T(8,128)(2,1)}, bf16[1024,768]{1,0:T(8,128)(2,1)}, bf16[768,1024]{1,0:T(8,128)(2,1)}, f32[3,1,512]{2,1,0:T(1,128)S(1)}, f32...) custom-call(s32[5]{0:T(128)S(1)} %stack.19.place_ref, f32[3,2048]{1,0:T(4,128)S(1)} %shard_map.192.mine_ref, ...), custom_call_target="tpu_custom_call" | custom-call | flops 2415919104 | tf_op jit(solution)/shard_map/pallas_call | solution.py:56
  87.5 2.5 %collective-permute-done.17.recv_ref = f32[256,1024]{1,0:T(8,128)S(1)} collective-permute-done((f32[256,1024]{1,0:T(8,128)S(1)}, f32[256,1024]{1,0:T(8,128)S(1)}, u32[]{:S(2)}, u32[]{:S(2)}) %collective-permute-start.17) | collective-permute-done | bytes 1048608 | tf_op jit(solution)/shard_map/ppermute | solution.py:227
  90.6 1.0 collective-permute-done.18
  91.7 0.7 copy.21
  92.4 8.1 %all-to-all-start = ((f32[128,1,1]{2,1,0:T(1,128)}), f32[128,1,1]{2,1,0:T(1,128)S(1)}, u32[]{:S(2)}, u32[]{:S(2)}) async-start(f32[128,1,1]{2,1,0:T(1,128)} %copy.21), calls=%async_computation | async-start | bytes 131072 | tf_op jit(solution)/shard_map/all_to_all | solution.py:478
  100.5 0.6 copy.22
  101.7 10.0 %all-to-all-done = f32[128,1,1]{2,1,0:T(1,128)S(1)} async-done(((f32[128,1,1]{2,1,0:T(1,128)}), f32[128,1,1]{2,1,0:T(1,128)S(1)}, u32[]{:S(2)}, u32[]{:S(2)}) %all-to-all-start) | async-done | bytes 544 | tf_op jit(solution)/shard_map/all_to_all | solution.py:478
  111.6 0.7 reduce_sum.9
  (35 shorter events, 3.1 us)
Async XLA Ops:
  1.4 9.3 %copy-start.1 = (f32[4,2048]{1,0:T(4,128)S(1)}, f32[4,2048]{1,0:T(4,128)}, u32[]{:S(2)}) copy-start(f32[4,2048]{1,0:T(4,128)} %r0.1) | copy-start | bytes 98308
  1.4 22.8 %copy-start.4 = (f32[1,3,512]{2,0,1:T(1,128)S(1)}, f32[1,3,512]{2,0,1:T(1,128)}, u32[]{:S(2)}) copy-start(f32[1,3,512]{2,0,1:T(1,128)} %param.23) | copy-start | bytes 18436
  10.6 54.7 %collective-permute-start.15 = (f32[512,1024]{1,0:T(8,128)S(1)}, f32[512,1024]{1,0:T(8,128)S(1)}, u32[]{:S(2)}, u32[]{:S(2)}) collective-permute-start(f32[512,1024]{1,0:T(8,128)S(1)} %get-tuple-element.37.own_ref), channel_id=1, source_target_pairs={{0,1},{1,0},{2,3},{3,2},{4,5},{5,4},{6,7},{7,6},{8,9},{9,8},{10,11... | collective-permute-start | bytes 6291464 | tf_op jit(solution)/shard_map/ppermute | solution.py:227
  10.7 4.5 %collective-permute-start.4 = (f32[4,2048]{1,0:T(4,128)S(1)}, f32[4,2048]{1,0:T(4,128)S(1)}, u32[]{:S(2)}, u32[]{:S(2)}) collective-permute-start(f32[4,2048]{1,0:T(4,128)S(1)} %copy-done.1), channel_id=1, source_target_pairs={{64,0},{128,64},{192,128},{0,192},{65,1},{129,65},{193,129},{1,193... | collective-permute-start | bytes 98312 | tf_op jit(solution)/shard_map/ppermute | solution.py:223
  13.5 5.4 %collective-permute-start.5 = (f32[4,2048]{1,0:T(4,128)S(1)}, f32[4,2048]{1,0:T(4,128)S(1)}, u32[]{:S(2)}, u32[]{:S(2)}) collective-permute-start(f32[4,2048]{1,0:T(4,128)S(1)} %copy-done.1), channel_id=1, source_target_pairs={{128,0},{192,64},{0,128},{64,192},{129,1},{193,65},{1,129},{65,193... | collective-permute-start | bytes 98312 | tf_op jit(solution)/shard_map/ppermute | solution.py:223
  14.3 5.1 %collective-permute-start.6 = (f32[4,2048]{1,0:T(4,128)S(1)}, f32[4,2048]{1,0:T(4,128)S(1)}, u32[]{:S(2)}, u32[]{:S(2)}) collective-permute-start(f32[4,2048]{1,0:T(4,128)S(1)} %copy-done.1), channel_id=1, source_target_pairs={{192,0},{0,64},{64,128},{128,192},{193,1},{1,65},{65,129},{129,193... | collective-permute-start | bytes 98312 | tf_op jit(solution)/shard_map/ppermute | solution.py:223
  19.4 20.7 %collective-permute-start.7 = (f32[16,2048]{1,0:T(8,128)S(1)}, f32[16,2048]{1,0:T(8,128)S(1)}, u32[]{:S(2)}, u32[]{:S(2)}) collective-permute-start(f32[16,2048]{1,0:T(8,128)S(1)} %shard_map.190.r0), channel_id=1, source_target_pairs={{16,0},{32,16},{48,32},{0,48},{17,1},{33,17},{49,33},{1,49},{18,2}... | collective-permute-start | bytes 393224 | tf_op jit(solution)/shard_map/ppermute | solution.py:223
  22.5 17.6 %collective-permute-start.8 = (f32[16,2048]{1,0:T(8,128)S(1)}, f32[16,2048]{1,0:T(8,128)S(1)}, u32[]{:S(2)}, u32[]{:S(2)}) collective-permute-start(f32[16,2048]{1,0:T(8,128)S(1)} %shard_map.190.r0), channel_id=1, source_target_pairs={{32,0},{48,16},{0,32},{16,48},{33,1},{49,17},{1,33},{17,49},{34,2}... | collective-permute-start | bytes 393224 | tf_op jit(solution)/shard_map/ppermute | solution.py:223
  23.2 17.0 %collective-permute-start.9 = (f32[16,2048]{1,0:T(8,128)S(1)}, f32[16,2048]{1,0:T(8,128)S(1)}, u32[]{:S(2)}, u32[]{:S(2)}) collective-permute-start(f32[16,2048]{1,0:T(8,128)S(1)} %shard_map.190.r0), channel_id=1, source_target_pairs={{48,0},{0,16},{16,32},{32,48},{49,1},{1,17},{17,33},{33,49},{50,2}... | collective-permute-start | bytes 393224 | tf_op jit(solution)/shard_map/ppermute | solution.py:223
  24.2 0.7 collective-permute-start
  24.8 3.7 %collective-permute-start.1 = (f32[3,1,512]{2,1,0:T(1,128)S(1)}, f32[3,1,512]{2,1,0:T(1,128)S(1)}, u32[]{:S(2)}, u32[]{:S(2)}) collective-permute-start(f32[3,1,512]{2,1,0:T(1,128)S(1)} %bitcast.27), channel_id=1, source_target_pairs={{2,0},{4,2},{6,4},{8,6},{10,8},{12,10},{14,12},{0,14},{13,1},{15,3... | collective-permute-start | bytes 18440 | tf_op jit(solution)/shard_map/ppermute | solution.py:243
  28.5 5.3 %collective-permute-start.2 = (f32[3,1,512]{2,1,0:T(1,128)S(1)}, f32[3,1,512]{2,1,0:T(1,128)S(1)}, u32[]{:S(2)}, u32[]{:S(2)}) collective-permute-start(f32[3,1,512]{2,1,0:T(1,128)S(1)} %bitcast.28), channel_id=1, source_target_pairs={{14,0},{0,2},{2,4},{4,6},{6,8},{8,10},{10,12},{12,14},{7,1},{9,3},... | collective-permute-start | bytes 18440 | tf_op jit(solution)/shard_map/ppermute | solution.py:243
  33.8 6.3 %collective-permute-start.3 = (f32[3,1,512]{2,1,0:T(1,128)S(1)}, f32[3,1,512]{2,1,0:T(1,128)S(1)}, u32[]{:S(2)}, u32[]{:S(2)}) collective-permute-start(f32[3,1,512]{2,1,0:T(1,128)S(1)} %bitcast.29), channel_id=1, source_target_pairs={{4,0},{6,2},{8,4},{10,6},{12,8},{14,10},{0,12},{2,14},{11,1},{13,3... | collective-permute-start | bytes 18440 | tf_op jit(solution)/shard_map/ppermute | solution.py:243
  41.9 5.0 %collective-permute-start.10 = (f32[3,2048]{1,0:T(4,128)S(1)}, f32[3,2048]{1,0:T(4,128)S(1)}, u32[]{:S(2)}, u32[]{:S(2)}) collective-permute-start(f32[3,2048]{1,0:T(4,128)S(1)} %get-tuple-element.33.own), channel_id=1, source_target_pairs={{1,9},{3,11},{5,13},{7,15},{9,1},{11,3},{13,5},{15,7},{17,25},{19,... | collective-permute-start | bytes 73736 | tf_op jit(solution)/shard_map/ppermute | solution.py:243
  42.6 4.4 %collective-permute-start.11 = (f32[3,2048]{1,0:T(4,128)S(1)}, f32[3,2048]{1,0:T(4,128)S(1)}, u32[]{:S(2)}, u32[]{:S(2)}) collective-permute-start(f32[3,2048]{1,0:T(4,128)S(1)} %get-tuple-element.34), channel_id=1, source_target_pairs={{0,2},{2,4},{4,6},{6,8},{8,10},{10,12},{12,14},{14,0},{1,13},{3,15... | collective-permute-start | bytes 73736 | tf_op jit(solution)/shard_map/ppermute | solution.py:243
  44.0 3.9 %collective-permute-start.12 = (f32[3,2048]{1,0:T(4,128)S(1)}, f32[3,2048]{1,0:T(4,128)S(1)}, u32[]{:S(2)}, u32[]{:S(2)}) collective-permute-start(f32[3,2048]{1,0:T(4,128)S(1)} %get-tuple-element.35), channel_id=1, source_target_pairs={{0,14},{2,0},{4,2},{6,4},{8,6},{10,8},{12,10},{14,12},{1,7},{3,9},... | collective-permute-start | bytes 73736 | tf_op jit(solution)/shard_map/ppermute | solution.py:243
  44.7 6.3 %collective-permute-start.13 = (f32[3,2048]{1,0:T(4,128)S(1)}, f32[3,2048]{1,0:T(4,128)S(1)}, u32[]{:S(2)}, u32[]{:S(2)}) collective-permute-start(f32[3,2048]{1,0:T(4,128)S(1)} %get-tuple-element.36), channel_id=1, source_target_pairs={{0,4},{2,6},{4,8},{6,10},{8,12},{10,14},{12,0},{14,2},{1,11},{3,13... | collective-permute-start | bytes 73736 | tf_op jit(solution)/shard_map/ppermute | solution.py:243
  51.6 20.0 %collective-permute-start.14 = (f32[3,2048]{1,0:T(4,128)S(1)}, f32[3,2048]{1,0:T(4,128)S(1)}, u32[]{:S(2)}, u32[]{:S(2)}) collective-permute-start(f32[3,2048]{1,0:T(4,128)S(1)} %shard_map.192.mine_ref), channel_id=1, source_target_pairs={{0,1},{1,0},{2,3},{3,2},{4,5},{5,4},{6,7},{7,6},{8,9},{9,8},{10,11... | collective-permute-start | bytes 73736 | tf_op jit(solution)/shard_map/ppermute | solution.py:227
  65.3 7.4 %copy-start = (f32[3,2048]{1,0:T(4,128)S(1)}, f32[3,2048]{1,0:T(4,128)}, u32[]{:S(2)}) copy-start(f32[3,2048]{1,0:T(4,128)} %in_w_ref.1) | copy-start | bytes 73732
  65.3 7.4 %copy-start.2 = (f32[512,5]{0,1:T(8,128)S(1)}, f32[512,5]{0,1:T(8,128)}, u32[]{:S(2)}) copy-start(f32[512,5]{0,1:T(8,128)} %param.28) | copy-start | bytes 30724
  65.3 7.4 %copy-start.3 = (f32[2048]{0:T(1024)S(1)}, f32[2048]{0:T(1024)}, u32[]{:S(2)}) copy-start(f32[2048]{0:T(1024)} %param.27) | copy-start | bytes 24580
  65.3 7.4 %copy-start.5 = (f32[1,3,512]{2,0,1:T(1,128)S(1)}, f32[1,3,512]{2,0,1:T(1,128)}, u32[]{:S(2)}) copy-start(f32[1,3,512]{2,0,1:T(1,128)} %param.24) | copy-start | bytes 18436
  65.3 7.4 %copy-start.6 = (f32[3,4]{1,0:T(4,128)S(1)}, f32[3,4]{1,0:T(4,128)}, u32[]{:S(2)}) copy-start(f32[3,4]{1,0:T(4,128)} %mlp_ref.1) | copy-start | bytes 148
  71.5 1.3 %collective-permute-start.16 = (f32[16,128]{1,0:T(8,128)S(1)}, f32[16,128]{1,0:T(8,128)S(1)}, u32[]{:S(2)}, u32[]{:S(2)}) collective-permute-start(f32[16,128]{1,0:T(8,128)S(1)} %get-tuple-element.45.sq_ref), channel_id=1, source_target_pairs={{0,1},{1,0},{2,3},{3,2},{4,5},{5,4},{6,7},{7,6},{8,9},{9,8},{10,11... | collective-permute-start | bytes 24584 | tf_op jit(solution)/shard_map/ppermute | solution.py:227
  87.3 2.7 %collective-permute-start.17 = (f32[256,1024]{1,0:T(8,128)S(1)}, f32[256,1024]{1,0:T(8,128)S(1)}, u32[]{:S(2)}, u32[]{:S(2)}) collective-permute-start(f32[256,1024]{1,0:T(8,128)S(1)} %get-tuple-element.58), channel_id=1, source_target_pairs={{0,1},{1,0},{2,3},{3,2},{4,5},{5,4},{6,7},{7,6},{8,9},{9,8},{10,11... | collective-permute-start | bytes 3145736 | tf_op jit(solution)/shard_map/ppermute | solution.py:227
  90.5 1.2 %collective-permute-start.18 = (f32[1,128]{1,0:T(1,128)S(1)}, f32[1,128]{1,0:T(1,128)S(1)}, u32[]{:S(2)}, u32[]{:S(2)}) collective-permute-start(f32[1,128]{1,0:T(1,128)S(1)} %shard_map.196), channel_id=1, source_target_pairs={{0,1},{1,0},{2,3},{3,2},{4,5},{5,4},{6,7},{7,6},{8,9},{9,8},{10,11... | collective-permute-start | bytes 1544 | tf_op jit(solution)/shard_map/ppermute | solution.py:227
  92.4 19.2 %all-to-all-start = ((f32[128,1,1]{2,1,0:T(1,128)}), f32[128,1,1]{2,1,0:T(1,128)S(1)}, u32[]{:S(2)}, u32[]{:S(2)}) async-start(f32[128,1,1]{2,1,0:T(1,128)} %copy.21), calls=%async_computation | async-start | bytes 131072 | tf_op jit(solution)/shard_map/all_to_all | solution.py:478

commit v2 on v1

--- a/solution.py
+++ b/solution.py
@@ -68,43 +68,11 @@
     return pl.ds(pl.multiple_of(j * CHUNK, CHUNK), CHUNK)
 
 
-def forward_kernel(
-    place_ref, x_hbm, wg_hbm, wu_hbm, wd_hbm, want_hbm, meta_hbm, meta_want_hbm,
-    wg_ref, wu_ref, wd_ref, want_ref, meta_ref, meta_want_ref, out_ref, p_ref, q_ref, act_t_ref, x_t_ref, sq_ref,
-    x_ref, sem_x, sem_w, sem_late,
-):
-    count = wg_ref.shape[1] // CHUNK
-    half = meta_want_ref.shape[0]
-
-    def weights(j):
-        at = piece(j)
-        return (
-            pltpu.make_async_copy(wg_hbm.at[:, at], wg_ref.at[:, at], sem_w.at[0, j]),
-            pltpu.make_async_copy(wu_hbm.at[:, at], wu_ref.at[:, at], sem_w.at[1, j]),
-            pltpu.make_async_copy(wd_hbm.at[at, :], wd_ref.at[at, :], sem_w.at[2, j]),
-        )
-
-    mine = pl.ds(pl.multiple_of(place_ref[3] * half, half), half)
-    late = (
-        pltpu.make_async_copy(want_hbm, want_ref, sem_late.at[0]),
-        pltpu.make_async_copy(meta_hbm, meta_ref, sem_late.at[1]),
-        pltpu.make_async_copy(meta_want_hbm.at[mine, :], meta_want_ref, sem_late.at[2]),
-    )
-    first = pltpu.make_async_copy(x_hbm, x_ref, sem_x)
-    first.start()
-    for j in range(count):
-        for copy in weights(j):
-            copy.start()
-    for copy in late:
-        copy.start()
+def forward_kernel(x_ref, wg_ref, wu_ref, wd_ref, out_ref, p_ref, q_ref, act_t_ref, x_t_ref, sq_ref):
     sq_ref[...] = jnp.zeros_like(sq_ref)
-    first.wait()
 
     def body(j, carry):
         at = piece(j)
-        copies = weights(j)
-        copies[0].wait()
-        copies[1].wait()
         x = x_ref[...]
         gate = dot(x, wg_ref[:, at])
         up = dot(x, wu_ref[:, at])
@@ -114,7 +82,6 @@
         p_ref[:, at] = up * sig * (1.0 + gate * (1.0 - sig))
         act = (silu * up).astype(bf16)
         act_t_ref[at, :] = act.T
-        copies[2].wait()
         part = dot(act, wd_ref[at, :])
 
         @pl.when(j == 0)
@@ -131,28 +98,18 @@
         sq_ref[2:3, :] += squares(wd_ref[at, :])
         return carry
 
-    lax.fori_loop(0, count, body, 0)
-    for copy in late:
-        copy.wait()
-
-
-def forward(place, x, wg, wu, wd, want, meta, meta_want):
+    lax.fori_loop(0, wg_ref.shape[1] // CHUNK, body, 0)
+
+
+def forward(x, wg, wu, wd):
     tok, width = x.shape
     hid = wg.shape[1]
     outs = vmem(
-        (wg.shape, bf16), (wu.shape, bf16), (wd.shape, bf16), (want.shape, bf16), (meta.shape, bf16),
-        ((tok // 2, width), bf16), ((tok, width), f32), ((tok, hid), f32), ((tok, hid), f32),
-        ((hid, tok), bf16), ((width, tok), bf16), ((8, 128), f32),
-    )
-    scratch = [
-        pltpu.VMEM((tok, width), bf16),
-        pltpu.SemaphoreType.DMA,
-        pltpu.SemaphoreType.DMA((3, hid // CHUNK)),
-        pltpu.SemaphoreType.DMA((3,)),
-    ]
-    return call(
-        forward_kernel, (place, x, wg, wu, wd, want, meta, meta_want), [IN_SMEM] + [IN_HBM] * 7,
-        outs, [IN_VMEM] * len(outs), scratch, 12, 6 * tok * width * hid,
+        ((tok, width), f32), ((tok, hid), f32), ((tok, hid), f32), ((hid, tok), bf16), ((width, tok), bf16), ((8, 128), f32),
+    )
+    return call(
+        forward_kernel, (x, wg, wu, wd), [IN_VMEM] * 4,
+        outs, [IN_VMEM] * len(outs), (), 8, 6 * tok * width * hid,
     )
 
 
@@ -227,7 +184,7 @@
     return lax.ppermute(array, SHARD, [(0, 1), (1, 0)])
 
 
-HOPS = ((None, 4), (1, -2), (-1, 3), (2, -3))
+HOPS = ((None, -1), (1, 2), (3, -2), (4, -3))
 
 
 def hop(array, index, back):
@@ -241,6 +198,24 @@
             there = (i + by) % size
             pairs.append((there * 2 + core, i * 2 + core) if back else (i * 2 + core, there * 2 + core))
     return lax.ppermute(array, (Z, SHARD), pairs)
+
+
+def first_kernel(place_ref, hidden_hbm, weight_hbm, hidden_ref, weight_ref, sems):
+    copies = (
+        pltpu.make_async_copy(weight_hbm, weight_ref, sems.at[0]),
+        pltpu.make_async_copy(hidden_hbm, hidden_ref, sems.at[1]),
+    )
+    for copy in copies:
+        copy.start()
+    for copy in copies:
+        copy.wait()
+
+
+def brought(place, hidden, weight):
+    return call(
+        first_kernel, (place, hidden, weight), [IN_SMEM] + [IN_HBM] * 2, vmem((hidden.shape, f32), (weight.shape, f32)),
+        [IN_VMEM] * 2, [pltpu.SemaphoreType.DMA((2,))], 1, 100_000_000_000,
+    )
 
 
 def line_kernel(r0, r1, r2, r3, out_ref):
@@ -439,16 +414,18 @@
     )
 
 
-def loss_kernel(scale, keep_ref, recv_ref, want_ref, out_ref):
-    error = keep_ref[...] + recv_ref[...] - want_ref[...].astype(f32)
+def loss_kernel(scale, place_ref, keep_ref, recv_ref, want_ref, out_ref):
+    half = keep_ref.shape[0]
+    mine = pl.ds(pl.multiple_of(place_ref[3] * half, half), half)
+    error = keep_ref[...] + recv_ref[...] - want_ref[mine, :].astype(f32)
     total = jnp.sum(jnp.sum(error * error, axis=0, keepdims=True), axis=1, keepdims=True)
     out_ref[...] = jnp.broadcast_to(scale * total, out_ref.shape)
 
 
-def loss_part(keep, recv, want, count):
-    scale = 0.25 / (want.shape[0] * want.shape[1]) / count
-    return call(
-        functools.partial(loss_kernel, scale), (keep, recv, want), [IN_VMEM] * 3,
+def loss_part(place, keep, recv, want, count):
+    scale = 0.5 / (want.shape[0] * want.shape[1]) / count
+    return call(
+        functools.partial(loss_kernel, scale), (place, keep, recv, want), [IN_SMEM] + [IN_VMEM] * 3,
         vmem(((1, 128), f32)), [IN_VMEM], (), 8,
     )[0]
 
@@ -459,21 +436,20 @@
 ):
     core = lax.axis_index(SHARD)
     place = jnp.stack([lax.axis_index(X), lax.axis_index(Y), lax.axis_index(Z), core, task_step[0]]).astype(jnp.int32)
-    hidden = hidden_state.transpose(1, 0, 2)
-    line = recurrent_line(recurrent_weight)
+    hidden, weight = brought(place, hidden_state.transpose(1, 0, 2), recurrent_weight)
+    line = recurrent_line(weight)
     hids = [hop(hidden, k, True) for k in range(4)]
-    wg, wu, wd, want, meta, meta_want, own, p, q, act_t, x_t, param_sq = forward(
-        place, tokens[0], gate_weight[0], up_weight[0], down_weight[0], targets[0], meta_tokens[0], meta_targets[0]
-    )
+    wg, wu, wd = gate_weight[0], up_weight[0], down_weight[0]
+    own, p, q, act_t, x_t, param_sq = forward(tokens[0], wg, wu, wd)
     recv = swapped(own)
     mine = recurrent(hidden, hids, line, place)
-    gg, gu, gd, sums = backward(own, recv, want, wd, p, q, act_t, x_t, param_sq)
+    gg, gu, gd, sums = backward(own, recv, targets[0], wd, p, q, act_t, x_t, param_sq)
     up_g, up_u, up_d, new_hidden, new_cell, send, keep = update(
         place, mine, swapped(mine), sums, swapped(sums), input_weight, lstm_bias[None], cell_state.transpose(1, 0, 2),
-        context_weight.T, mlp_weight, wg, wu, wd, gg, gu, gd, meta,
+        context_weight.T, mlp_weight, wg, wu, wd, gg, gu, gd, meta_tokens[0],
     )
     count = lax.axis_size(TASK)
-    part = loss_part(keep, swapped(send), meta_want, count)
+    part = loss_part(place, keep, swapped(send), meta_targets[0], count)
     part = part + swapped(part)
     everyone = lax.all_to_all(part.reshape(count), TASK, 0, 0, tiled=True)
     meta_loss = jnp.sum(everyone)

time: 114 us -> 118 us (1.035)
  local copies, waits for them, and re-layouts: 2.03 us -> 10.7 us
  waiting for transfers between devices: 31.1 us -> 28.3 us
    ppermute x5, starting transfers between devices: 14.4 us -> 1.65 us  [swapped(): return lax.ppermute(array, SHARD, [(0, 1), (1, 0)])]
    unnamed x16 -> x44, local copies, waits for them, and re-layouts: 1.22 us -> 9.87 us
    ppermute x8, starting transfers between devices: 12.7 us -> 21.3 us  [hop(): return lax.ppermute(array, (Z, SHARD), pairs)]
    ppermute x6, starting transfers between devices: 9.22 us -> 11.6 us  [shifted(): lax.ppermute(array, axis, [((i + shift) % size, i) for i in range(size)])]
    ppermute x6, waiting for transfers between devices: 4.24 us -> 2.49 us  [shifted(): lax.ppermute(array, axis, [((i + shift) % size, i) for i in range(size)])]
    pallas_call x7 -> x8, Pallas kernels: 32.7 us -> 31.8 us  [call(): pl.pallas_call(body, in_specs=specs, out_specs=out_specs, out_shape=outs,...]
  transfers between devices with their start and end apart: 20 -> 20, of which waited for: 11 -> 11; matrix products, arithmetic and copies ran while one was open for 1% -> 1% of each run, Pallas kernels for 8% -> 10%
where the time goes in v2:
time: 118 us; the launch traced here: 117 us
  starting transfers between devices  43.6 us (37%)
  Pallas kernels  31.8 us (27%)
  waiting for transfers between devices  28.3 us (24%)
  local copies, waits for them, and re-layouts  10.7 us (9%)
  between operations  1.61 us (1%)
    pallas_call x8, Pallas kernels, call(): pl.pallas_call(body, in_specs=specs, out_specs=out_specs, out_shape=outs,...  31.8 us
    ppermute x8, starting transfers between devices, hop(): return lax.ppermute(array, (Z, SHARD), pairs)  21.3 us
    ppermute x8, waiting for transfers between devices, hop(): return lax.ppermute(array, (Z, SHARD), pairs)  11.9 us
    ppermute x6, starting transfers between devices, shifted(): lax.ppermute(array, axis, [((i + shift) % size, i) for i in range(size)])  11.6 us
    all_to_all x1, waiting for transfers between devices, local(): everyone = lax.all_to_all(part.reshape(count), TASK, 0, 0, tiled=True)  9.96 us
    unnamed x44, local copies, waits for them, and re-layouts  9.87 us
    all_to_all x1, starting transfers between devices, local(): everyone = lax.all_to_all(part.reshape(count), TASK, 0, 0, tiled=True)  8.95 us
    ppermute x5, waiting for transfers between devices, swapped(): return lax.ppermute(array, SHARD, [(0, 1), (1, 0)])  3.95 us
  transfers between devices with their start and end apart: 20, of which 11 were waited for; matrix products, arithmetic and copies ran while one was open for 1% of the time, Pallas kernels for 10%

profile of v2, /device:TPU:32, one launch (start us, length us, event | category | flops | bytes accessed | tf_op | source)
XLA Modules:
  0.0 116.6 jit_solution(2844977464280645221)
XLA Ops:
  0.6 1.4 %copy-done = bf16[1,1024,768]{2,1,0:T(8,128)(2,1)S(1)} copy-done((bf16[1,1024,768]{2,1,0:T(8,128)(2,1)S(1)}, bf16[1,1024,768]{2,1,0:T(8,128)(2,1)}, u32[]{:S(2)}) %copy-start) | copy-done | bytes 1572888
  2.0 1.4 %copy-done.2 = bf16[1,1024,768]{2,1,0:T(8,128)(2,1)S(1)} copy-done((bf16[1,1024,768]{2,1,0:T(8,128)(2,1)S(1)}, bf16[1,1024,768]{2,1,0:T(8,128)(2,1)}, u32[]{:S(2)}) %copy-start.2) | copy-done | bytes 1572888
  3.5 1.4 %copy-done.4 = bf16[1,768,1024]{2,1,0:T(8,128)(2,1)S(1)} copy-done((bf16[1,768,1024]{2,1,0:T(8,128)(2,1)S(1)}, bf16[1,768,1024]{2,1,0:T(8,128)(2,1)}, u32[]{:S(2)}) %copy-start.4) | copy-done | bytes 1572888
  4.9 1.2 %copy-done.13 = bf16[1,512,1024]{2,1,0:T(8,128)(2,1)S(1)} copy-done((bf16[1,512,1024]{2,1,0:T(8,128)(2,1)S(1)}, bf16[1,512,1024]{2,1,0:T(8,128)(2,1)}, u32[]{:S(2)}) %copy-start.13) | copy-done | bytes 1048600
  6.1 4.4 %shard_map.194 = (f32[512,1024]{1,0:T(8,128)S(1)}, f32[512,768]{1,0:T(8,128)S(1)}, f32[512,768]{1,0:T(8,128)S(1)}, bf16[768,512]{1,0:T(8,128)(2,1)S(1)}, bf16[10...) custom-call(bf16[512,1024]{1,0:T(8,128)(2,1)S(1)} %bitcast.36, bf16[1024,768]{1,0:T(8,128)(2,1)S(1)} %bitcast.24, ...), custom_call_target="tpu_custom_call" | custom-call | flops 2415919104 | tf_op jit(solution)/shard_map/pallas_call | solution.py:56
  10.5 1.1 copy-done.15
  11.6 1.1 copy-done.17
  14.4 1.6 %shard_map.190 = (f32[3,1,512]{2,1,0:T(1,128)S(1)}, f32[4,2048]{1,0:T(4,128)S(1)}) custom-call(s32[5]{0:T(128)S(1)} %stack.19.place_ref, f32[3,1,512]{2,1,0:T(1,128)} %bitcast.41, f32[4,2048]{1,0:T(4,128)} %weight_hbm.1), custom_call_target="tpu_custom_call" | custom-call | flops 99999997952 | tf_op jit(solution)/shard_map/pallas_call | solution.py:56
  16.0 1.6 %collective-permute-start.6 = (f32[4,2048]{1,0:T(4,128)S(1)}, f32[4,2048]{1,0:T(4,128)S(1)}, u32[]{:S(2)}, u32[]{:S(2)}) collective-permute-start(f32[4,2048]{1,0:T(4,128)S(1)} %get-tuple-element.30.r0), channel_id=1, source_target_pairs={{192,0},{0,64},{64,128},{128,192},{193,1},{1,65},{65,129},{129,193... | collective-permute-start | bytes 98312 | tf_op jit(solution)/shard_map/ppermute | solution.py:180
  17.6 2.7 %collective-permute-start.5 = (f32[4,2048]{1,0:T(4,128)S(1)}, f32[4,2048]{1,0:T(4,128)S(1)}, u32[]{:S(2)}, u32[]{:S(2)}) collective-permute-start(f32[4,2048]{1,0:T(4,128)S(1)} %get-tuple-element.30.r0), channel_id=1, source_target_pairs={{128,0},{192,64},{0,128},{64,192},{129,1},{193,65},{1,129},{65,193... | collective-permute-start | bytes 98312 | tf_op jit(solution)/shard_map/ppermute | solution.py:180
  20.3 1.4 %collective-permute-start.4 = (f32[4,2048]{1,0:T(4,128)S(1)}, f32[4,2048]{1,0:T(4,128)S(1)}, u32[]{:S(2)}, u32[]{:S(2)}) collective-permute-start(f32[4,2048]{1,0:T(4,128)S(1)} %get-tuple-element.30.r0), channel_id=1, source_target_pairs={{64,0},{128,64},{192,128},{0,192},{65,1},{129,65},{193,129},{1,193... | collective-permute-start | bytes 98312 | tf_op jit(solution)/shard_map/ppermute | solution.py:180
  21.8 1.3 %collective-permute-done.5.r2 = f32[4,2048]{1,0:T(4,128)S(1)} collective-permute-done((f32[4,2048]{1,0:T(4,128)S(1)}, f32[4,2048]{1,0:T(4,128)S(1)}, u32[]{:S(2)}, u32[]{:S(2)}) %collective-permute-start.5) | collective-permute-done | bytes 32800 | tf_op jit(solution)/shard_map/ppermute | solution.py:180
  23.0 1.2 %collective-permute-done.4.r1 = f32[4,2048]{1,0:T(4,128)S(1)} collective-permute-done((f32[4,2048]{1,0:T(4,128)S(1)}, f32[4,2048]{1,0:T(4,128)S(1)}, u32[]{:S(2)}, u32[]{:S(2)}) %collective-permute-start.4) | collective-permute-done | bytes 32800 | tf_op jit(solution)/shard_map/ppermute | solution.py:180
  24.3 1.7 %collective-permute-start.9 = (f32[16,2048]{1,0:T(8,128)S(1)}, f32[16,2048]{1,0:T(8,128)S(1)}, u32[]{:S(2)}, u32[]{:S(2)}) collective-permute-start(f32[16,2048]{1,0:T(8,128)S(1)} %shard_map.191.r0), channel_id=1, source_target_pairs={{48,0},{0,16},{16,32},{32,48},{49,1},{1,17},{17,33},{33,49},{50,2}... | collective-permute-start | bytes 393224 | tf_op jit(solution)/shard_map/ppermute | solution.py:180
  25.9 2.9 %collective-permute-start.8 = (f32[16,2048]{1,0:T(8,128)S(1)}, f32[16,2048]{1,0:T(8,128)S(1)}, u32[]{:S(2)}, u32[]{:S(2)}) collective-permute-start(f32[16,2048]{1,0:T(8,128)S(1)} %shard_map.191.r0), channel_id=1, source_target_pairs={{32,0},{48,16},{0,32},{16,48},{33,1},{49,17},{1,33},{17,49},{34,2}... | collective-permute-start | bytes 393224 | tf_op jit(solution)/shard_map/ppermute | solution.py:180
  28.8 1.3 %collective-permute-start.7 = (f32[16,2048]{1,0:T(8,128)S(1)}, f32[16,2048]{1,0:T(8,128)S(1)}, u32[]{:S(2)}, u32[]{:S(2)}) collective-permute-start(f32[16,2048]{1,0:T(8,128)S(1)} %shard_map.191.r0), channel_id=1, source_target_pairs={{16,0},{32,16},{48,32},{0,48},{17,1},{33,17},{49,33},{1,49},{18,2}... | collective-permute-start | bytes 393224 | tf_op jit(solution)/shard_map/ppermute | solution.py:180
  30.2 6.3 %collective-permute-start.3 = (f32[3,1,512]{2,1,0:T(1,128)S(1)}, f32[3,1,512]{2,1,0:T(1,128)S(1)}, u32[]{:S(2)}, u32[]{:S(2)}) collective-permute-start(f32[3,1,512]{2,1,0:T(1,128)S(1)} %get-tuple-element.29.own), channel_id=1, source_target_pairs={{8,0},{10,2},{12,4},{14,6},{0,8},{2,10},{4,12},{6,14},{11,1},{13,3... | collective-permute-start | bytes 18440 | tf_op jit(solution)/shard_map/ppermute | solution.py:200
  36.5 1.6 %collective-permute-done.3.h3 = f32[3,1,512]{2,1,0:T(1,128)S(1)} collective-permute-done((f32[3,1,512]{2,1,0:T(1,128)S(1)}, f32[3,1,512]{2,1,0:T(1,128)S(1)}, u32[]{:S(2)}, u32[]{:S(2)}) %collective-permute-start.3) | collective-permute-done | bytes 6176 | tf_op jit(solution)/shard_map/ppermute | solution.py:200
  38.1 5.5 %collective-permute-start.2 = (f32[3,1,512]{2,1,0:T(1,128)S(1)}, f32[3,1,512]{2,1,0:T(1,128)S(1)}, u32[]{:S(2)}, u32[]{:S(2)}) collective-permute-start(f32[3,1,512]{2,1,0:T(1,128)S(1)} %get-tuple-element.29.own), channel_id=1, source_target_pairs={{6,0},{8,2},{10,4},{12,6},{14,8},{0,10},{2,12},{4,14},{13,1},{15,3... | collective-permute-start | bytes 18440 | tf_op jit(solution)/shard_map/ppermute | solution.py:200
  43.6 1.6 %collective-permute-done.2.h2 = f32[3,1,512]{2,1,0:T(1,128)S(1)} collective-permute-done((f32[3,1,512]{2,1,0:T(1,128)S(1)}, f32[3,1,512]{2,1,0:T(1,128)S(1)}, u32[]{:S(2)}, u32[]{:S(2)}) %collective-permute-start.2) | collective-permute-done | bytes 6176 | tf_op jit(solution)/shard_map/ppermute | solution.py:200
  45.9 2.9 %collective-permute-done.1.h1 = f32[3,1,512]{2,1,0:T(1,128)S(1)} collective-permute-done((f32[3,1,512]{2,1,0:T(1,128)S(1)}, f32[3,1,512]{2,1,0:T(1,128)S(1)}, u32[]{:S(2)}, u32[]{:S(2)}) %collective-permute-start.1) | collective-permute-done | bytes 6176 | tf_op jit(solution)/shard_map/ppermute | solution.py:200
  49.5 1.8 %shard_map.192 = (f32[3,2048]{1,0:T(4,128)S(1)}, f32[3,2048]{1,0:T(4,128)S(1)}, f32[3,2048]{1,0:T(4,128)S(1)}, f32[3,2048]{1,0:T(4,128)S(1)}) custom-call(s32[5]{0:T(128)S(1)} %stack.19.place_ref, f32[3,1,512]{2,1,0:T(1,128)S(1)} %get-tuple-element.29.own, f32[3,1,512]{2,1,0:T(1,128)S(1)} %collective-permute-done.h0, ...), custom_call_target="tpu_custom_call" | custom-call | flops 4194304 | tf_op jit(solution)/shard_map/pallas_call | solution.py:56
  51.3 1.2 %collective-permute-start.11 = (f32[3,2048]{1,0:T(4,128)S(1)}, f32[3,2048]{1,0:T(4,128)S(1)}, u32[]{:S(2)}, u32[]{:S(2)}) collective-permute-start(f32[3,2048]{1,0:T(4,128)S(1)} %get-tuple-element.32), channel_id=1, source_target_pairs={{0,2},{2,4},{4,6},{6,8},{8,10},{10,12},{12,14},{14,0},{1,5},{3,7},... | collective-permute-start | bytes 73736 | tf_op jit(solution)/shard_map/ppermute | solution.py:200
  52.5 4.9 %collective-permute-start.12 = (f32[3,2048]{1,0:T(4,128)S(1)}, f32[3,2048]{1,0:T(4,128)S(1)}, u32[]{:S(2)}, u32[]{:S(2)}) collective-permute-start(f32[3,2048]{1,0:T(4,128)S(1)} %get-tuple-element.33), channel_id=1, source_target_pairs={{0,6},{2,8},{4,10},{6,12},{8,14},{10,0},{12,2},{14,4},{1,13},{3,15... | collective-permute-start | bytes 73736 | tf_op jit(solution)/shard_map/ppermute | solution.py:200
  57.4 1.4 %collective-permute-start.13 = (f32[3,2048]{1,0:T(4,128)S(1)}, f32[3,2048]{1,0:T(4,128)S(1)}, u32[]{:S(2)}, u32[]{:S(2)}) collective-permute-start(f32[3,2048]{1,0:T(4,128)S(1)} %get-tuple-element.34), channel_id=1, source_target_pairs={{0,8},{2,10},{4,12},{6,14},{8,0},{10,2},{12,4},{14,6},{1,11},{3,13... | collective-permute-start | bytes 73736 | tf_op jit(solution)/shard_map/ppermute | solution.py:200
  59.4 1.8 %collective-permute-done.12.m2 = f32[3,2048]{1,0:T(4,128)S(1)} collective-permute-done((f32[3,2048]{1,0:T(4,128)S(1)}, f32[3,2048]{1,0:T(4,128)S(1)}, u32[]{:S(2)}, u32[]{:S(2)}) %collective-permute-start.12) | collective-permute-done | bytes 24608 | tf_op jit(solution)/shard_map/ppermute | solution.py:200
  61.2 4.0 %collective-permute-done.13.m3 = f32[3,2048]{1,0:T(4,128)S(1)} collective-permute-done((f32[3,2048]{1,0:T(4,128)S(1)}, f32[3,2048]{1,0:T(4,128)S(1)}, u32[]{:S(2)}, u32[]{:S(2)}) %collective-permute-start.13) | collective-permute-done | bytes 24608 | tf_op jit(solution)/shard_map/ppermute | solution.py:200
  66.2 7.9 %shard_map.195 = (f32[1024,768]{1,0:T(8,128)S(1)}, f32[1024,768]{1,0:T(8,128)S(1)}, f32[768,1024]{1,0:T(8,128)S(1)}, f32[16,128]{1,0:T(8,128)S(1)}) custom-call(f32[512,1024]{1,0:T(8,128)S(1)} %get-tuple-element.35.own_ref, f32[512,1024]{1,0:T(8,128)} %collective-permute-done.15.recv_ref, bf16[512,1024]{1,0:T(8,128)(2,1)S(1)} %bitcast.37, ...), custom_call_target="tpu_custom_call" | custom-call | flops 3221225472 | tf_op jit(solution)/shard_map/pallas_call | solution.py:56
  75.6 14.5 %shard_map.196 = (bf16[1024,768]{1,0:T(8,128)(2,1)}, bf16[1024,768]{1,0:T(8,128)(2,1)}, bf16[768,1024]{1,0:T(8,128)(2,1)}, f32[3,1,512]{2,1,0:T(1,128)S(1)}, f32...) custom-call(s32[5]{0:T(128)S(1)} %stack.19.place_ref, f32[3,2048]{1,0:T(4,128)S(1)} %shard_map.193.mine_ref, ...), custom_call_target="tpu_custom_call" | custom-call | flops 2415919104 | tf_op jit(solution)/shard_map/pallas_call | solution.py:56
  90.6 2.3 %collective-permute-done.17.recv_ref = f32[256,1024]{1,0:T(8,128)S(1)} collective-permute-done((f32[256,1024]{1,0:T(8,128)S(1)}, f32[256,1024]{1,0:T(8,128)S(1)}, u32[]{:S(2)}, u32[]{:S(2)}) %collective-permute-start.17) | collective-permute-done | bytes 1048608 | tf_op jit(solution)/shard_map/ppermute | solution.py:184
  95.8 9.0 %all-to-all-start = ((f32[128,1,1]{2,1,0:T(1,128)}), f32[128,1,1]{2,1,0:T(1,128)S(1)}, u32[]{:S(2)}, u32[]{:S(2)}) async-start(f32[128,1,1]{2,1,0:T(1,128)} %copy.21), calls=%async_computation | async-start | bytes 131072 | tf_op jit(solution)/shard_map/all_to_all | solution.py:454
  105.9 10.0 %all-to-all-done = f32[128,1,1]{2,1,0:T(1,128)S(1)} async-done(((f32[128,1,1]{2,1,0:T(1,128)}), f32[128,1,1]{2,1,0:T(1,128)S(1)}, u32[]{:S(2)}, u32[]{:S(2)}) %all-to-all-start) | async-done | bytes 544 | tf_op jit(solution)/shard_map/all_to_all | solution.py:454
  (64 shorter events, 10.6 us)
Async XLA Ops:
  13.7 52.4 %collective-permute-start.15 = (f32[512,1024]{1,0:T(8,128)S(1)}, f32[512,1024]{1,0:T(8,128)}, u32[]{:S(2)}, u32[]{:S(2)}) collective-permute-start(f32[512,1024]{1,0:T(8,128)S(1)} %get-tuple-element.35.own_ref), channel_id=1, source_target_pairs={{0,1},{1,0},{2,3},{3,2},{4,5},{5,4},{6,7},{7,6},{8,9},{9,8},{10,11... | collective-permute-start | bytes 6291464 | tf_op jit(solution)/shard_map/ppermute | solution.py:184
  14.4 51.7 %copy-start.5 = (bf16[1,768,1024]{2,1,0:T(8,128)(2,1)S(1)}, bf16[1,768,1024]{2,1,0:T(8,128)(2,1)}, u32[]{:S(2)}) copy-start(bf16[1,768,1024]{2,1,0:T(8,128)(2,1)} %param.21) | copy-start | bytes 4718596
  14.4 51.7 %copy-start.14 = (bf16[1,512,1024]{2,1,0:T(8,128)(2,1)S(1)}, bf16[1,512,1024]{2,1,0:T(8,128)(2,1)}, u32[]{:S(2)}) copy-start(bf16[1,512,1024]{2,1,0:T(8,128)(2,1)} %param.16) | copy-start | bytes 3145732
  14.4 51.7 %copy-start.16 = (f32[512,768]{1,0:T(8,128)S(1)}, f32[512,768]{1,0:T(8,128)}, u32[]{:S(2)}) copy-start(f32[512,768]{1,0:T(8,128)} %copy-done.15) | copy-start | bytes 4718596
  14.4 51.7 %copy-start.18 = (f32[512,768]{1,0:T(8,128)S(1)}, f32[512,768]{1,0:T(8,128)}, u32[]{:S(2)}) copy-start(f32[512,768]{1,0:T(8,128)} %copy-done.17) | copy-start | bytes 4718596
  14.4 51.7 %copy-start.20 = (bf16[768,512]{1,0:T(8,128)(2,1)S(1)}, bf16[768,512]{1,0:T(8,128)(2,1)}, u32[]{:S(2)}) copy-start(bf16[768,512]{1,0:T(8,128)(2,1)} %copy-done.19) | copy-start | bytes 2359300
  16.0 5.7 %collective-permute-start.6 = (f32[4,2048]{1,0:T(4,128)S(1)}, f32[4,2048]{1,0:T(4,128)S(1)}, u32[]{:S(2)}, u32[]{:S(2)}) collective-permute-start(f32[4,2048]{1,0:T(4,128)S(1)} %get-tuple-element.30.r0), channel_id=1, source_target_pairs={{192,0},{0,64},{64,128},{128,192},{193,1},{1,65},{65,129},{129,193... | collective-permute-start | bytes 98312 | tf_op jit(solution)/shard_map/ppermute | solution.py:180
  17.6 5.4 %collective-permute-start.5 = (f32[4,2048]{1,0:T(4,128)S(1)}, f32[4,2048]{1,0:T(4,128)S(1)}, u32[]{:S(2)}, u32[]{:S(2)}) collective-permute-start(f32[4,2048]{1,0:T(4,128)S(1)} %get-tuple-element.30.r0), channel_id=1, source_target_pairs={{128,0},{192,64},{0,128},{64,192},{129,1},{193,65},{1,129},{65,193... | collective-permute-start | bytes 98312 | tf_op jit(solution)/shard_map/ppermute | solution.py:180
  20.3 3.9 %collective-permute-start.4 = (f32[4,2048]{1,0:T(4,128)S(1)}, f32[4,2048]{1,0:T(4,128)S(1)}, u32[]{:S(2)}, u32[]{:S(2)}) collective-permute-start(f32[4,2048]{1,0:T(4,128)S(1)} %get-tuple-element.30.r0), channel_id=1, source_target_pairs={{64,0},{128,64},{192,128},{0,192},{65,1},{129,65},{193,129},{1,193... | collective-permute-start | bytes 98312 | tf_op jit(solution)/shard_map/ppermute | solution.py:180
  24.3 25.2 %collective-permute-start.9 = (f32[16,2048]{1,0:T(8,128)S(1)}, f32[16,2048]{1,0:T(8,128)S(1)}, u32[]{:S(2)}, u32[]{:S(2)}) collective-permute-start(f32[16,2048]{1,0:T(8,128)S(1)} %shard_map.191.r0), channel_id=1, source_target_pairs={{48,0},{0,16},{16,32},{32,48},{49,1},{1,17},{17,33},{33,49},{50,2}... | collective-permute-start | bytes 393224 | tf_op jit(solution)/shard_map/ppermute | solution.py:180
  25.9 23.5 %collective-permute-start.8 = (f32[16,2048]{1,0:T(8,128)S(1)}, f32[16,2048]{1,0:T(8,128)S(1)}, u32[]{:S(2)}, u32[]{:S(2)}) collective-permute-start(f32[16,2048]{1,0:T(8,128)S(1)} %shard_map.191.r0), channel_id=1, source_target_pairs={{32,0},{48,16},{0,32},{16,48},{33,1},{49,17},{1,33},{17,49},{34,2}... | collective-permute-start | bytes 393224 | tf_op jit(solution)/shard_map/ppermute | solution.py:180
  28.8 20.7 %collective-permute-start.7 = (f32[16,2048]{1,0:T(8,128)S(1)}, f32[16,2048]{1,0:T(8,128)S(1)}, u32[]{:S(2)}, u32[]{:S(2)}) collective-permute-start(f32[16,2048]{1,0:T(8,128)S(1)} %shard_map.191.r0), channel_id=1, source_target_pairs={{16,0},{32,16},{48,32},{0,48},{17,1},{33,17},{49,33},{1,49},{18,2}... | collective-permute-start | bytes 393224 | tf_op jit(solution)/shard_map/ppermute | solution.py:180
  30.2 7.9 %collective-permute-start.3 = (f32[3,1,512]{2,1,0:T(1,128)S(1)}, f32[3,1,512]{2,1,0:T(1,128)S(1)}, u32[]{:S(2)}, u32[]{:S(2)}) collective-permute-start(f32[3,1,512]{2,1,0:T(1,128)S(1)} %get-tuple-element.29.own), channel_id=1, source_target_pairs={{8,0},{10,2},{12,4},{14,6},{0,8},{2,10},{4,12},{6,14},{11,1},{13,3... | collective-permute-start | bytes 18440 | tf_op jit(solution)/shard_map/ppermute | solution.py:200
  38.1 7.1 %collective-permute-start.2 = (f32[3,1,512]{2,1,0:T(1,128)S(1)}, f32[3,1,512]{2,1,0:T(1,128)S(1)}, u32[]{:S(2)}, u32[]{:S(2)}) collective-permute-start(f32[3,1,512]{2,1,0:T(1,128)S(1)} %get-tuple-element.29.own), channel_id=1, source_target_pairs={{6,0},{8,2},{10,4},{12,6},{14,8},{0,10},{2,12},{4,14},{13,1},{15,3... | collective-permute-start | bytes 18440 | tf_op jit(solution)/shard_map/ppermute | solution.py:200
  45.2 3.6 %collective-permute-start.1 = (f32[3,1,512]{2,1,0:T(1,128)S(1)}, f32[3,1,512]{2,1,0:T(1,128)S(1)}, u32[]{:S(2)}, u32[]{:S(2)}) collective-permute-start(f32[3,1,512]{2,1,0:T(1,128)S(1)} %get-tuple-element.29.own), channel_id=1, source_target_pairs={{2,0},{4,2},{6,4},{8,6},{10,8},{12,10},{14,12},{0,14},{5,1},{7,3},... | collective-permute-start | bytes 18440 | tf_op jit(solution)/shard_map/ppermute | solution.py:200
  48.8 0.7 collective-permute-start
  51.3 8.1 %collective-permute-start.11 = (f32[3,2048]{1,0:T(4,128)S(1)}, f32[3,2048]{1,0:T(4,128)S(1)}, u32[]{:S(2)}, u32[]{:S(2)}) collective-permute-start(f32[3,2048]{1,0:T(4,128)S(1)} %get-tuple-element.32), channel_id=1, source_target_pairs={{0,2},{2,4},{4,6},{6,8},{8,10},{10,12},{12,14},{14,0},{1,5},{3,7},... | collective-permute-start | bytes 73736 | tf_op jit(solution)/shard_map/ppermute | solution.py:200
  52.5 8.8 %collective-permute-start.12 = (f32[3,2048]{1,0:T(4,128)S(1)}, f32[3,2048]{1,0:T(4,128)S(1)}, u32[]{:S(2)}, u32[]{:S(2)}) collective-permute-start(f32[3,2048]{1,0:T(4,128)S(1)} %get-tuple-element.33), channel_id=1, source_target_pairs={{0,6},{2,8},{4,10},{6,12},{8,14},{10,0},{12,2},{14,4},{1,13},{3,15... | collective-permute-start | bytes 73736 | tf_op jit(solution)/shard_map/ppermute | solution.py:200
  57.4 7.8 %collective-permute-start.13 = (f32[3,2048]{1,0:T(4,128)S(1)}, f32[3,2048]{1,0:T(4,128)S(1)}, u32[]{:S(2)}, u32[]{:S(2)}) collective-permute-start(f32[3,2048]{1,0:T(4,128)S(1)} %get-tuple-element.34), channel_id=1, source_target_pairs={{0,8},{2,10},{4,12},{6,14},{8,0},{10,2},{12,4},{14,6},{1,11},{3,13... | collective-permute-start | bytes 73736 | tf_op jit(solution)/shard_map/ppermute | solution.py:200
  58.8 6.4 %collective-permute-start.10 = (f32[3,2048]{1,0:T(4,128)S(1)}, f32[3,2048]{1,0:T(4,128)S(1)}, u32[]{:S(2)}, u32[]{:S(2)}) collective-permute-start(f32[3,2048]{1,0:T(4,128)S(1)} %get-tuple-element.31.own), channel_id=1, source_target_pairs={{1,15},{3,1},{5,3},{7,5},{9,7},{11,9},{13,11},{15,13},{17,31},{19,... | collective-permute-start | bytes 73736 | tf_op jit(solution)/shard_map/ppermute | solution.py:200
  65.8 8.9 %collective-permute-start.14 = (f32[3,2048]{1,0:T(4,128)S(1)}, f32[3,2048]{1,0:T(4,128)S(1)}, u32[]{:S(2)}, u32[]{:S(2)}) collective-permute-start(f32[3,2048]{1,0:T(4,128)S(1)} %shard_map.193.mine_ref), channel_id=1, source_target_pairs={{0,1},{1,0},{2,3},{3,2},{4,5},{5,4},{6,7},{7,6},{8,9},{9,8},{10,11... | collective-permute-start | bytes 73736 | tf_op jit(solution)/shard_map/ppermute | solution.py:184
  66.1 9.4 %copy-start.1 = (bf16[1,1024,768]{2,1,0:T(8,128)(2,1)S(1)}, bf16[1,1024,768]{2,1,0:T(8,128)(2,1)}, u32[]{:S(2)}) copy-start(bf16[1,1024,768]{2,1,0:T(8,128)(2,1)} %param.19) | copy-start | bytes 4718596
  66.1 9.4 %copy-start.3 = (bf16[1,1024,768]{2,1,0:T(8,128)(2,1)S(1)}, bf16[1,1024,768]{2,1,0:T(8,128)(2,1)}, u32[]{:S(2)}) copy-start(bf16[1,1024,768]{2,1,0:T(8,128)(2,1)} %param.20) | copy-start | bytes 4718596
  66.1 9.4 %copy-start.7 = (bf16[1,512,1024]{2,1,0:T(8,128)(2,1)S(1)}, bf16[1,512,1024]{2,1,0:T(8,128)(2,1)}, u32[]{:S(2)}) copy-start(bf16[1,512,1024]{2,1,0:T(8,128)(2,1)} %param.17) | copy-start | bytes 3145732
  66.2 9.4 %copy-start.8 = (f32[3,2048]{1,0:T(4,128)S(1)}, f32[3,2048]{1,0:T(4,128)}, u32[]{:S(2)}) copy-start(f32[3,2048]{1,0:T(4,128)} %in_w_ref.1) | copy-start | bytes 73732
  66.2 9.3 %copy-start.9 = (f32[512,5]{0,1:T(8,128)S(1)}, f32[512,5]{0,1:T(8,128)}, u32[]{:S(2)}) copy-start(f32[512,5]{0,1:T(8,128)} %param.28) | copy-start | bytes 30724
  66.2 9.3 %copy-start.10 = (f32[2048]{0:T(1024)S(1)}, f32[2048]{0:T(1024)}, u32[]{:S(2)}) copy-start(f32[2048]{0:T(1024)} %param.27) | copy-start | bytes 24580
  74.1 1.4 %collective-permute-start.16 = (f32[16,128]{1,0:T(8,128)S(1)}, f32[16,128]{1,0:T(8,128)S(1)}, u32[]{:S(2)}, u32[]{:S(2)}) collective-permute-start(f32[16,128]{1,0:T(8,128)S(1)} %get-tuple-element.41.sq_ref), channel_id=1, source_target_pairs={{0,1},{1,0},{2,3},{3,2},{4,5},{5,4},{6,7},{7,6},{8,9},{9,8},{10,11... | collective-permute-start | bytes 24584 | tf_op jit(solution)/shard_map/ppermute | solution.py:184
  75.6 17.3 %copy-start.6 = (bf16[1,512,1024]{2,1,0:T(8,128)(2,1)S(1)}, bf16[1,512,1024]{2,1,0:T(8,128)(2,1)}, u32[]{:S(2)}) copy-start(bf16[1,512,1024]{2,1,0:T(8,128)(2,1)} %param.18) | copy-start | bytes 3145732
  90.1 2.7 %collective-permute-start.17 = (f32[256,1024]{1,0:T(8,128)S(1)}, f32[256,1024]{1,0:T(8,128)S(1)}, u32[]{:S(2)}, u32[]{:S(2)}) collective-permute-start(f32[256,1024]{1,0:T(8,128)S(1)} %get-tuple-element.51), channel_id=1, source_target_pairs={{0,1},{1,0},{2,3},{3,2},{4,5},{5,4},{6,7},{7,6},{8,9},{9,8},{10,11... | collective-permute-start | bytes 3145736 | tf_op jit(solution)/shard_map/ppermute | solution.py:184
  93.8 1.2 %collective-permute-start.18 = (f32[1,128]{1,0:T(1,128)S(1)}, f32[1,128]{1,0:T(1,128)S(1)}, u32[]{:S(2)}, u32[]{:S(2)}) collective-permute-start(f32[1,128]{1,0:T(1,128)S(1)} %shard_map.197), channel_id=1, source_target_pairs={{0,1},{1,0},{2,3},{3,2},{4,5},{5,4},{6,7},{7,6},{8,9},{9,8},{10,11... | collective-permute-start | bytes 1544 | tf_op jit(solution)/shard_map/ppermute | solution.py:184
  95.8 20.1 %all-to-all-start = ((f32[128,1,1]{2,1,0:T(1,128)}), f32[128,1,1]{2,1,0:T(1,128)S(1)}, u32[]{:S(2)}, u32[]{:S(2)}) async-start(f32[128,1,1]{2,1,0:T(1,128)} %copy.21), calls=%async_computation | async-start | bytes 131072 | tf_op jit(solution)/shard_map/all_to_all | solution.py:454
  (9 other events, 27.3 us)

commit v3 on v2

--- a/solution.py
+++ b/solution.py
@@ -151,15 +151,15 @@
     )
 
 
-def recurrent_kernel(place_ref, own, h0, h1, h2, h3, r0, r1, r2, r3, o0, o1, o2, o3, stack):
-    px, py, pz, core = place_ref[0], place_ref[1], place_ref[2], place_ref[3]
+def recurrent_kernel(info_ref, own, h1, h2, h3, h4, across, r0, r1, r2, r3, o0, o1, o2, o3, stack):
+    px, py, pz, core = (info_ref[k : k + 1, 0:1] for k in range(4))
     state = own.shape[2]
     stack[...] = jnp.zeros_like(stack)
     for j in range(own.shape[0]):
-        stack[j : j + 1, :] = jnp.where(core == 0, own[j], h0[j])
-        stack[8 + j : 9 + j, :] = h1[j]
-        stack[16 + j : 17 + j, :] = h2[j]
-        stack[24 + j : 25 + j, :] = h3[j]
+        stack[j : j + 1, :] = jnp.where(core == 0, own[j], h1[j])
+        stack[8 + j : 9 + j, :] = jnp.where(core == 0, h1[j], across[j])
+        stack[16 + j : 17 + j, :] = jnp.where(core == 0, h3[j], h2[j])
+        stack[24 + j : 25 + j, :] = jnp.where(core == 0, h4[j], h3[j])
     shape = (state, 128)
     row = lax.broadcasted_iota(jnp.int32, shape, 0)
     col = lax.broadcasted_iota(jnp.int32, shape, 1)
@@ -187,34 +187,43 @@
 HOPS = ((None, -1), (1, 2), (3, -2), (4, -3))
 
 
-def hop(array, index, back):
+def hop(array, amounts):
     size = lax.axis_size(Z)
     pairs = []
-    for core in range(2):
-        by = HOPS[index][core]
-        if by is None:
-            continue
-        for i in range(size):
-            there = (i + by) % size
-            pairs.append((there * 2 + core, i * 2 + core) if back else (i * 2 + core, there * 2 + core))
+    for core, by in enumerate(amounts):
+        if by is not None:
+            pairs += [(i * 2 + core, (i + by) % size * 2 + core) for i in range(size)]
     return lax.ppermute(array, (Z, SHARD), pairs)
 
 
-def first_kernel(place_ref, hidden_hbm, weight_hbm, hidden_ref, weight_ref, sems):
+def states_along_z(hidden):
+    held = [hidden]
+    for amounts in ((-1, 1), (-1, 1), (-1, 1), (-1, None)):
+        held.append(hop(held[-1], amounts))
+    across = lax.ppermute(held[2], SHARD, [(0, 1)])
+    return held[1:] + [across]
+
+
+def first_kernel(place_ref, hidden_hbm, weight_hbm, hidden_ref, weight_ref, info_ref, sems):
     copies = (
         pltpu.make_async_copy(weight_hbm, weight_ref, sems.at[0]),
         pltpu.make_async_copy(hidden_hbm, hidden_ref, sems.at[1]),
     )
     for copy in copies:
         copy.start()
+    row = lax.broadcasted_iota(jnp.int32, info_ref.shape, 0)
+    info = jnp.zeros(info_ref.shape, jnp.int32)
+    for k in range(5):
+        info = jnp.where(row == k, place_ref[k], info)
+    info_ref[...] = info
     for copy in copies:
         copy.wait()
 
 
 def brought(place, hidden, weight):
     return call(
-        first_kernel, (place, hidden, weight), [IN_SMEM] + [IN_HBM] * 2, vmem((hidden.shape, f32), (weight.shape, f32)),
-        [IN_VMEM] * 2, [pltpu.SemaphoreType.DMA((2,))], 1, 100_000_000_000,
+        first_kernel, (place, hidden, weight), [IN_SMEM] + [IN_HBM] * 2, vmem((hidden.shape, f32), (weight.shape, f32), ((8, 128), jnp.int32)),
+        [IN_VMEM] * 3, [pltpu.SemaphoreType.DMA((2,))], 1, 100_000_000_000,
     )
 
 
@@ -223,32 +232,36 @@
         out_ref[4 * k : 4 * k + 4, :] = r_ref[...]
 
 
-def sum_kernel(place_ref, own, m0, m1, m2, m3, out_ref):
-    out_ref[...] = (jnp.where(place_ref[3] == 0, own[...], m0[...]) + m1[...]) + (m2[...] + m3[...])
+def sum_kernel(info_ref, own, m0, m1, m2, m3, out_ref):
+    out_ref[...] = (jnp.where(info_ref[3:4, 0:1] == 0, own[...], m0[...]) + m1[...]) + (m2[...] + m3[...])
 
 
 def recurrent_line(weight):
-    others = [shifted(weight, X, k) for k in (1, 2, 3)]
+    above = shifted(weight, X, 1)
+    below = shifted(weight, X, 3)
+    others = (above, shifted(above, X, 1), below)
     shape = (4 * weight.shape[0], weight.shape[1])
     return call(line_kernel, (weight, *others), [IN_VMEM] * 4, vmem((shape, f32)), [IN_VMEM], (), 1, 1 << 16)[0]
 
 
-def recurrent(hidden, hids, line, place):
-    plane = [line] + [shifted(line, Y, k) for k in (1, 2, 3)]
+def recurrent(hidden, hids, line, info):
+    plane = [line]
+    for k in (1, 2, 3):
+        plane.append(shifted(line, Y, k))
     out = (hidden.shape[0], line.shape[1])
     parts = call(
-        recurrent_kernel, (place, hidden, *hids, *plane), [IN_SMEM] + [IN_VMEM] * 9,
+        recurrent_kernel, (info, hidden, *hids, *plane), [IN_VMEM] * 11,
         vmem(*[(out, f32)] * 4), [IN_VMEM] * 4, [pltpu.VMEM((32, hidden.shape[2]), f32)], 4, 1 << 22,
     )
-    moved = [hop(part, k, False) for k, part in enumerate(parts)]
-    return call(
-        sum_kernel, (place, parts[0], *moved), [IN_SMEM] + [IN_VMEM] * 5,
+    moved = [hop(part, HOPS[k]) for k, part in enumerate(parts)]
+    return call(
+        sum_kernel, (info, parts[0], *moved), [IN_VMEM] * 6,
         vmem((out, f32)), [IN_VMEM], (), 1, 1 << 16,
     )[0]
 
 
 def update_kernel(
-    place_ref,
+    info_ref,
     mine_ref, theirs_ref, sq_ref, sq_recv_ref, in_w_ref, bias_ref, cell_ref, ctx_w_ref, mlp_ref,
     wg_ref, wu_ref, wd_ref, gg_ref, gu_ref, gd_ref, meta_ref,
     up_g_hbm, up_u_hbm, up_d_hbm, hidden_ref, new_cell_ref, send_ref, keep_ref,
@@ -263,7 +276,7 @@
     rms = jnp.sqrt(total / entries + epsilon)
     rms_g, rms_p = rms[0:3], rms[8:11]
     logs = jnp.log(rms)
-    fraction = place_ref[4].astype(f32) / STEPS
+    fraction = info_ref[4:5, 0:1].astype(f32) / STEPS
     in_w = in_w_ref[...]
     lstm_in = (
         (logs[0:3] * in_w[0:1] + logs[8:11] * in_w[1:2] + fraction * in_w[2:3])
@@ -376,9 +389,9 @@
 
     lax.fori_loop(0, count, body, 0)
     half = acc.shape[0] // 2
-    core = place_ref[3]
-    keep_ref[...] = acc[pl.ds(pl.multiple_of(core * half, half), half), :]
-    send_ref[...] = acc[pl.ds(pl.multiple_of((1 - core) * half, half), half), :]
+    lower = info_ref[3:4, 0:1] == 0
+    keep_ref[...] = jnp.where(lower, acc[:half], acc[half:])
+    send_ref[...] = jnp.where(lower, acc[half:], acc[:half])
     for j in range(count):
         for copy in results(j):
             copy.wait()
@@ -387,7 +400,7 @@
 STRIP = 64
 
 
-def update(place, mine, theirs, sums, sums_recv, in_w, bias, cell, ctx_w, mlp, wg, wu, wd, gg, gu, gd, meta):
+def update(info, mine, theirs, sums, sums_recv, in_w, bias, cell, ctx_w, mlp, wg, wu, wd, gg, gu, gd, meta):
     tok, width = meta.shape
     hid = wg.shape[1]
     outs = [pltpu.HBM(wg.shape, bf16), pltpu.HBM(wu.shape, bf16), pltpu.HBM(wd.shape, bf16)]
@@ -407,27 +420,37 @@
         pltpu.VMEM((CHUNK, width), bf16),
         pltpu.VMEM((tok, width), f32),
     ]
-    operands = (place, mine, theirs, sums, sums_recv, in_w, bias, cell, ctx_w, mlp, wg, wu, wd, gg, gu, gd, meta)
-    return call(
-        update_kernel, operands, [IN_SMEM] + [IN_VMEM] * 16,
+    operands = (info, mine, theirs, sums, sums_recv, in_w, bias, cell, ctx_w, mlp, wg, wu, wd, gg, gu, gd, meta)
+    return call(
+        update_kernel, operands, [IN_VMEM] * 17,
         outs, [IN_HBM] * 3 + [IN_VMEM] * 4, scratch, 20, 6 * tok * width * hid,
     )
 
 
-def loss_kernel(scale, place_ref, keep_ref, recv_ref, want_ref, out_ref):
+def loss_kernel(scale, info_ref, keep_ref, recv_ref, want_ref, out_ref):
     half = keep_ref.shape[0]
-    mine = pl.ds(pl.multiple_of(place_ref[3] * half, half), half)
-    error = keep_ref[...] + recv_ref[...] - want_ref[mine, :].astype(f32)
+    want = jnp.where(info_ref[3:4, 0:1] == 0, want_ref[:half].astype(f32), want_ref[half:].astype(f32))
+    error = keep_ref[...] + recv_ref[...] - want
     total = jnp.sum(jnp.sum(error * error, axis=0, keepdims=True), axis=1, keepdims=True)
     out_ref[...] = jnp.broadcast_to(scale * total, out_ref.shape)
 
 
-def loss_part(place, keep, recv, want, count):
+def loss_part(info, keep, recv, want, count):
     scale = 0.5 / (want.shape[0] * want.shape[1]) / count
     return call(
-        functools.partial(loss_kernel, scale), (place, keep, recv, want), [IN_SMEM] + [IN_VMEM] * 3,
+        functools.partial(loss_kernel, scale), (info, keep, recv, want), [IN_VMEM] * 4,
         vmem(((1, 128), f32)), [IN_VMEM], (), 8,
     )[0]
+
+
+def spread_kernel(mine_ref, theirs_ref, out_ref):
+    both = mine_ref[:, 0:1] + theirs_ref[:, 0:1]
+    for k in range(out_ref.shape[0]):
+        out_ref[k] = both
+
+
+def spread(part, count):
+    return call(spread_kernel, (part, swapped(part)), [IN_VMEM] * 2, vmem(((count, 1, 1), f32)), [IN_VMEM], (), 1)[0]
 
 
 def local(
@@ -436,22 +459,21 @@
 ):
     core = lax.axis_index(SHARD)
     place = jnp.stack([lax.axis_index(X), lax.axis_index(Y), lax.axis_index(Z), core, task_step[0]]).astype(jnp.int32)
-    hidden, weight = brought(place, hidden_state.transpose(1, 0, 2), recurrent_weight)
+    hidden, weight, info = brought(place, hidden_state.transpose(1, 0, 2), recurrent_weight)
     line = recurrent_line(weight)
-    hids = [hop(hidden, k, True) for k in range(4)]
+    hids = states_along_z(hidden)
     wg, wu, wd = gate_weight[0], up_weight[0], down_weight[0]
     own, p, q, act_t, x_t, param_sq = forward(tokens[0], wg, wu, wd)
     recv = swapped(own)
-    mine = recurrent(hidden, hids, line, place)
+    mine = recurrent(hidden, hids, line, info)
     gg, gu, gd, sums = backward(own, recv, targets[0], wd, p, q, act_t, x_t, param_sq)
     up_g, up_u, up_d, new_hidden, new_cell, send, keep = update(
-        place, mine, swapped(mine), sums, swapped(sums), input_weight, lstm_bias[None], cell_state.transpose(1, 0, 2),
+        info, mine, swapped(mine), sums, swapped(sums), input_weight, lstm_bias[None], cell_state.transpose(1, 0, 2),
         context_weight.T, mlp_weight, wg, wu, wd, gg, gu, gd, meta_tokens[0],
     )
     count = lax.axis_size(TASK)
-    part = loss_part(place, keep, swapped(send), meta_targets[0], count)
-    part = part + swapped(part)
-    everyone = lax.all_to_all(part.reshape(count), TASK, 0, 0, tiled=True)
+    part = loss_part(info, keep, swapped(send), meta_targets[0], count)
+    everyone = lax.all_to_all(spread(part, count), TASK, 0, 0, tiled=True)
     meta_loss = jnp.sum(everyone)
     return (
         up_g[None], up_u[None], up_d[None], new_hidden.transpose(1, 0, 2), new_cell.transpose(1, 0, 2), meta_loss

time: 118 us -> 122 us (1.034)
  starting transfers between devices: 43.6 us -> 49.4 us
    all_to_all x1, starting transfers between devices: 8.95 us -> 13 us  [local(): everyone = lax.all_to_all(spread(part, count), TASK, 0, 0, tiled=True)]
    ppermute x8, waiting for transfers between devices: 11.9 us -> 10.2 us  [hop(): return lax.ppermute(array, (Z, SHARD), pairs)]
    ppermute x0 -> x1, starting transfers between devices: none -> 1.28 us  [states_along_z(): across = lax.ppermute(held[2], SHARD, [(0, 1)])]
    pallas_call x8 -> x9, Pallas kernels: 31.8 us -> 30.6 us  [call(): pl.pallas_call(body, in_specs=specs, out_specs=out_specs, out_shape=outs,...]
  transfers between devices with their start and end apart: 20 -> 21, of which waited for: 11 -> 13; matrix products, arithmetic and copies ran while one was open for 1% -> 1% of each run, Pallas kernels for 10% -> 9%
where the time goes in v3:
time: 122 us; the launch traced here: 120 us
  starting transfers between devices  49.4 us (40%)
  Pallas kernels  30.6 us (25%)
  waiting for transfers between devices  28.1 us (23%)
  local copies, waits for them, and re-layouts  9.95 us (8%)
  between operations  1.59 us (1%)
    pallas_call x9, Pallas kernels, call(): pl.pallas_call(body, in_specs=specs, out_specs=out_specs, out_shape=outs,...  30.6 us
    ppermute x8, starting transfers between devices, hop(): return lax.ppermute(array, (Z, SHARD), pairs)  21.4 us
    all_to_all x1, starting transfers between devices, local(): everyone = lax.all_to_all(spread(part, count), TASK, 0, 0, tiled=True)  13 us
    ppermute x6, starting transfers between devices, shifted(): lax.ppermute(array, axis, [((i + shift) % size, i) for i in range(size)])  12.3 us
    ppermute x8, waiting for transfers between devices, hop(): return lax.ppermute(array, (Z, SHARD), pairs)  10.2 us
    all_to_all x1, waiting for transfers between devices, local(): everyone = lax.all_to_all(spread(part, count), TASK, 0, 0, tiled=True)  9.98 us
    unnamed x44, local copies, waits for them, and re-layouts  9.87 us
    ppermute x5, waiting for transfers between devices, swapped(): return lax.ppermute(array, SHARD, [(0, 1), (1, 0)])  3.95 us
  transfers between devices with their start and end apart: 21, of which 13 were waited for; matrix products, arithmetic and copies ran while one was open for 1% of the time, Pallas kernels for 9%

profile of v3, /device:TPU:32, one launch (start us, length us, event | category | flops | bytes accessed | tf_op | source)
XLA Modules:
  0.0 120.5 jit_solution(13790085662294148669)
XLA Ops:
  0.6 1.4 %copy-done = bf16[1,1024,768]{2,1,0:T(8,128)(2,1)S(1)} copy-done((bf16[1,1024,768]{2,1,0:T(8,128)(2,1)S(1)}, bf16[1,1024,768]{2,1,0:T(8,128)(2,1)}, u32[]{:S(2)}) %copy-start) | copy-done | bytes 1572888
  2.0 1.4 %copy-done.2 = bf16[1,1024,768]{2,1,0:T(8,128)(2,1)S(1)} copy-done((bf16[1,1024,768]{2,1,0:T(8,128)(2,1)S(1)}, bf16[1,1024,768]{2,1,0:T(8,128)(2,1)}, u32[]{:S(2)}) %copy-start.2) | copy-done | bytes 1572888
  3.5 1.4 %copy-done.4 = bf16[1,768,1024]{2,1,0:T(8,128)(2,1)S(1)} copy-done((bf16[1,768,1024]{2,1,0:T(8,128)(2,1)S(1)}, bf16[1,768,1024]{2,1,0:T(8,128)(2,1)}, u32[]{:S(2)}) %copy-start.4) | copy-done | bytes 1572888
  4.9 1.2 %copy-done.13 = bf16[1,512,1024]{2,1,0:T(8,128)(2,1)S(1)} copy-done((bf16[1,512,1024]{2,1,0:T(8,128)(2,1)S(1)}, bf16[1,512,1024]{2,1,0:T(8,128)(2,1)}, u32[]{:S(2)}) %copy-start.13) | copy-done | bytes 1048600
  6.1 4.4 %shard_map.194 = (f32[512,1024]{1,0:T(8,128)S(1)}, f32[512,768]{1,0:T(8,128)S(1)}, f32[512,768]{1,0:T(8,128)S(1)}, bf16[768,512]{1,0:T(8,128)(2,1)S(1)}, bf16[10...) custom-call(bf16[512,1024]{1,0:T(8,128)(2,1)S(1)} %bitcast.34, bf16[1024,768]{1,0:T(8,128)(2,1)S(1)} %bitcast.22, ...), custom_call_target="tpu_custom_call" | custom-call | flops 2415919104 | tf_op jit(solution)/shard_map/pallas_call | solution.py:56
  11.6 1.1 copy-done.17
  14.4 1.6 %shard_map.190 = (f32[3,1,512]{2,1,0:T(1,128)S(1)}, f32[4,2048]{1,0:T(4,128)S(1)}, s32[8,128]{1,0:T(8,128)S(1)}) custom-call(s32[5]{0:T(128)S(1)} %stack.19.place_ref, f32[3,1,512]{2,1,0:T(1,128)} %bitcast.39, f32[4,2048]{1,0:T(4,128)} %weight_hbm.1), custom_call_target="tpu_custom_call" | custom-call | flops 99999997952 | tf_op jit(solution)/shard_map/pallas_call | solution.py:56
  16.0 2.8 %collective-permute-start.5 = (f32[4,2048]{1,0:T(4,128)S(1)}, f32[4,2048]{1,0:T(4,128)S(1)}, u32[]{:S(2)}, u32[]{:S(2)}) collective-permute-start(f32[4,2048]{1,0:T(4,128)S(1)} %get-tuple-element.32.r0), channel_id=1, source_target_pairs={{64,0},{128,64},{192,128},{0,192},{65,1},{129,65},{193,129},{1,193... | collective-permute-start | bytes 98312 | tf_op jit(solution)/shard_map/ppermute | solution.py:180
  18.9 1.6 %collective-permute-done.5.r1 = f32[4,2048]{1,0:T(4,128)S(1)} collective-permute-done((f32[4,2048]{1,0:T(4,128)S(1)}, f32[4,2048]{1,0:T(4,128)S(1)}, u32[]{:S(2)}, u32[]{:S(2)}) %collective-permute-start.5) | collective-permute-done | bytes 32800 | tf_op jit(solution)/shard_map/ppermute | solution.py:180
  20.5 3.5 %collective-permute-start.6 = (f32[4,2048]{1,0:T(4,128)S(1)}, f32[4,2048]{1,0:T(4,128)S(1)}, u32[]{:S(2)}, u32[]{:S(2)}) collective-permute-start(f32[4,2048]{1,0:T(4,128)S(1)} %collective-permute-done.5.r1), channel_id=1, source_target_pairs={{64,0},{128,64},{192,128},{0,192},{65,1},{129,65},{193,129},{1,193... | collective-permute-start | bytes 98312 | tf_op jit(solution)/shard_map/ppermute | solution.py:180
  24.0 1.6 %collective-permute-done.6.r2 = f32[4,2048]{1,0:T(4,128)S(1)} collective-permute-done((f32[4,2048]{1,0:T(4,128)S(1)}, f32[4,2048]{1,0:T(4,128)S(1)}, u32[]{:S(2)}, u32[]{:S(2)}) %collective-permute-start.6) | collective-permute-done | bytes 32800 | tf_op jit(solution)/shard_map/ppermute | solution.py:180
  25.6 1.7 %collective-permute-start.10 = (f32[16,2048]{1,0:T(8,128)S(1)}, f32[16,2048]{1,0:T(8,128)S(1)}, u32[]{:S(2)}, u32[]{:S(2)}) collective-permute-start(f32[16,2048]{1,0:T(8,128)S(1)} %shard_map.191.r0), channel_id=1, source_target_pairs={{48,0},{0,16},{16,32},{32,48},{49,1},{1,17},{17,33},{33,49},{50,2}... | collective-permute-start | bytes 393224 | tf_op jit(solution)/shard_map/ppermute | solution.py:180
  27.3 2.9 %collective-permute-start.9 = (f32[16,2048]{1,0:T(8,128)S(1)}, f32[16,2048]{1,0:T(8,128)S(1)}, u32[]{:S(2)}, u32[]{:S(2)}) collective-permute-start(f32[16,2048]{1,0:T(8,128)S(1)} %shard_map.191.r0), channel_id=1, source_target_pairs={{32,0},{48,16},{0,32},{16,48},{33,1},{49,17},{1,33},{17,49},{34,2}... | collective-permute-start | bytes 393224 | tf_op jit(solution)/shard_map/ppermute | solution.py:180
  30.2 1.3 %collective-permute-start.8 = (f32[16,2048]{1,0:T(8,128)S(1)}, f32[16,2048]{1,0:T(8,128)S(1)}, u32[]{:S(2)}, u32[]{:S(2)}) collective-permute-start(f32[16,2048]{1,0:T(8,128)S(1)} %shard_map.191.r0), channel_id=1, source_target_pairs={{16,0},{32,16},{48,32},{0,48},{17,1},{33,17},{49,33},{1,49},{18,2}... | collective-permute-start | bytes 393224 | tf_op jit(solution)/shard_map/ppermute | solution.py:180
  31.6 3.5 %collective-permute-done.h1 = f32[3,1,512]{2,1,0:T(1,128)S(1)} collective-permute-done((f32[3,1,512]{2,1,0:T(1,128)S(1)}, f32[3,1,512]{2,1,0:T(1,128)S(1)}, u32[]{:S(2)}, u32[]{:S(2)}) %collective-permute-start) | collective-permute-done | bytes 6176 | tf_op jit(solution)/shard_map/ppermute | solution.py:196
  35.2 3.7 %collective-permute-start.1 = (f32[3,1,512]{2,1,0:T(1,128)S(1)}, f32[3,1,512]{2,1,0:T(1,128)S(1)}, u32[]{:S(2)}, u32[]{:S(2)}) collective-permute-start(f32[3,1,512]{2,1,0:T(1,128)S(1)} %collective-permute-done.h1), channel_id=1, source_target_pairs={{0,14},{2,0},{4,2},{6,4},{8,6},{10,8},{12,10},{14,12},{1,3},{3,5},... | collective-permute-start | bytes 18440 | tf_op jit(solution)/shard_map/ppermute | solution.py:196
  38.8 1.3 %collective-permute-done.1.h2 = f32[3,1,512]{2,1,0:T(1,128)S(1)} collective-permute-done((f32[3,1,512]{2,1,0:T(1,128)S(1)}, f32[3,1,512]{2,1,0:T(1,128)S(1)}, u32[]{:S(2)}, u32[]{:S(2)}) %collective-permute-start.1) | collective-permute-done | bytes 6176 | tf_op jit(solution)/shard_map/ppermute | solution.py:196
  40.2 1.3 %collective-permute-start.4 = (f32[3,1,512]{2,1,0:T(1,128)S(1)}, f32[3,1,512]{2,1,0:T(1,128)S(1)}, u32[]{:S(2)}, u32[]{:S(2)}) collective-permute-start(f32[3,1,512]{2,1,0:T(1,128)S(1)} %collective-permute-done.1.h2), channel_id=1, source_target_pairs={{0,1},{2,3},{4,5},{6,7},{8,9},{10,11},{12,13},{14,15},{16,17},{18,... | collective-permute-start | bytes 18440 | tf_op jit(solution)/shard_map/ppermute | solution.py:203
  42.3 3.5 %collective-permute-start.2 = (f32[3,1,512]{2,1,0:T(1,128)S(1)}, f32[3,1,512]{2,1,0:T(1,128)S(1)}, u32[]{:S(2)}, u32[]{:S(2)}) collective-permute-start(f32[3,1,512]{2,1,0:T(1,128)S(1)} %collective-permute-done.1.h2), channel_id=1, source_target_pairs={{0,14},{2,0},{4,2},{6,4},{8,6},{10,8},{12,10},{14,12},{1,3},{3,5},... | collective-permute-start | bytes 18440 | tf_op jit(solution)/shard_map/ppermute | solution.py:196
  45.8 1.3 %collective-permute-done.2.h3 = f32[3,1,512]{2,1,0:T(1,128)S(1)} collective-permute-done((f32[3,1,512]{2,1,0:T(1,128)S(1)}, f32[3,1,512]{2,1,0:T(1,128)S(1)}, u32[]{:S(2)}, u32[]{:S(2)}) %collective-permute-start.2) | collective-permute-done | bytes 6176 | tf_op jit(solution)/shard_map/ppermute | solution.py:196
  47.1 5.4 %collective-permute-start.3 = (f32[3,1,512]{2,1,0:T(1,128)S(1)}, f32[3,1,512]{2,1,0:T(1,128)S(1)}, u32[]{:S(2)}, u32[]{:S(2)}) collective-permute-start(f32[3,1,512]{2,1,0:T(1,128)S(1)} %collective-permute-done.2.h3), channel_id=1, source_target_pairs={{0,14},{2,0},{4,2},{6,4},{8,6},{10,8},{12,10},{14,12},{16,30},{18,... | collective-permute-start | bytes 18440 | tf_op jit(solution)/shard_map/ppermute | solution.py:196
  52.5 1.3 %collective-permute-done.3.h4 = f32[3,1,512]{2,1,0:T(1,128)S(1)} collective-permute-done((f32[3,1,512]{2,1,0:T(1,128)S(1)}, f32[3,1,512]{2,1,0:T(1,128)S(1)}, u32[]{:S(2)}, u32[]{:S(2)}) %collective-permute-start.3) | collective-permute-done | bytes 6176 | tf_op jit(solution)/shard_map/ppermute | solution.py:196
  53.9 1.3 %shard_map.192 = (f32[3,2048]{1,0:T(4,128)S(1)}, f32[3,2048]{1,0:T(4,128)S(1)}, f32[3,2048]{1,0:T(4,128)S(1)}, f32[3,2048]{1,0:T(4,128)S(1)}) custom-call(s32[8,128]{1,0:T(8,128)S(1)} %get-tuple-element.30.info_ref, f32[3,1,512]{2,1,0:T(1,128)S(1)} %get-tuple-element.31.own, f32[3,1,512]{2,1,0:T(1,128)S(1)} %collective-permute-done.h1, ...), custom_call_target="tpu_custom_call" | custom-call | flops 4194304 | tf_op jit(solution)/shard_map/pallas_call | solution.py:56
  55.2 1.7 %collective-permute-start.12 = (f32[3,2048]{1,0:T(4,128)S(1)}, f32[3,2048]{1,0:T(4,128)S(1)}, u32[]{:S(2)}, u32[]{:S(2)}) collective-permute-start(f32[3,2048]{1,0:T(4,128)S(1)} %get-tuple-element.34), channel_id=1, source_target_pairs={{0,2},{2,4},{4,6},{6,8},{8,10},{10,12},{12,14},{14,0},{1,5},{3,7},... | collective-permute-start | bytes 73736 | tf_op jit(solution)/shard_map/ppermute | solution.py:196
  56.9 1.9 %collective-permute-start.13 = (f32[3,2048]{1,0:T(4,128)S(1)}, f32[3,2048]{1,0:T(4,128)S(1)}, u32[]{:S(2)}, u32[]{:S(2)}) collective-permute-start(f32[3,2048]{1,0:T(4,128)S(1)} %get-tuple-element.35), channel_id=1, source_target_pairs={{0,6},{2,8},{4,10},{6,12},{8,14},{10,0},{12,2},{14,4},{1,13},{3,15... | collective-permute-start | bytes 73736 | tf_op jit(solution)/shard_map/ppermute | solution.py:196
  58.8 4.5 %collective-permute-start.14 = (f32[3,2048]{1,0:T(4,128)S(1)}, f32[3,2048]{1,0:T(4,128)S(1)}, u32[]{:S(2)}, u32[]{:S(2)}) collective-permute-start(f32[3,2048]{1,0:T(4,128)S(1)} %get-tuple-element.36), channel_id=1, source_target_pairs={{0,8},{2,10},{4,12},{6,14},{8,0},{10,2},{12,4},{14,6},{1,11},{3,13... | collective-permute-start | bytes 73736 | tf_op jit(solution)/shard_map/ppermute | solution.py:196
  64.0 1.8 %collective-permute-done.13.m2 = f32[3,2048]{1,0:T(4,128)S(1)} collective-permute-done((f32[3,2048]{1,0:T(4,128)S(1)}, f32[3,2048]{1,0:T(4,128)S(1)}, u32[]{:S(2)}, u32[]{:S(2)}) %collective-permute-start.13) | collective-permute-done | bytes 24608 | tf_op jit(solution)/shard_map/ppermute | solution.py:196
  66.9 7.9 %shard_map.195 = (f32[1024,768]{1,0:T(8,128)S(1)}, f32[1024,768]{1,0:T(8,128)S(1)}, f32[768,1024]{1,0:T(8,128)S(1)}, f32[16,128]{1,0:T(8,128)S(1)}) custom-call(f32[512,1024]{1,0:T(8,128)S(1)} %get-tuple-element.37.own_ref, f32[512,1024]{1,0:T(8,128)} %collective-permute-done.16.recv_ref, bf16[512,1024]{1,0:T(8,128)(2,1)S(1)} %bitcast.35, ...), custom_call_target="tpu_custom_call" | custom-call | flops 3221225472 | tf_op jit(solution)/shard_map/pallas_call | solution.py:56
  76.3 14.1 %shard_map.196 = (bf16[1024,768]{1,0:T(8,128)(2,1)}, bf16[1024,768]{1,0:T(8,128)(2,1)}, bf16[768,1024]{1,0:T(8,128)(2,1)}, f32[3,1,512]{2,1,0:T(1,128)S(1)}, f32...) custom-call(s32[8,128]{1,0:T(8,128)S(1)} %get-tuple-element.30.info_ref, ...), custom_call_target="tpu_custom_call" | custom-call | flops 2415919104 | tf_op jit(solution)/shard_map/pallas_call | solution.py:56
  90.8 2.3 %collective-permute-done.18.recv_ref = f32[256,1024]{1,0:T(8,128)S(1)} collective-permute-done((f32[256,1024]{1,0:T(8,128)S(1)}, f32[256,1024]{1,0:T(8,128)S(1)}, u32[]{:S(2)}, u32[]{:S(2)}) %collective-permute-start.18) | collective-permute-done | bytes 1048608 | tf_op jit(solution)/shard_map/ppermute | solution.py:184
  95.6 13.0 %all-to-all-start = ((f32[128,1,1]{2,1,0:T(1,128)}), f32[128,1,1]{2,1,0:T(1,128)S(1)}, u32[]{:S(2)}, u32[]{:S(2)}) async-start(f32[128,1,1]{2,1,0:T(1,128)} %shard_map.198), calls=%async_computation | async-start | bytes 131072 | tf_op jit(solution)/shard_map/all_to_all | solution.py:476
  109.7 10.0 %all-to-all-done = f32[128,1,1]{2,1,0:T(1,128)S(1)} async-done(((f32[128,1,1]{2,1,0:T(1,128)}), f32[128,1,1]{2,1,0:T(1,128)S(1)}, u32[]{:S(2)}, u32[]{:S(2)}) %all-to-all-start) | async-done | bytes 544 | tf_op jit(solution)/shard_map/all_to_all | solution.py:476
  (65 shorter events, 11.0 us)
Async XLA Ops:
  13.7 53.1 %collective-permute-start.16 = (f32[512,1024]{1,0:T(8,128)S(1)}, f32[512,1024]{1,0:T(8,128)}, u32[]{:S(2)}, u32[]{:S(2)}) collective-permute-start(f32[512,1024]{1,0:T(8,128)S(1)} %get-tuple-element.37.own_ref), channel_id=1, source_target_pairs={{0,1},{1,0},{2,3},{3,2},{4,5},{5,4},{6,7},{7,6},{8,9},{9,8},{10,11... | collective-permute-start | bytes 6291464 | tf_op jit(solution)/shard_map/ppermute | solution.py:184
  14.4 52.4 %copy-start.5 = (bf16[1,768,1024]{2,1,0:T(8,128)(2,1)S(1)}, bf16[1,768,1024]{2,1,0:T(8,128)(2,1)}, u32[]{:S(2)}) copy-start(bf16[1,768,1024]{2,1,0:T(8,128)(2,1)} %param.21) | copy-start | bytes 4718596
  14.4 52.4 %copy-start.14 = (bf16[1,512,1024]{2,1,0:T(8,128)(2,1)S(1)}, bf16[1,512,1024]{2,1,0:T(8,128)(2,1)}, u32[]{:S(2)}) copy-start(bf16[1,512,1024]{2,1,0:T(8,128)(2,1)} %param.16) | copy-start | bytes 3145732
  14.4 52.4 %copy-start.16 = (f32[512,768]{1,0:T(8,128)S(1)}, f32[512,768]{1,0:T(8,128)}, u32[]{:S(2)}) copy-start(f32[512,768]{1,0:T(8,128)} %copy-done.15) | copy-start | bytes 4718596
  14.4 52.4 %copy-start.18 = (f32[512,768]{1,0:T(8,128)S(1)}, f32[512,768]{1,0:T(8,128)}, u32[]{:S(2)}) copy-start(f32[512,768]{1,0:T(8,128)} %copy-done.17) | copy-start | bytes 4718596
  14.4 52.4 %copy-start.20 = (bf16[768,512]{1,0:T(8,128)(2,1)S(1)}, bf16[768,512]{1,0:T(8,128)(2,1)}, u32[]{:S(2)}) copy-start(bf16[768,512]{1,0:T(8,128)(2,1)} %copy-done.19) | copy-start | bytes 2359300
  16.0 4.4 %collective-permute-start.5 = (f32[4,2048]{1,0:T(4,128)S(1)}, f32[4,2048]{1,0:T(4,128)S(1)}, u32[]{:S(2)}, u32[]{:S(2)}) collective-permute-start(f32[4,2048]{1,0:T(4,128)S(1)} %get-tuple-element.32.r0), channel_id=1, source_target_pairs={{64,0},{128,64},{192,128},{0,192},{65,1},{129,65},{193,129},{1,193... | collective-permute-start | bytes 98312 | tf_op jit(solution)/shard_map/ppermute | solution.py:180
  18.9 5.1 %collective-permute-start.7 = (f32[4,2048]{1,0:T(4,128)S(1)}, f32[4,2048]{1,0:T(4,128)S(1)}, u32[]{:S(2)}, u32[]{:S(2)}) collective-permute-start(f32[4,2048]{1,0:T(4,128)S(1)} %get-tuple-element.32.r0), channel_id=1, source_target_pairs={{192,0},{0,64},{64,128},{128,192},{193,1},{1,65},{65,129},{129,193... | collective-permute-start | bytes 98312 | tf_op jit(solution)/shard_map/ppermute | solution.py:180
  20.5 5.1 %collective-permute-start.6 = (f32[4,2048]{1,0:T(4,128)S(1)}, f32[4,2048]{1,0:T(4,128)S(1)}, u32[]{:S(2)}, u32[]{:S(2)}) collective-permute-start(f32[4,2048]{1,0:T(4,128)S(1)} %collective-permute-done.5.r1), channel_id=1, source_target_pairs={{64,0},{128,64},{192,128},{0,192},{65,1},{129,65},{193,129},{1,193... | collective-permute-start | bytes 98312 | tf_op jit(solution)/shard_map/ppermute | solution.py:180
  25.6 28.2 %collective-permute-start.10 = (f32[16,2048]{1,0:T(8,128)S(1)}, f32[16,2048]{1,0:T(8,128)S(1)}, u32[]{:S(2)}, u32[]{:S(2)}) collective-permute-start(f32[16,2048]{1,0:T(8,128)S(1)} %shard_map.191.r0), channel_id=1, source_target_pairs={{48,0},{0,16},{16,32},{32,48},{49,1},{1,17},{17,33},{33,49},{50,2}... | collective-permute-start | bytes 393224 | tf_op jit(solution)/shard_map/ppermute | solution.py:180
  27.3 26.6 %collective-permute-start.9 = (f32[16,2048]{1,0:T(8,128)S(1)}, f32[16,2048]{1,0:T(8,128)S(1)}, u32[]{:S(2)}, u32[]{:S(2)}) collective-permute-start(f32[16,2048]{1,0:T(8,128)S(1)} %shard_map.191.r0), channel_id=1, source_target_pairs={{32,0},{48,16},{0,32},{16,48},{33,1},{49,17},{1,33},{17,49},{34,2}... | collective-permute-start | bytes 393224 | tf_op jit(solution)/shard_map/ppermute | solution.py:180
  30.2 23.7 %collective-permute-start.8 = (f32[16,2048]{1,0:T(8,128)S(1)}, f32[16,2048]{1,0:T(8,128)S(1)}, u32[]{:S(2)}, u32[]{:S(2)}) collective-permute-start(f32[16,2048]{1,0:T(8,128)S(1)} %shard_map.191.r0), channel_id=1, source_target_pairs={{16,0},{32,16},{48,32},{0,48},{17,1},{33,17},{49,33},{1,49},{18,2}... | collective-permute-start | bytes 393224 | tf_op jit(solution)/shard_map/ppermute | solution.py:180
  31.5 3.6 %collective-permute-start = (f32[3,1,512]{2,1,0:T(1,128)S(1)}, f32[3,1,512]{2,1,0:T(1,128)S(1)}, u32[]{:S(2)}, u32[]{:S(2)}) collective-permute-start(f32[3,1,512]{2,1,0:T(1,128)S(1)} %get-tuple-element.31.own), channel_id=1, source_target_pairs={{0,14},{2,0},{4,2},{6,4},{8,6},{10,8},{12,10},{14,12},{1,3},{3,5},... | collective-permute-start | bytes 18440 | tf_op jit(solution)/shard_map/ppermute | solution.py:196
  35.2 5.0 %collective-permute-start.1 = (f32[3,1,512]{2,1,0:T(1,128)S(1)}, f32[3,1,512]{2,1,0:T(1,128)S(1)}, u32[]{:S(2)}, u32[]{:S(2)}) collective-permute-start(f32[3,1,512]{2,1,0:T(1,128)S(1)} %collective-permute-done.h1), channel_id=1, source_target_pairs={{0,14},{2,0},{4,2},{6,4},{8,6},{10,8},{12,10},{14,12},{1,3},{3,5},... | collective-permute-start | bytes 18440 | tf_op jit(solution)/shard_map/ppermute | solution.py:196
  40.2 2.1 %collective-permute-start.4 = (f32[3,1,512]{2,1,0:T(1,128)S(1)}, f32[3,1,512]{2,1,0:T(1,128)S(1)}, u32[]{:S(2)}, u32[]{:S(2)}) collective-permute-start(f32[3,1,512]{2,1,0:T(1,128)S(1)} %collective-permute-done.1.h2), channel_id=1, source_target_pairs={{0,1},{2,3},{4,5},{6,7},{8,9},{10,11},{12,13},{14,15},{16,17},{18,... | collective-permute-start | bytes 18440 | tf_op jit(solution)/shard_map/ppermute | solution.py:203
  42.3 4.8 %collective-permute-start.2 = (f32[3,1,512]{2,1,0:T(1,128)S(1)}, f32[3,1,512]{2,1,0:T(1,128)S(1)}, u32[]{:S(2)}, u32[]{:S(2)}) collective-permute-start(f32[3,1,512]{2,1,0:T(1,128)S(1)} %collective-permute-done.1.h2), channel_id=1, source_target_pairs={{0,14},{2,0},{4,2},{6,4},{8,6},{10,8},{12,10},{14,12},{1,3},{3,5},... | collective-permute-start | bytes 18440 | tf_op jit(solution)/shard_map/ppermute | solution.py:196
  47.1 6.7 %collective-permute-start.3 = (f32[3,1,512]{2,1,0:T(1,128)S(1)}, f32[3,1,512]{2,1,0:T(1,128)S(1)}, u32[]{:S(2)}, u32[]{:S(2)}) collective-permute-start(f32[3,1,512]{2,1,0:T(1,128)S(1)} %collective-permute-done.2.h3), channel_id=1, source_target_pairs={{0,14},{2,0},{4,2},{6,4},{8,6},{10,8},{12,10},{14,12},{16,30},{18,... | collective-permute-start | bytes 18440 | tf_op jit(solution)/shard_map/ppermute | solution.py:196
  55.2 8.8 %collective-permute-start.12 = (f32[3,2048]{1,0:T(4,128)S(1)}, f32[3,2048]{1,0:T(4,128)S(1)}, u32[]{:S(2)}, u32[]{:S(2)}) collective-permute-start(f32[3,2048]{1,0:T(4,128)S(1)} %get-tuple-element.34), channel_id=1, source_target_pairs={{0,2},{2,4},{4,6},{6,8},{8,10},{10,12},{12,14},{14,0},{1,5},{3,7},... | collective-permute-start | bytes 73736 | tf_op jit(solution)/shard_map/ppermute | solution.py:196
  56.9 8.8 %collective-permute-start.13 = (f32[3,2048]{1,0:T(4,128)S(1)}, f32[3,2048]{1,0:T(4,128)S(1)}, u32[]{:S(2)}, u32[]{:S(2)}) collective-permute-start(f32[3,2048]{1,0:T(4,128)S(1)} %get-tuple-element.35), channel_id=1, source_target_pairs={{0,6},{2,8},{4,10},{6,12},{8,14},{10,0},{12,2},{14,4},{1,13},{3,15... | collective-permute-start | bytes 73736 | tf_op jit(solution)/shard_map/ppermute | solution.py:196
  58.8 7.8 %collective-permute-start.14 = (f32[3,2048]{1,0:T(4,128)S(1)}, f32[3,2048]{1,0:T(4,128)S(1)}, u32[]{:S(2)}, u32[]{:S(2)}) collective-permute-start(f32[3,2048]{1,0:T(4,128)S(1)} %get-tuple-element.36), channel_id=1, source_target_pairs={{0,8},{2,10},{4,12},{6,14},{8,0},{10,2},{12,4},{14,6},{1,11},{3,13... | collective-permute-start | bytes 73736 | tf_op jit(solution)/shard_map/ppermute | solution.py:196
  63.3 3.3 %collective-permute-start.11 = (f32[3,2048]{1,0:T(4,128)S(1)}, f32[3,2048]{1,0:T(4,128)S(1)}, u32[]{:S(2)}, u32[]{:S(2)}) collective-permute-start(f32[3,2048]{1,0:T(4,128)S(1)} %get-tuple-element.33.own), channel_id=1, source_target_pairs={{1,15},{3,1},{5,3},{7,5},{9,7},{11,9},{13,11},{15,13},{17,31},{19,... | collective-permute-start | bytes 73736 | tf_op jit(solution)/shard_map/ppermute | solution.py:196
  66.7 8.7 %collective-permute-start.15 = (f32[3,2048]{1,0:T(4,128)S(1)}, f32[3,2048]{1,0:T(4,128)S(1)}, u32[]{:S(2)}, u32[]{:S(2)}) collective-permute-start(f32[3,2048]{1,0:T(4,128)S(1)} %shard_map.193.mine_ref), channel_id=1, source_target_pairs={{0,1},{1,0},{2,3},{3,2},{4,5},{5,4},{6,7},{7,6},{8,9},{9,8},{10,11... | collective-permute-start | bytes 73736 | tf_op jit(solution)/shard_map/ppermute | solution.py:184
  66.8 9.4 %copy-start.1 = (bf16[1,1024,768]{2,1,0:T(8,128)(2,1)S(1)}, bf16[1,1024,768]{2,1,0:T(8,128)(2,1)}, u32[]{:S(2)}) copy-start(bf16[1,1024,768]{2,1,0:T(8,128)(2,1)} %param.19) | copy-start | bytes 4718596
  66.8 9.4 %copy-start.3 = (bf16[1,1024,768]{2,1,0:T(8,128)(2,1)S(1)}, bf16[1,1024,768]{2,1,0:T(8,128)(2,1)}, u32[]{:S(2)}) copy-start(bf16[1,1024,768]{2,1,0:T(8,128)(2,1)} %param.20) | copy-start | bytes 4718596
  66.9 9.4 %copy-start.6 = (bf16[1,512,1024]{2,1,0:T(8,128)(2,1)S(1)}, bf16[1,512,1024]{2,1,0:T(8,128)(2,1)}, u32[]{:S(2)}) copy-start(bf16[1,512,1024]{2,1,0:T(8,128)(2,1)} %param.17) | copy-start | bytes 3145732
  66.9 9.4 %copy-start.8 = (f32[3,2048]{1,0:T(4,128)S(1)}, f32[3,2048]{1,0:T(4,128)}, u32[]{:S(2)}) copy-start(f32[3,2048]{1,0:T(4,128)} %in_w_ref.1) | copy-start | bytes 73732
  66.9 9.3 %copy-start.9 = (f32[512,5]{0,1:T(8,128)S(1)}, f32[512,5]{0,1:T(8,128)}, u32[]{:S(2)}) copy-start(f32[512,5]{0,1:T(8,128)} %param.28) | copy-start | bytes 30724
  74.8 1.4 %collective-permute-start.17 = (f32[16,128]{1,0:T(8,128)S(1)}, f32[16,128]{1,0:T(8,128)S(1)}, u32[]{:S(2)}, u32[]{:S(2)}) collective-permute-start(f32[16,128]{1,0:T(8,128)S(1)} %get-tuple-element.43.sq_ref), channel_id=1, source_target_pairs={{0,1},{1,0},{2,3},{3,2},{4,5},{5,4},{6,7},{7,6},{8,9},{9,8},{10,11... | collective-permute-start | bytes 24584 | tf_op jit(solution)/shard_map/ppermute | solution.py:184
  76.3 16.9 %copy-start.7 = (bf16[1,512,1024]{2,1,0:T(8,128)(2,1)S(1)}, bf16[1,512,1024]{2,1,0:T(8,128)(2,1)}, u32[]{:S(2)}) copy-start(bf16[1,512,1024]{2,1,0:T(8,128)(2,1)} %param.18) | copy-start | bytes 3145732
  90.4 2.7 %collective-permute-start.18 = (f32[256,1024]{1,0:T(8,128)S(1)}, f32[256,1024]{1,0:T(8,128)S(1)}, u32[]{:S(2)}, u32[]{:S(2)}) collective-permute-start(f32[256,1024]{1,0:T(8,128)S(1)} %get-tuple-element.53), channel_id=1, source_target_pairs={{0,1},{1,0},{2,3},{3,2},{4,5},{5,4},{6,7},{7,6},{8,9},{9,8},{10,11... | collective-permute-start | bytes 3145736 | tf_op jit(solution)/shard_map/ppermute | solution.py:184
  93.7 1.2 collective-permute-start.19
  95.6 24.2 %all-to-all-start = ((f32[128,1,1]{2,1,0:T(1,128)}), f32[128,1,1]{2,1,0:T(1,128)S(1)}, u32[]{:S(2)}, u32[]{:S(2)}) async-start(f32[128,1,1]{2,1,0:T(1,128)} %shard_map.198), calls=%async_computation | async-start | bytes 131072 | tf_op jit(solution)/shard_map/all_to_all | solution.py:476
  (10 other events, 36.6 us)

commit v4 on v3

--- a/solution.py
+++ b/solution.py
@@ -151,20 +151,21 @@
     )
 
 
-def recurrent_kernel(info_ref, own, h1, h2, h3, h4, across, r0, r1, r2, r3, o0, o1, o2, o3, stack):
+def recurrent_kernel(info_ref, h0, h1, h2, h3, r0, r1, r2, r3, o0, o1, o2, o3, stack):
     px, py, pz, core = (info_ref[k : k + 1, 0:1] for k in range(4))
-    state = own.shape[2]
+    state = h0.shape[2]
     stack[...] = jnp.zeros_like(stack)
-    for j in range(own.shape[0]):
-        stack[j : j + 1, :] = jnp.where(core == 0, own[j], h1[j])
-        stack[8 + j : 9 + j, :] = jnp.where(core == 0, h1[j], across[j])
-        stack[16 + j : 17 + j, :] = jnp.where(core == 0, h3[j], h2[j])
-        stack[24 + j : 25 + j, :] = jnp.where(core == 0, h4[j], h3[j])
+    for k, hid_ref in enumerate((h0, h1, h2, h3)):
+        for j in range(hid_ref.shape[0]):
+            stack[8 * k + j : 8 * k + j + 1, :] = hid_ref[j]
     shape = (state, 128)
     row = lax.broadcasted_iota(jnp.int32, shape, 0)
-    col = lax.broadcasted_iota(jnp.int32, shape, 1)
+    col = lax.broadcasted_iota(jnp.int32, (1, 128), 1)
     step, block, inner = col >> 4, (col >> 2) & 3, col & 3
-    pick = (((px + block) & 3) << 7) + (((py + step) & 3) << 5) + (pz << 2) + inner
+    away = jnp.zeros((1, 128), jnp.int32)
+    for k, (south, north) in enumerate(HOPS):
+        away = jnp.where(block == k, jnp.where(core == 0, south, north), away)
+    pick = (px << 7) + (((py + step) & 3) << 5) + (((pz + away) & 7) << 2) + inner
     chosen = (row == pick).astype(f32)
     hidden = jnp.dot(stack[...], chosen, precision=highest, preferred_element_type=f32)
     total = None
@@ -184,24 +185,16 @@
     return lax.ppermute(array, SHARD, [(0, 1), (1, 0)])
 
 
-HOPS = ((None, -1), (1, 2), (3, -2), (4, -3))
-
-
-def hop(array, amounts):
+HOPS = ((0, 1), (2, -1), (3, -2), (4, -3))
+
+
+def from_along_z(array, amounts):
     size = lax.axis_size(Z)
     pairs = []
     for core, by in enumerate(amounts):
-        if by is not None:
-            pairs += [(i * 2 + core, (i + by) % size * 2 + core) for i in range(size)]
+        if by != 0:
+            pairs += [((i + by) % size * 2 + core, i * 2 + core) for i in range(size)]
     return lax.ppermute(array, (Z, SHARD), pairs)
-
-
-def states_along_z(hidden):
-    held = [hidden]
-    for amounts in ((-1, 1), (-1, 1), (-1, 1), (-1, None)):
-        held.append(hop(held[-1], amounts))
-    across = lax.ppermute(held[2], SHARD, [(0, 1)])
-    return held[1:] + [across]
 
 
 def first_kernel(place_ref, hidden_hbm, weight_hbm, hidden_ref, weight_ref, info_ref, sems):
@@ -222,42 +215,37 @@
 
 def brought(place, hidden, weight):
     return call(
-        first_kernel, (place, hidden, weight), [IN_SMEM] + [IN_HBM] * 2, vmem((hidden.shape, f32), (weight.shape, f32), ((8, 128), jnp.int32)),
+        first_kernel, (place, hidden, weight), [IN_SMEM] + [IN_HBM] * 2,
+        vmem((hidden.shape, f32), (weight.shape, f32), ((8, 128), jnp.int32)),
         [IN_VMEM] * 3, [pltpu.SemaphoreType.DMA((2,))], 1, 100_000_000_000,
     )
 
 
-def line_kernel(r0, r1, r2, r3, out_ref):
-    for k, r_ref in enumerate((r0, r1, r2, r3)):
-        out_ref[4 * k : 4 * k + 4, :] = r_ref[...]
-
-
-def sum_kernel(info_ref, own, m0, m1, m2, m3, out_ref):
-    out_ref[...] = (jnp.where(info_ref[3:4, 0:1] == 0, own[...], m0[...]) + m1[...]) + (m2[...] + m3[...])
-
-
-def recurrent_line(weight):
-    above = shifted(weight, X, 1)
-    below = shifted(weight, X, 3)
-    others = (above, shifted(above, X, 1), below)
+def line_kernel(info_ref, own, r0, r1, r2, r3, out_ref):
+    out_ref[0:4, :] = jnp.where(info_ref[3:4, 0:1] == 0, own[...], r0[...])
+    for k, r_ref in enumerate((r1, r2, r3)):
+        out_ref[4 * k + 4 : 4 * k + 8, :] = r_ref[...]
+
+
+def sum_kernel(own, m1, m2, m3, out_ref):
+    out_ref[...] = (own[...] + m1[...]) + (m2[...] + m3[...])
+
+
+def recurrent_line(weight, info):
+    others = [from_along_z(weight, amounts) for amounts in HOPS]
     shape = (4 * weight.shape[0], weight.shape[1])
-    return call(line_kernel, (weight, *others), [IN_VMEM] * 4, vmem((shape, f32)), [IN_VMEM], (), 1, 1 << 16)[0]
-
-
-def recurrent(hidden, hids, line, info):
-    plane = [line]
-    for k in (1, 2, 3):
-        plane.append(shifted(line, Y, k))
-    out = (hidden.shape[0], line.shape[1])
+    return call(line_kernel, (info, weight, *others), [IN_VMEM] * 6, vmem((shape, f32)), [IN_VMEM], (), 1, 1 << 16)[0]
+
+
+def recurrent(hids, line, info):
+    plane = [line] + [shifted(line, Y, k) for k in (1, 2, 3)]
+    out = (hids[0].shape[0], line.shape[1])
     parts = call(
-        recurrent_kernel, (info, hidden, *hids, *plane), [IN_VMEM] * 11,
-        vmem(*[(out, f32)] * 4), [IN_VMEM] * 4, [pltpu.VMEM((32, hidden.shape[2]), f32)], 4, 1 << 22,
-    )
-    moved = [hop(part, HOPS[k]) for k, part in enumerate(parts)]
-    return call(
-        sum_kernel, (info, parts[0], *moved), [IN_VMEM] * 6,
-        vmem((out, f32)), [IN_VMEM], (), 1, 1 << 16,
-    )[0]
+        recurrent_kernel, (info, *hids, *plane), [IN_VMEM] * 9,
+        vmem(*[(out, f32)] * 4), [IN_VMEM] * 4, [pltpu.VMEM((32, hids[0].shape[2]), f32)], 4, 1 << 22,
+    )
+    moved = [shifted(parts[k], X, -k) for k in (1, 2, 3)]
+    return call(sum_kernel, (parts[0], *moved), [IN_VMEM] * 4, vmem((out, f32)), [IN_VMEM], (), 1, 1 << 16)[0]
 
 
 def update_kernel(
@@ -460,12 +448,12 @@
     core = lax.axis_index(SHARD)
     place = jnp.stack([lax.axis_index(X), lax.axis_index(Y), lax.axis_index(Z), core, task_step[0]]).astype(jnp.int32)
     hidden, weight, info = brought(place, hidden_state.transpose(1, 0, 2), recurrent_weight)
-    line = recurrent_line(weight)
-    hids = states_along_z(hidden)
+    line = recurrent_line(weight, info)
+    hids = [hidden] + [shifted(hidden, X, k) for k in (1, 2, 3)]
     wg, wu, wd = gate_weight[0], up_weight[0], down_weight[0]
     own, p, q, act_t, x_t, param_sq = forward(tokens[0], wg, wu, wd)
     recv = swapped(own)
-    mine = recurrent(hidden, hids, line, info)
+    mine = recurrent(hids, line, info)
     gg, gu, gd, sums = backward(own, recv, targets[0], wd, p, q, act_t, x_t, param_sq)
     up_g, up_u, up_d, new_hidden, new_cell, send, keep = update(
         info, mine, swapped(mine), sums, swapped(sums), input_weight, lstm_bias[None], cell_state.transpose(1, 0, 2),

time: 122 us -> 109 us (0.89)
  starting transfers between devices: 49.4 us -> 33.8 us
  waiting for transfers between devices: 28.1 us -> 31.2 us
    ppermute x9 -> x4, starting transfers between devices: 22.7 us -> 8.48 us  [from_along_z(): return lax.ppermute(array, (Z, SHARD), pairs)]
    ppermute x6 -> x9, waiting for transfers between devices: 3.2 us -> 12.5 us  [shifted(): lax.ppermute(array, axis, [((i + shift) % size, i) for i in range(size)])]
    ppermute x9 -> x4, waiting for transfers between devices: 11 us -> 4.8 us  [from_along_z(): return lax.ppermute(array, (Z, SHARD), pairs)]
    all_to_all x1, starting transfers between devices: 13 us -> 8.48 us  [local(): everyone = lax.all_to_all(spread(part, count), TASK, 0, 0, tiled=True)]
    ppermute x6 -> x9, starting transfers between devices: 12.3 us -> 15.2 us  [shifted(): lax.ppermute(array, axis, [((i + shift) % size, i) for i in range(size)])]
  transfers between devices with their start and end apart: 21 -> 19, of which waited for: 13 -> 11; matrix products, arithmetic and copies ran while one was open for 1% -> 1% of each run, Pallas kernels for 9% -> 10%
where the time goes in v4:
time: 109 us; the launch traced here: 108 us
  starting transfers between devices  33.8 us (31%)
  waiting for transfers between devices  31.2 us (29%)
  Pallas kernels  30.6 us (28%)
  local copies, waits for them, and re-layouts  9.95 us (9%)
  between operations  1.57 us (1%)
    pallas_call x9, Pallas kernels, call(): pl.pallas_call(body, in_specs=specs, out_specs=out_specs, out_shape=outs,...  30.6 us
    ppermute x9, starting transfers between devices, shifted(): lax.ppermute(array, axis, [((i + shift) % size, i) for i in range(size)])  15.2 us
    ppermute x9, waiting for transfers between devices, shifted(): lax.ppermute(array, axis, [((i + shift) % size, i) for i in range(size)])  12.5 us
    all_to_all x1, waiting for transfers between devices, local(): everyone = lax.all_to_all(spread(part, count), TASK, 0, 0, tiled=True)  9.99 us
    unnamed x44, local copies, waits for them, and re-layouts  9.87 us
    all_to_all x1, starting transfers between devices, local(): everyone = lax.all_to_all(spread(part, count), TASK, 0, 0, tiled=True)  8.48 us
    ppermute x4, starting transfers between devices, from_along_z(): return lax.ppermute(array, (Z, SHARD), pairs)  8.48 us
    ppermute x4, waiting for transfers between devices, from_along_z(): return lax.ppermute(array, (Z, SHARD), pairs)  4.8 us
  transfers between devices with their start and end apart: 19, of which 11 were waited for; matrix products, arithmetic and copies ran while one was open for 1% of the time, Pallas kernels for 10%

profile of v4, /device:TPU:32, one launch (start us, length us, event | category | flops | bytes accessed | tf_op | source)
XLA Modules:
  0.0 108.0 jit_solution(680299248385672547)
XLA Ops:
  0.6 1.4 %copy-done = bf16[1,1024,768]{2,1,0:T(8,128)(2,1)S(1)} copy-done((bf16[1,1024,768]{2,1,0:T(8,128)(2,1)S(1)}, bf16[1,1024,768]{2,1,0:T(8,128)(2,1)}, u32[]{:S(2)}) %copy-start) | copy-done | bytes 1572888
  2.0 1.4 %copy-done.2 = bf16[1,1024,768]{2,1,0:T(8,128)(2,1)S(1)} copy-done((bf16[1,1024,768]{2,1,0:T(8,128)(2,1)S(1)}, bf16[1,1024,768]{2,1,0:T(8,128)(2,1)}, u32[]{:S(2)}) %copy-start.2) | copy-done | bytes 1572888
  3.5 1.4 %copy-done.4 = bf16[1,768,1024]{2,1,0:T(8,128)(2,1)S(1)} copy-done((bf16[1,768,1024]{2,1,0:T(8,128)(2,1)S(1)}, bf16[1,768,1024]{2,1,0:T(8,128)(2,1)}, u32[]{:S(2)}) %copy-start.4) | copy-done | bytes 1572888
  4.9 1.2 %copy-done.13 = bf16[1,512,1024]{2,1,0:T(8,128)(2,1)S(1)} copy-done((bf16[1,512,1024]{2,1,0:T(8,128)(2,1)S(1)}, bf16[1,512,1024]{2,1,0:T(8,128)(2,1)}, u32[]{:S(2)}) %copy-start.13) | copy-done | bytes 1048600
  6.1 4.4 %shard_map.194 = (f32[512,1024]{1,0:T(8,128)S(1)}, f32[512,768]{1,0:T(8,128)S(1)}, f32[512,768]{1,0:T(8,128)S(1)}, bf16[768,512]{1,0:T(8,128)(2,1)S(1)}, bf16[10...) custom-call(bf16[512,1024]{1,0:T(8,128)(2,1)S(1)} %bitcast.34, bf16[1024,768]{1,0:T(8,128)(2,1)S(1)} %bitcast.22, ...), custom_call_target="tpu_custom_call" | custom-call | flops 2415919104 | tf_op jit(solution)/shard_map/pallas_call | solution.py:56
  10.5 1.1 %copy-done.15 = f32[512,768]{1,0:T(8,128)} copy-done((f32[512,768]{1,0:T(8,128)}, f32[512,768]{1,0:T(8,128)S(1)}, u32[]{:S(2)}) %copy-start.15) | copy-done | bytes 1572888
  11.6 1.1 %copy-done.17 = f32[512,768]{1,0:T(8,128)} copy-done((f32[512,768]{1,0:T(8,128)}, f32[512,768]{1,0:T(8,128)S(1)}, u32[]{:S(2)}) %copy-start.17) | copy-done | bytes 1572888
  12.8 0.9 copy-done.19
  14.4 1.6 %shard_map.190 = (f32[3,1,512]{2,1,0:T(1,128)S(1)}, f32[4,2048]{1,0:T(4,128)S(1)}, s32[8,128]{1,0:T(8,128)S(1)}) custom-call(s32[5]{0:T(128)S(1)} %stack.19.place_ref, f32[3,1,512]{2,1,0:T(1,128)} %bitcast.39, f32[4,2048]{1,0:T(4,128)} %weight_hbm.1), custom_call_target="tpu_custom_call" | custom-call | flops 99999997952 | tf_op jit(solution)/shard_map/pallas_call | solution.py:56
  16.0 6.4 %collective-permute-start.6 = (f32[4,2048]{1,0:T(4,128)S(1)}, f32[4,2048]{1,0:T(4,128)S(1)}, u32[]{:S(2)}, u32[]{:S(2)}) collective-permute-start(f32[4,2048]{1,0:T(4,128)S(1)} %get-tuple-element.32.own), channel_id=1, source_target_pairs={{8,0},{10,2},{12,4},{14,6},{0,8},{2,10},{4,12},{6,14},{11,1},{13,3... | collective-permute-start | bytes 98312 | tf_op jit(solution)/shard_map/ppermute | solution.py:197
  22.5 1.4 %collective-permute-start.4 = (f32[4,2048]{1,0:T(4,128)S(1)}, f32[4,2048]{1,0:T(4,128)S(1)}, u32[]{:S(2)}, u32[]{:S(2)}) collective-permute-start(f32[4,2048]{1,0:T(4,128)S(1)} %get-tuple-element.32.own), channel_id=1, source_target_pairs={{4,0},{6,2},{8,4},{10,6},{12,8},{14,10},{0,12},{2,14},{15,1},{1,3}... | collective-permute-start | bytes 98312 | tf_op jit(solution)/shard_map/ppermute | solution.py:197
  24.5 4.8 %collective-permute-done.5.r2 = f32[4,2048]{1,0:T(4,128)S(1)} collective-permute-done((f32[4,2048]{1,0:T(4,128)S(1)}, f32[4,2048]{1,0:T(4,128)S(1)}, u32[]{:S(2)}, u32[]{:S(2)}) %collective-permute-start.5) | collective-permute-done | bytes 32800 | tf_op jit(solution)/shard_map/ppermute | solution.py:197
  29.4 1.7 %collective-permute-start.9 = (f32[16,2048]{1,0:T(8,128)S(1)}, f32[16,2048]{1,0:T(8,128)S(1)}, u32[]{:S(2)}, u32[]{:S(2)}) collective-permute-start(f32[16,2048]{1,0:T(8,128)S(1)} %shard_map.191.r0), channel_id=1, source_target_pairs={{48,0},{0,16},{16,32},{32,48},{49,1},{1,17},{17,33},{33,49},{50,2}... | collective-permute-start | bytes 393224 | tf_op jit(solution)/shard_map/ppermute | solution.py:181
  31.0 2.9 %collective-permute-start.8 = (f32[16,2048]{1,0:T(8,128)S(1)}, f32[16,2048]{1,0:T(8,128)S(1)}, u32[]{:S(2)}, u32[]{:S(2)}) collective-permute-start(f32[16,2048]{1,0:T(8,128)S(1)} %shard_map.191.r0), channel_id=1, source_target_pairs={{32,0},{48,16},{0,32},{16,48},{33,1},{49,17},{1,33},{17,49},{34,2}... | collective-permute-start | bytes 393224 | tf_op jit(solution)/shard_map/ppermute | solution.py:181
  33.9 1.3 %collective-permute-start.7 = (f32[16,2048]{1,0:T(8,128)S(1)}, f32[16,2048]{1,0:T(8,128)S(1)}, u32[]{:S(2)}, u32[]{:S(2)}) collective-permute-start(f32[16,2048]{1,0:T(8,128)S(1)} %shard_map.191.r0), channel_id=1, source_target_pairs={{16,0},{32,16},{48,32},{0,48},{17,1},{33,17},{49,33},{1,49},{18,2}... | collective-permute-start | bytes 393224 | tf_op jit(solution)/shard_map/ppermute | solution.py:181
  35.3 1.5 %collective-permute-start.2 = (f32[3,1,512]{2,1,0:T(1,128)S(1)}, f32[3,1,512]{2,1,0:T(1,128)S(1)}, u32[]{:S(2)}, u32[]{:S(2)}) collective-permute-start(f32[3,1,512]{2,1,0:T(1,128)S(1)} %get-tuple-element.31.h0), channel_id=1, source_target_pairs={{192,0},{0,64},{64,128},{128,192},{193,1},{1,65},{65,129},{129,193... | collective-permute-start | bytes 18440 | tf_op jit(solution)/shard_map/ppermute | solution.py:181
  36.8 3.3 %collective-permute-done.2.h3 = f32[3,1,512]{2,1,0:T(1,128)S(1)} collective-permute-done((f32[3,1,512]{2,1,0:T(1,128)S(1)}, f32[3,1,512]{2,1,0:T(1,128)S(1)}, u32[]{:S(2)}, u32[]{:S(2)}) %collective-permute-start.2) | collective-permute-done | bytes 6176 | tf_op jit(solution)/shard_map/ppermute | solution.py:181
  40.1 1.8 %collective-permute-start.1 = (f32[3,1,512]{2,1,0:T(1,128)S(1)}, f32[3,1,512]{2,1,0:T(1,128)S(1)}, u32[]{:S(2)}, u32[]{:S(2)}) collective-permute-start(f32[3,1,512]{2,1,0:T(1,128)S(1)} %get-tuple-element.31.h0), channel_id=1, source_target_pairs={{128,0},{192,64},{0,128},{64,192},{129,1},{193,65},{1,129},{65,193... | collective-permute-start | bytes 18440 | tf_op jit(solution)/shard_map/ppermute | solution.py:181
  41.9 3.3 %collective-permute-done.1.h2 = f32[3,1,512]{2,1,0:T(1,128)S(1)} collective-permute-done((f32[3,1,512]{2,1,0:T(1,128)S(1)}, f32[3,1,512]{2,1,0:T(1,128)S(1)}, u32[]{:S(2)}, u32[]{:S(2)}) %collective-permute-start.1) | collective-permute-done | bytes 6176 | tf_op jit(solution)/shard_map/ppermute | solution.py:181
  45.3 1.5 %collective-permute-start = (f32[3,1,512]{2,1,0:T(1,128)S(1)}, f32[3,1,512]{2,1,0:T(1,128)S(1)}, u32[]{:S(2)}, u32[]{:S(2)}) collective-permute-start(f32[3,1,512]{2,1,0:T(1,128)S(1)} %get-tuple-element.31.h0), channel_id=1, source_target_pairs={{64,0},{128,64},{192,128},{0,192},{65,1},{129,65},{193,129},{1,193... | collective-permute-start | bytes 18440 | tf_op jit(solution)/shard_map/ppermute | solution.py:181
  46.8 2.1 %collective-permute-done.h1 = f32[3,1,512]{2,1,0:T(1,128)S(1)} collective-permute-done((f32[3,1,512]{2,1,0:T(1,128)S(1)}, f32[3,1,512]{2,1,0:T(1,128)S(1)}, u32[]{:S(2)}, u32[]{:S(2)}) %collective-permute-start) | collective-permute-done | bytes 6176 | tf_op jit(solution)/shard_map/ppermute | solution.py:181
  48.9 1.3 %shard_map.192 = (f32[3,2048]{1,0:T(4,128)S(1)}, f32[3,2048]{1,0:T(4,128)S(1)}, f32[3,2048]{1,0:T(4,128)S(1)}, f32[3,2048]{1,0:T(4,128)S(1)}) custom-call(s32[8,128]{1,0:T(8,128)S(1)} %get-tuple-element.30.info_ref, f32[3,1,512]{2,1,0:T(1,128)S(1)} %get-tuple-element.31.h0, f32[3,1,512]{2,1,0:T(1,128)S(1)} %collective-permute-done.h1, ...), custom_call_target="tpu_custom_call" | custom-call | flops 4194304 | tf_op jit(solution)/shard_map/pallas_call | solution.py:56
  50.6 4.0 %collective-permute-start.11 = (f32[3,2048]{1,0:T(4,128)S(1)}, f32[3,2048]{1,0:T(4,128)S(1)}, u32[]{:S(2)}, u32[]{:S(2)}) collective-permute-start(f32[3,2048]{1,0:T(4,128)S(1)} %get-tuple-element.35), channel_id=1, source_target_pairs={{128,0},{192,64},{0,128},{64,192},{129,1},{193,65},{1,129},{65,193... | collective-permute-start | bytes 73736 | tf_op jit(solution)/shard_map/ppermute | solution.py:181
  55.4 1.3 %collective-permute-done.11.m2 = f32[3,2048]{1,0:T(4,128)S(1)} collective-permute-done((f32[3,2048]{1,0:T(4,128)S(1)}, f32[3,2048]{1,0:T(4,128)S(1)}, u32[]{:S(2)}, u32[]{:S(2)}) %collective-permute-start.11) | collective-permute-done | bytes 24608 | tf_op jit(solution)/shard_map/ppermute | solution.py:181
  56.8 1.7 %collective-permute-done.12.m3 = f32[3,2048]{1,0:T(4,128)S(1)} collective-permute-done((f32[3,2048]{1,0:T(4,128)S(1)}, f32[3,2048]{1,0:T(4,128)S(1)}, u32[]{:S(2)}, u32[]{:S(2)}) %collective-permute-start.12) | collective-permute-done | bytes 24608 | tf_op jit(solution)/shard_map/ppermute | solution.py:181
  58.9 7.9 %shard_map.195 = (f32[1024,768]{1,0:T(8,128)S(1)}, f32[1024,768]{1,0:T(8,128)S(1)}, f32[768,1024]{1,0:T(8,128)S(1)}, f32[16,128]{1,0:T(8,128)S(1)}) custom-call(f32[512,1024]{1,0:T(8,128)S(1)} %get-tuple-element.37.own_ref, f32[512,1024]{1,0:T(8,128)} %collective-permute-done.14.recv_ref, bf16[512,1024]{1,0:T(8,128)(2,1)S(1)} %bitcast.35, ...), custom_call_target="tpu_custom_call" | custom-call | flops 3221225472 | tf_op jit(solution)/shard_map/pallas_call | solution.py:56
  67.4 0.8 collective-permute-done.15.sq_recv_ref
  68.2 14.1 %shard_map.196 = (bf16[1024,768]{1,0:T(8,128)(2,1)}, bf16[1024,768]{1,0:T(8,128)(2,1)}, bf16[768,1024]{1,0:T(8,128)(2,1)}, f32[3,1,512]{2,1,0:T(1,128)S(1)}, f32...) custom-call(s32[8,128]{1,0:T(8,128)S(1)} %get-tuple-element.30.info_ref, ...), custom_call_target="tpu_custom_call" | custom-call | flops 2415919104 | tf_op jit(solution)/shard_map/pallas_call | solution.py:56
  82.8 2.3 %collective-permute-done.16.recv_ref = f32[256,1024]{1,0:T(8,128)S(1)} collective-permute-done((f32[256,1024]{1,0:T(8,128)S(1)}, f32[256,1024]{1,0:T(8,128)S(1)}, u32[]{:S(2)}, u32[]{:S(2)}) %collective-permute-start.16) | collective-permute-done | bytes 1048608 | tf_op jit(solution)/shard_map/ppermute | solution.py:185
  86.1 0.8 collective-permute-done.17.theirs_ref
  87.6 8.5 %all-to-all-start = ((f32[128,1,1]{2,1,0:T(1,128)}), f32[128,1,1]{2,1,0:T(1,128)S(1)}, u32[]{:S(2)}, u32[]{:S(2)}) async-start(f32[128,1,1]{2,1,0:T(1,128)} %shard_map.198), calls=%async_computation | async-start | bytes 131072 | tf_op jit(solution)/shard_map/all_to_all | solution.py:464
  97.2 10.0 %all-to-all-done = f32[128,1,1]{2,1,0:T(1,128)S(1)} async-done(((f32[128,1,1]{2,1,0:T(1,128)}), f32[128,1,1]{2,1,0:T(1,128)S(1)}, u32[]{:S(2)}, u32[]{:S(2)}) %all-to-all-start) | async-done | bytes 544 | tf_op jit(solution)/shard_map/all_to_all | solution.py:464
  (61 shorter events, 7.0 us)
Async XLA Ops:
  13.7 45.1 %collective-permute-start.14 = (f32[512,1024]{1,0:T(8,128)S(1)}, f32[512,1024]{1,0:T(8,128)}, u32[]{:S(2)}, u32[]{:S(2)}) collective-permute-start(f32[512,1024]{1,0:T(8,128)S(1)} %get-tuple-element.37.own_ref), channel_id=1, source_target_pairs={{0,1},{1,0},{2,3},{3,2},{4,5},{5,4},{6,7},{7,6},{8,9},{9,8},{10,11... | collective-permute-start | bytes 6291464 | tf_op jit(solution)/shard_map/ppermute | solution.py:185
  14.4 44.3 %copy-start.5 = (bf16[1,768,1024]{2,1,0:T(8,128)(2,1)S(1)}, bf16[1,768,1024]{2,1,0:T(8,128)(2,1)}, u32[]{:S(2)}) copy-start(bf16[1,768,1024]{2,1,0:T(8,128)(2,1)} %param.21) | copy-start | bytes 4718596
  14.4 44.4 %copy-start.14 = (bf16[1,512,1024]{2,1,0:T(8,128)(2,1)S(1)}, bf16[1,512,1024]{2,1,0:T(8,128)(2,1)}, u32[]{:S(2)}) copy-start(bf16[1,512,1024]{2,1,0:T(8,128)(2,1)} %param.16) | copy-start | bytes 3145732
  14.4 44.4 %copy-start.16 = (f32[512,768]{1,0:T(8,128)S(1)}, f32[512,768]{1,0:T(8,128)}, u32[]{:S(2)}) copy-start(f32[512,768]{1,0:T(8,128)} %copy-done.15) | copy-start | bytes 4718596
  14.4 44.4 %copy-start.18 = (f32[512,768]{1,0:T(8,128)S(1)}, f32[512,768]{1,0:T(8,128)}, u32[]{:S(2)}) copy-start(f32[512,768]{1,0:T(8,128)} %copy-done.17) | copy-start | bytes 4718596
  14.4 44.4 %copy-start.20 = (bf16[768,512]{1,0:T(8,128)(2,1)S(1)}, bf16[768,512]{1,0:T(8,128)(2,1)}, u32[]{:S(2)}) copy-start(bf16[768,512]{1,0:T(8,128)(2,1)} %copy-done.19) | copy-start | bytes 2359300
  16.0 8.5 %collective-permute-start.6 = (f32[4,2048]{1,0:T(4,128)S(1)}, f32[4,2048]{1,0:T(4,128)S(1)}, u32[]{:S(2)}, u32[]{:S(2)}) collective-permute-start(f32[4,2048]{1,0:T(4,128)S(1)} %get-tuple-element.32.own), channel_id=1, source_target_pairs={{8,0},{10,2},{12,4},{14,6},{0,8},{2,10},{4,12},{6,14},{11,1},{13,3... | collective-permute-start | bytes 98312 | tf_op jit(solution)/shard_map/ppermute | solution.py:197
  22.4 6.9 %collective-permute-start.5 = (f32[4,2048]{1,0:T(4,128)S(1)}, f32[4,2048]{1,0:T(4,128)S(1)}, u32[]{:S(2)}, u32[]{:S(2)}) collective-permute-start(f32[4,2048]{1,0:T(4,128)S(1)} %get-tuple-element.32.own), channel_id=1, source_target_pairs={{6,0},{8,2},{10,4},{12,6},{14,8},{0,10},{2,12},{4,14},{13,1},{15,3... | collective-permute-start | bytes 98312 | tf_op jit(solution)/shard_map/ppermute | solution.py:197
  22.5 6.8 %collective-permute-start.4 = (f32[4,2048]{1,0:T(4,128)S(1)}, f32[4,2048]{1,0:T(4,128)S(1)}, u32[]{:S(2)}, u32[]{:S(2)}) collective-permute-start(f32[4,2048]{1,0:T(4,128)S(1)} %get-tuple-element.32.own), channel_id=1, source_target_pairs={{4,0},{6,2},{8,4},{10,6},{12,8},{14,10},{0,12},{2,14},{15,1},{1,3}... | collective-permute-start | bytes 98312 | tf_op jit(solution)/shard_map/ppermute | solution.py:197
  23.9 5.5 %collective-permute-start.3 = (f32[4,2048]{1,0:T(4,128)S(1)}, f32[4,2048]{1,0:T(4,128)S(1)}, u32[]{:S(2)}, u32[]{:S(2)}) collective-permute-start(f32[4,2048]{1,0:T(4,128)S(1)} %get-tuple-element.32.own), channel_id=1, source_target_pairs={{3,1},{5,3},{7,5},{9,7},{11,9},{13,11},{15,13},{1,15},{19,17},{21,... | collective-permute-start | bytes 98312 | tf_op jit(solution)/shard_map/ppermute | solution.py:197
  29.4 19.5 %collective-permute-start.9 = (f32[16,2048]{1,0:T(8,128)S(1)}, f32[16,2048]{1,0:T(8,128)S(1)}, u32[]{:S(2)}, u32[]{:S(2)}) collective-permute-start(f32[16,2048]{1,0:T(8,128)S(1)} %shard_map.191.r0), channel_id=1, source_target_pairs={{48,0},{0,16},{16,32},{32,48},{49,1},{1,17},{17,33},{33,49},{50,2}... | collective-permute-start | bytes 393224 | tf_op jit(solution)/shard_map/ppermute | solution.py:181
  31.0 17.9 %collective-permute-start.8 = (f32[16,2048]{1,0:T(8,128)S(1)}, f32[16,2048]{1,0:T(8,128)S(1)}, u32[]{:S(2)}, u32[]{:S(2)}) collective-permute-start(f32[16,2048]{1,0:T(8,128)S(1)} %shard_map.191.r0), channel_id=1, source_target_pairs={{32,0},{48,16},{0,32},{16,48},{33,1},{49,17},{1,33},{17,49},{34,2}... | collective-permute-start | bytes 393224 | tf_op jit(solution)/shard_map/ppermute | solution.py:181
  33.9 15.0 %collective-permute-start.7 = (f32[16,2048]{1,0:T(8,128)S(1)}, f32[16,2048]{1,0:T(8,128)S(1)}, u32[]{:S(2)}, u32[]{:S(2)}) collective-permute-start(f32[16,2048]{1,0:T(8,128)S(1)} %shard_map.191.r0), channel_id=1, source_target_pairs={{16,0},{32,16},{48,32},{0,48},{17,1},{33,17},{49,33},{1,49},{18,2}... | collective-permute-start | bytes 393224 | tf_op jit(solution)/shard_map/ppermute | solution.py:181
  35.3 4.8 %collective-permute-start.2 = (f32[3,1,512]{2,1,0:T(1,128)S(1)}, f32[3,1,512]{2,1,0:T(1,128)S(1)}, u32[]{:S(2)}, u32[]{:S(2)}) collective-permute-start(f32[3,1,512]{2,1,0:T(1,128)S(1)} %get-tuple-element.31.h0), channel_id=1, source_target_pairs={{192,0},{0,64},{64,128},{128,192},{193,1},{1,65},{65,129},{129,193... | collective-permute-start | bytes 18440 | tf_op jit(solution)/shard_map/ppermute | solution.py:181
  40.1 5.1 %collective-permute-start.1 = (f32[3,1,512]{2,1,0:T(1,128)S(1)}, f32[3,1,512]{2,1,0:T(1,128)S(1)}, u32[]{:S(2)}, u32[]{:S(2)}) collective-permute-start(f32[3,1,512]{2,1,0:T(1,128)S(1)} %get-tuple-element.31.h0), channel_id=1, source_target_pairs={{128,0},{192,64},{0,128},{64,192},{129,1},{193,65},{1,129},{65,193... | collective-permute-start | bytes 18440 | tf_op jit(solution)/shard_map/ppermute | solution.py:181
  45.3 3.6 %collective-permute-start = (f32[3,1,512]{2,1,0:T(1,128)S(1)}, f32[3,1,512]{2,1,0:T(1,128)S(1)}, u32[]{:S(2)}, u32[]{:S(2)}) collective-permute-start(f32[3,1,512]{2,1,0:T(1,128)S(1)} %get-tuple-element.31.h0), channel_id=1, source_target_pairs={{64,0},{128,64},{192,128},{0,192},{65,1},{129,65},{193,129},{1,193... | collective-permute-start | bytes 18440 | tf_op jit(solution)/shard_map/ppermute | solution.py:181
  50.3 5.2 %collective-permute-start.10 = (f32[3,2048]{1,0:T(4,128)S(1)}, f32[3,2048]{1,0:T(4,128)S(1)}, u32[]{:S(2)}, u32[]{:S(2)}) collective-permute-start(f32[3,2048]{1,0:T(4,128)S(1)} %get-tuple-element.34), channel_id=1, source_target_pairs={{192,0},{0,64},{64,128},{128,192},{193,1},{1,65},{65,129},{129,193... | collective-permute-start | bytes 73736 | tf_op jit(solution)/shard_map/ppermute | solution.py:181
  50.6 6.2 %collective-permute-start.11 = (f32[3,2048]{1,0:T(4,128)S(1)}, f32[3,2048]{1,0:T(4,128)S(1)}, u32[]{:S(2)}, u32[]{:S(2)}) collective-permute-start(f32[3,2048]{1,0:T(4,128)S(1)} %get-tuple-element.35), channel_id=1, source_target_pairs={{128,0},{192,64},{0,128},{64,192},{129,1},{193,65},{1,129},{65,193... | collective-permute-start | bytes 73736 | tf_op jit(solution)/shard_map/ppermute | solution.py:181
  54.5 3.9 %collective-permute-start.12 = (f32[3,2048]{1,0:T(4,128)S(1)}, f32[3,2048]{1,0:T(4,128)S(1)}, u32[]{:S(2)}, u32[]{:S(2)}) collective-permute-start(f32[3,2048]{1,0:T(4,128)S(1)} %get-tuple-element.36), channel_id=1, source_target_pairs={{64,0},{128,64},{192,128},{0,192},{65,1},{129,65},{193,129},{1,193... | collective-permute-start | bytes 73736 | tf_op jit(solution)/shard_map/ppermute | solution.py:181
  58.5 8.9 %collective-permute-start.13 = (f32[3,2048]{1,0:T(4,128)S(1)}, f32[3,2048]{1,0:T(4,128)S(1)}, u32[]{:S(2)}, u32[]{:S(2)}) collective-permute-start(f32[3,2048]{1,0:T(4,128)S(1)} %shard_map.193.mine_ref), channel_id=1, source_target_pairs={{0,1},{1,0},{2,3},{3,2},{4,5},{5,4},{6,7},{7,6},{8,9},{9,8},{10,11... | collective-permute-start | bytes 73736 | tf_op jit(solution)/shard_map/ppermute | solution.py:185
  58.8 9.4 %copy-start.1 = (bf16[1,1024,768]{2,1,0:T(8,128)(2,1)S(1)}, bf16[1,1024,768]{2,1,0:T(8,128)(2,1)}, u32[]{:S(2)}) copy-start(bf16[1,1024,768]{2,1,0:T(8,128)(2,1)} %param.19) | copy-start | bytes 4718596
  58.8 9.4 %copy-start.3 = (bf16[1,1024,768]{2,1,0:T(8,128)(2,1)S(1)}, bf16[1,1024,768]{2,1,0:T(8,128)(2,1)}, u32[]{:S(2)}) copy-start(bf16[1,1024,768]{2,1,0:T(8,128)(2,1)} %param.20) | copy-start | bytes 4718596
  58.8 9.4 %copy-start.6 = (bf16[1,512,1024]{2,1,0:T(8,128)(2,1)S(1)}, bf16[1,512,1024]{2,1,0:T(8,128)(2,1)}, u32[]{:S(2)}) copy-start(bf16[1,512,1024]{2,1,0:T(8,128)(2,1)} %param.17) | copy-start | bytes 3145732
  58.8 9.4 %copy-start.8 = (f32[3,2048]{1,0:T(4,128)S(1)}, f32[3,2048]{1,0:T(4,128)}, u32[]{:S(2)}) copy-start(f32[3,2048]{1,0:T(4,128)} %in_w_ref.1) | copy-start | bytes 73732
  58.8 9.3 %copy-start.9 = (f32[512,5]{0,1:T(8,128)S(1)}, f32[512,5]{0,1:T(8,128)}, u32[]{:S(2)}) copy-start(f32[512,5]{0,1:T(8,128)} %param.28) | copy-start | bytes 30724
  58.9 9.3 %copy-start.10 = (f32[2048]{0:T(1024)S(1)}, f32[2048]{0:T(1024)}, u32[]{:S(2)}) copy-start(f32[2048]{0:T(1024)} %param.27) | copy-start | bytes 24580
  58.9 9.3 %copy-start.11 = (f32[1,3,512]{2,0,1:T(1,128)S(1)}, f32[1,3,512]{2,0,1:T(1,128)}, u32[]{:S(2)}) copy-start(f32[1,3,512]{2,0,1:T(1,128)} %param.24) | copy-start | bytes 18436
  66.8 1.4 %collective-permute-start.15 = (f32[16,128]{1,0:T(8,128)S(1)}, f32[16,128]{1,0:T(8,128)S(1)}, u32[]{:S(2)}, u32[]{:S(2)}) collective-permute-start(f32[16,128]{1,0:T(8,128)S(1)} %get-tuple-element.43.sq_ref), channel_id=1, source_target_pairs={{0,1},{1,0},{2,3},{3,2},{4,5},{5,4},{6,7},{7,6},{8,9},{9,8},{10,11... | collective-permute-start | bytes 24584 | tf_op jit(solution)/shard_map/ppermute | solution.py:185
  68.2 16.9 %copy-start.7 = (bf16[1,512,1024]{2,1,0:T(8,128)(2,1)S(1)}, bf16[1,512,1024]{2,1,0:T(8,128)(2,1)}, u32[]{:S(2)}) copy-start(bf16[1,512,1024]{2,1,0:T(8,128)(2,1)} %param.18) | copy-start | bytes 3145732
  82.4 2.7 %collective-permute-start.16 = (f32[256,1024]{1,0:T(8,128)S(1)}, f32[256,1024]{1,0:T(8,128)S(1)}, u32[]{:S(2)}, u32[]{:S(2)}) collective-permute-start(f32[256,1024]{1,0:T(8,128)S(1)} %get-tuple-element.53), channel_id=1, source_target_pairs={{0,1},{1,0},{2,3},{3,2},{4,5},{5,4},{6,7},{7,6},{8,9},{9,8},{10,11... | collective-permute-start | bytes 3145736 | tf_op jit(solution)/shard_map/ppermute | solution.py:185
  85.7 1.2 %collective-permute-start.17 = (f32[1,128]{1,0:T(1,128)S(1)}, f32[1,128]{1,0:T(1,128)S(1)}, u32[]{:S(2)}, u32[]{:S(2)}) collective-permute-start(f32[1,128]{1,0:T(1,128)S(1)} %shard_map.197.mine_ref), channel_id=1, source_target_pairs={{0,1},{1,0},{2,3},{3,2},{4,5},{5,4},{6,7},{7,6},{8,9},{9,8},{10,11... | collective-permute-start | bytes 1544 | tf_op jit(solution)/shard_map/ppermute | solution.py:185
  87.6 19.7 %all-to-all-start = ((f32[128,1,1]{2,1,0:T(1,128)}), f32[128,1,1]{2,1,0:T(1,128)S(1)}, u32[]{:S(2)}, u32[]{:S(2)}) async-start(f32[128,1,1]{2,1,0:T(1,128)} %shard_map.198), calls=%async_computation | async-start | bytes 131072 | tf_op jit(solution)/shard_map/all_to_all | solution.py:464
  (8 other events, 18.0 us)

commit v5 on v4

--- a/solution.py
+++ b/solution.py
@@ -231,8 +231,8 @@
     out_ref[...] = (own[...] + m1[...]) + (m2[...] + m3[...])
 
 
-def recurrent_line(weight, info):
-    others = [from_along_z(weight, amounts) for amounts in HOPS]
+def recurrent_line(held, weight, info):
+    others = [from_along_z(held, amounts) for amounts in HOPS]
     shape = (4 * weight.shape[0], weight.shape[1])
     return call(line_kernel, (info, weight, *others), [IN_VMEM] * 6, vmem((shape, f32)), [IN_VMEM], (), 1, 1 << 16)[0]
 
@@ -248,12 +248,47 @@
     return call(sum_kernel, (parts[0], *moved), [IN_VMEM] * 4, vmem((out, f32)), [IN_VMEM], (), 1, 1 << 16)[0]
 
 
+def meta_piece(j, meta, new_g, new_u, new_d, acc):
+    at = piece(j)
+    gate = dot(meta, new_g[:, at])
+    up = dot(meta, new_u[:, at])
+    act = (gate * jax.nn.sigmoid(gate) * up).astype(bf16)
+    part = dot(act, new_d[at, :])
+
+    @pl.when(j == 0)
+    def _():
+        acc[...] = part
+
+    @pl.when(j > 0)
+    def _():
+        acc[...] += part
+
+
+def keep_kernel(info_ref, meta_ref, new_g, new_u, new_d, keep_ref, mine):
+    half = mine.shape[0]
+    mine[...] = jnp.where(info_ref[3:4, 0:1] == 0, meta_ref[:half], meta_ref[half:])
+
+    def body(j, carry):
+        meta_piece(j, mine[...], new_g, new_u, new_d, keep_ref)
+        return carry
+
+    lax.fori_loop(0, new_d.shape[0] // CHUNK, body, 0)
+
+
+def kept(info, meta, new_g, new_u, new_d):
+    tok, width = meta.shape
+    return call(
+        keep_kernel, (info, meta, new_g, new_u, new_d), [IN_VMEM] * 5,
+        vmem(((tok // 2, width), f32)), [IN_VMEM], [pltpu.VMEM((tok // 2, width), bf16)], 6, 1 << 30,
+    )[0]
+
+
 def update_kernel(
     info_ref,
     mine_ref, theirs_ref, sq_ref, sq_recv_ref, in_w_ref, bias_ref, cell_ref, ctx_w_ref, mlp_ref,
     wg_ref, wu_ref, wd_ref, gg_ref, gu_ref, gd_ref, meta_ref,
-    up_g_hbm, up_u_hbm, up_d_hbm, hidden_ref, new_cell_ref, send_ref, keep_ref,
-    cell_old, table, table_s, order, sem, sem_out, out_g, out_u, out_d, new_g, new_u, new_d, acc,
+    up_g_hbm, up_u_hbm, up_d_hbm, hidden_ref, new_cell_ref, send_ref, new_g, new_u, new_d,
+    cell_old, table, table_s, order, sem, sem_out, out_g, out_u, out_d, theirs,
 ):
     count = wg_ref.shape[1] // CHUNK
     units = mlp_ref.shape[1]
@@ -335,10 +370,10 @@
                     total = term if total is None else total + term
                 upd = scale * (total + offset)
                 out_ref[there, lanes] = upd.astype(bf16)
-                new_ref[here, :] = (p - rate * upd).astype(bf16)
+                new_ref[there, lanes] = (p - rate * upd).astype(bf16)
                 return carry
 
-            lax.fori_loop(0, new_ref.shape[0] // strip, body, 0)
+            lax.fori_loop(0, (CHUNK if by_rows else new_ref.shape[0]) // strip, body, 0)
 
         for top in range(units + 1):
             pl.when(positive == top)(functools.partial(variant, top))
@@ -350,6 +385,9 @@
             pltpu.make_async_copy(out_u.at[:, at], up_u_hbm.at[:, at], sem_out.at[1, j]),
             pltpu.make_async_copy(out_d.at[at, :], up_d_hbm.at[at, :], sem_out.at[2, j]),
         )
+
+    half = theirs.shape[0]
+    theirs[...] = jnp.where(info_ref[3:4, 0:1] == 0, meta_ref[half:], meta_ref[:half])
 
     def body(j, carry):
         copies = results(j)
@@ -359,27 +397,10 @@
         copies[1].start()
         change(2, j, wd_ref, gd_ref, out_d, new_d, True, STRIP // 4)
         copies[2].start()
-        meta = meta_ref[...]
-        gate = dot(meta, new_g[...])
-        up = dot(meta, new_u[...])
-        act = (gate * jax.nn.sigmoid(gate) * up).astype(bf16)
-        part = dot(act, new_d[...])
-
-        @pl.when(j == 0)
-        def _():
-            acc[...] = part
-
-        @pl.when(j > 0)
-        def _():
-            acc[...] += part
-
+        meta_piece(j, theirs[...], new_g, new_u, new_d, send_ref)
         return carry
 
     lax.fori_loop(0, count, body, 0)
-    half = acc.shape[0] // 2
-    lower = info_ref[3:4, 0:1] == 0
-    keep_ref[...] = jnp.where(lower, acc[:half], acc[half:])
-    send_ref[...] = jnp.where(lower, acc[half:], acc[:half])
     for j in range(count):
         for copy in results(j):
             copy.wait()
@@ -392,7 +413,8 @@
     tok, width = meta.shape
     hid = wg.shape[1]
     outs = [pltpu.HBM(wg.shape, bf16), pltpu.HBM(wu.shape, bf16), pltpu.HBM(wd.shape, bf16)]
-    outs += vmem((cell.shape, f32), (cell.shape, f32), ((tok // 2, width), f32), ((tok // 2, width), f32))
+    outs += vmem((cell.shape, f32), (cell.shape, f32), ((tok // 2, width), f32))
+    outs += vmem((wg.shape, bf16), (wu.shape, bf16), (wd.shape, bf16))
     scratch = [
         pltpu.VMEM((8, cell.shape[2]), f32),
         pltpu.VMEM((48, 128), f32),
@@ -403,15 +425,12 @@
         pltpu.VMEM(wg.shape, bf16),
         pltpu.VMEM(wu.shape, bf16),
         pltpu.VMEM(wd.shape, bf16),
-        pltpu.VMEM((width, CHUNK), bf16),
-        pltpu.VMEM((width, CHUNK), bf16),
-        pltpu.VMEM((CHUNK, width), bf16),
-        pltpu.VMEM((tok, width), f32),
+        pltpu.VMEM((tok // 2, width), bf16),
     ]
     operands = (info, mine, theirs, sums, sums_recv, in_w, bias, cell, ctx_w, mlp, wg, wu, wd, gg, gu, gd, meta)
     return call(
         update_kernel, operands, [IN_VMEM] * 17,
-        outs, [IN_HBM] * 3 + [IN_VMEM] * 4, scratch, 20, 6 * tok * width * hid,
+        outs, [IN_HBM] * 3 + [IN_VMEM] * 6, scratch, 12, 6 * tok * width * hid,
     )
 
 
@@ -448,19 +467,25 @@
     core = lax.axis_index(SHARD)
     place = jnp.stack([lax.axis_index(X), lax.axis_index(Y), lax.axis_index(Z), core, task_step[0]]).astype(jnp.int32)
     hidden, weight, info = brought(place, hidden_state.transpose(1, 0, 2), recurrent_weight)
-    line = recurrent_line(weight, info)
-    hids = [hidden] + [shifted(hidden, X, k) for k in (1, 2, 3)]
+    state = hidden_state.transpose(1, 0, 2)
+    above = shifted(state, X, 1)
+    below = shifted(state, X, 3)
+    far = shifted(above, X, 1)
+    line = recurrent_line(recurrent_weight, weight, info)
+    hids = (hidden, above, far, below)
     wg, wu, wd = gate_weight[0], up_weight[0], down_weight[0]
     own, p, q, act_t, x_t, param_sq = forward(tokens[0], wg, wu, wd)
     recv = swapped(own)
     mine = recurrent(hids, line, info)
     gg, gu, gd, sums = backward(own, recv, targets[0], wd, p, q, act_t, x_t, param_sq)
-    up_g, up_u, up_d, new_hidden, new_cell, send, keep = update(
+    up_g, up_u, up_d, new_hidden, new_cell, send, new_g, new_u, new_d = update(
         info, mine, swapped(mine), sums, swapped(sums), input_weight, lstm_bias[None], cell_state.transpose(1, 0, 2),
         context_weight.T, mlp_weight, wg, wu, wd, gg, gu, gd, meta_tokens[0],
     )
     count = lax.axis_size(TASK)
-    part = loss_part(info, keep, swapped(send), meta_targets[0], count)
+    theirs = swapped(send)
+    keep = kept(info, meta_tokens[0], new_g, new_u, new_d)
+    part = loss_part(info, keep, theirs, meta_targets[0], count)
     everyone = lax.all_to_all(spread(part, count), TASK, 0, 0, tiled=True)
     meta_loss = jnp.sum(everyone)
     return (

time: 109 us -> 104 us (0.954)
  waiting for transfers between devices: 31.2 us -> 22.3 us
  starting transfers between devices: 33.8 us -> 36.6 us
    ppermute x4, waiting for transfers between devices: 4.8 us -> 0.01 us  [from_along_z(): return lax.ppermute(array, (Z, SHARD), pairs)]
    ppermute x5, waiting for transfers between devices: 3.96 us -> 1.68 us  [swapped(): return lax.ppermute(array, SHARD, [(0, 1), (1, 0)])]
    ppermute x9, waiting for transfers between devices: 12.5 us -> 10.7 us  [shifted(): lax.ppermute(array, axis, [((i + shift) % size, i) for i in range(size)])]
    ppermute x5, starting transfers between devices: 1.65 us -> 3.18 us  [swapped(): return lax.ppermute(array, SHARD, [(0, 1), (1, 0)])]
    ppermute x9, starting transfers between devices: 15.2 us -> 16.7 us  [shifted(): lax.ppermute(array, axis, [((i + shift) % size, i) for i in range(size)])]
    pallas_call x9 -> x10, Pallas kernels: 30.6 us -> 31.5 us  [call(): pl.pallas_call(body, in_specs=specs, out_specs=out_specs, out_shape=outs,...]
    unnamed x44 -> x46, local copies, waits for them, and re-layouts: 9.87 us -> 9.87 us
  transfers between devices with their start and end apart: 19 -> 19, of which waited for: 11 -> 9; matrix products, arithmetic and copies ran while one was open for 1% -> 1% of each run, Pallas kernels for 10% -> 17%
where the time goes in v5:
time: 104 us; the launch traced here: 103 us
  starting transfers between devices  36.6 us (35%)
  Pallas kernels  31.5 us (30%)
  waiting for transfers between devices  22.3 us (21%)
  local copies, waits for them, and re-layouts  9.96 us (10%)
  between operations  1.62 us (2%)
    pallas_call x10, Pallas kernels, call(): pl.pallas_call(body, in_specs=specs, out_specs=out_specs, out_shape=outs,...  31.5 us
    ppermute x9, starting transfers between devices, shifted(): lax.ppermute(array, axis, [((i + shift) % size, i) for i in range(size)])  16.7 us
    ppermute x9, waiting for transfers between devices, shifted(): lax.ppermute(array, axis, [((i + shift) % size, i) for i in range(size)])  10.7 us
    all_to_all x1, waiting for transfers between devices, local(): everyone = lax.all_to_all(spread(part, count), TASK, 0, 0, tiled=True)  9.96 us
    unnamed x46, local copies, waits for them, and re-layouts  9.87 us
    ppermute x4, starting transfers between devices, from_along_z(): return lax.ppermute(array, (Z, SHARD), pairs)  8.55 us
    all_to_all x1, starting transfers between devices, local(): everyone = lax.all_to_all(spread(part, count), TASK, 0, 0, tiled=True)  8.15 us
    ppermute x5, starting transfers between devices, swapped(): return lax.ppermute(array, SHARD, [(0, 1), (1, 0)])  3.18 us
  transfers between devices with their start and end apart: 19, of which 9 were waited for; matrix products, arithmetic and copies ran while one was open for 1% of the time, Pallas kernels for 17%

profile of v5, /device:TPU:32, one launch (start us, length us, event | category | flops | bytes accessed | tf_op | source)
XLA Modules:
  0.0 102.7 jit_solution(4016458079758479859)
XLA Ops:
  0.6 5.5 %collective-permute-start.4 = (f32[4,2048]{1,0:T(4,128)}, f32[4,2048]{1,0:T(4,128)S(1)}, u32[]{:S(2)}, u32[]{:S(2)}) collective-permute-start(f32[4,2048]{1,0:T(4,128)} %weight_hbm.1), channel_id=1, source_target_pairs={{4,0},{6,2},{8,4},{10,6},{12,8},{14,10},{0,12},{2,14},{15,1},{1,3}... | collective-permute-start | bytes 98312 | tf_op jit(solution)/shard_map/ppermute | solution.py:197
  6.8 1.5 %collective-permute-start.6 = (f32[4,2048]{1,0:T(4,128)}, f32[4,2048]{1,0:T(4,128)S(1)}, u32[]{:S(2)}, u32[]{:S(2)}) collective-permute-start(f32[4,2048]{1,0:T(4,128)} %weight_hbm.1), channel_id=1, source_target_pairs={{8,0},{10,2},{12,4},{14,6},{0,8},{2,10},{4,12},{6,14},{11,1},{13,3... | collective-permute-start | bytes 98312 | tf_op jit(solution)/shard_map/ppermute | solution.py:197
  8.3 0.9 collective-permute-start.5
  9.2 1.4 %copy-done.1 = bf16[1,1024,768]{2,1,0:T(8,128)(2,1)S(1)} copy-done((bf16[1,1024,768]{2,1,0:T(8,128)(2,1)S(1)}, bf16[1,1024,768]{2,1,0:T(8,128)(2,1)}, u32[]{:S(2)}) %copy-start.1) | copy-done | bytes 1572888
  10.6 1.4 %copy-done.3 = bf16[1,1024,768]{2,1,0:T(8,128)(2,1)S(1)} copy-done((bf16[1,1024,768]{2,1,0:T(8,128)(2,1)S(1)}, bf16[1,1024,768]{2,1,0:T(8,128)(2,1)}, u32[]{:S(2)}) %copy-start.3) | copy-done | bytes 1572888
  12.0 1.4 %copy-done.5 = bf16[1,768,1024]{2,1,0:T(8,128)(2,1)S(1)} copy-done((bf16[1,768,1024]{2,1,0:T(8,128)(2,1)S(1)}, bf16[1,768,1024]{2,1,0:T(8,128)(2,1)}, u32[]{:S(2)}) %copy-start.5) | copy-done | bytes 1572888
  13.4 1.2 %copy-done.13 = bf16[1,512,1024]{2,1,0:T(8,128)(2,1)S(1)} copy-done((bf16[1,512,1024]{2,1,0:T(8,128)(2,1)S(1)}, bf16[1,512,1024]{2,1,0:T(8,128)(2,1)}, u32[]{:S(2)}) %copy-start.13) | copy-done | bytes 1048600
  14.6 4.4 %shard_map.194 = (f32[512,1024]{1,0:T(8,128)S(1)}, f32[512,768]{1,0:T(8,128)S(1)}, f32[512,768]{1,0:T(8,128)S(1)}, bf16[768,512]{1,0:T(8,128)(2,1)S(1)}, bf16[10...) custom-call(bf16[512,1024]{1,0:T(8,128)(2,1)S(1)} %bitcast.35, bf16[1024,768]{1,0:T(8,128)(2,1)S(1)} %bitcast.24, ...), custom_call_target="tpu_custom_call" | custom-call | flops 2415919104 | tf_op jit(solution)/shard_map/pallas_call | solution.py:56
  19.1 1.1 %copy-done.15 = f32[512,768]{1,0:T(8,128)} copy-done((f32[512,768]{1,0:T(8,128)}, f32[512,768]{1,0:T(8,128)S(1)}, u32[]{:S(2)}) %copy-start.15) | copy-done | bytes 1572888
  20.2 1.1 %copy-done.17 = f32[512,768]{1,0:T(8,128)} copy-done((f32[512,768]{1,0:T(8,128)}, f32[512,768]{1,0:T(8,128)S(1)}, u32[]{:S(2)}) %copy-start.17) | copy-done | bytes 1572888
  21.4 0.9 copy-done.19
  22.2 1.6 %collective-permute-start.14 = (f32[512,1024]{1,0:T(8,128)S(1)}, f32[512,1024]{1,0:T(8,128)}, u32[]{:S(2)}, u32[]{:S(2)}) collective-permute-start(f32[512,1024]{1,0:T(8,128)S(1)} %get-tuple-element.39.own_ref), channel_id=1, source_target_pairs={{0,1},{1,0},{2,3},{3,2},{4,5},{5,4},{6,7},{7,6},{8,9},{9,8},{10,11... | collective-permute-start | bytes 6291464 | tf_op jit(solution)/shard_map/ppermute | solution.py:185
  24.6 1.6 %shard_map.190 = (f32[3,1,512]{2,1,0:T(1,128)S(1)}, f32[4,2048]{1,0:T(4,128)S(1)}, s32[8,128]{1,0:T(8,128)S(1)}) custom-call(s32[5]{0:T(128)S(1)} %stack.19.place_ref, f32[3,1,512]{2,1,0:T(1,128)} %bitcast.40, f32[4,2048]{1,0:T(4,128)} %weight_hbm.1), custom_call_target="tpu_custom_call" | custom-call | flops 99999997952 | tf_op jit(solution)/shard_map/pallas_call | solution.py:56
  26.3 1.7 %collective-permute-start.9 = (f32[16,2048]{1,0:T(8,128)S(1)}, f32[16,2048]{1,0:T(8,128)S(1)}, u32[]{:S(2)}, u32[]{:S(2)}) collective-permute-start(f32[16,2048]{1,0:T(8,128)S(1)} %shard_map.191.r0), channel_id=1, source_target_pairs={{48,0},{0,16},{16,32},{32,48},{49,1},{1,17},{17,33},{33,49},{50,2}... | collective-permute-start | bytes 393224 | tf_op jit(solution)/shard_map/ppermute | solution.py:181
  27.9 2.9 %collective-permute-start.8 = (f32[16,2048]{1,0:T(8,128)S(1)}, f32[16,2048]{1,0:T(8,128)S(1)}, u32[]{:S(2)}, u32[]{:S(2)}) collective-permute-start(f32[16,2048]{1,0:T(8,128)S(1)} %shard_map.191.r0), channel_id=1, source_target_pairs={{32,0},{48,16},{0,32},{16,48},{33,1},{49,17},{1,33},{17,49},{34,2}... | collective-permute-start | bytes 393224 | tf_op jit(solution)/shard_map/ppermute | solution.py:181
  30.8 1.3 %collective-permute-start.7 = (f32[16,2048]{1,0:T(8,128)S(1)}, f32[16,2048]{1,0:T(8,128)S(1)}, u32[]{:S(2)}, u32[]{:S(2)}) collective-permute-start(f32[16,2048]{1,0:T(8,128)S(1)} %shard_map.191.r0), channel_id=1, source_target_pairs={{16,0},{32,16},{48,32},{0,48},{17,1},{33,17},{49,33},{1,49},{18,2}... | collective-permute-start | bytes 393224 | tf_op jit(solution)/shard_map/ppermute | solution.py:181
  32.2 1.5 %collective-permute-start.2 = (f32[3,1,512]{2,1,0:T(1,128)S(1)}, f32[3,1,512]{2,1,0:T(1,128)S(1)}, u32[]{:S(2)}, u32[]{:S(2)}) collective-permute-start(f32[3,1,512]{2,1,0:T(1,128)S(1)} %bitcast.41), channel_id=1, source_target_pairs={{192,0},{0,64},{64,128},{128,192},{193,1},{1,65},{65,129},{129,193... | collective-permute-start | bytes 18440 | tf_op jit(solution)/shard_map/ppermute | solution.py:181
  33.7 3.3 %collective-permute-done.2.h3 = f32[3,1,512]{2,1,0:T(1,128)S(1)} collective-permute-done((f32[3,1,512]{2,1,0:T(1,128)S(1)}, f32[3,1,512]{2,1,0:T(1,128)S(1)}, u32[]{:S(2)}, u32[]{:S(2)}) %collective-permute-start.2) | collective-permute-done | bytes 6176 | tf_op jit(solution)/shard_map/ppermute | solution.py:181
  37.0 1.6 %collective-permute-start = (f32[3,1,512]{2,1,0:T(1,128)S(1)}, f32[3,1,512]{2,1,0:T(1,128)S(1)}, u32[]{:S(2)}, u32[]{:S(2)}) collective-permute-start(f32[3,1,512]{2,1,0:T(1,128)S(1)} %bitcast.42), channel_id=1, source_target_pairs={{64,0},{128,64},{192,128},{0,192},{65,1},{129,65},{193,129},{1,193... | collective-permute-start | bytes 18440 | tf_op jit(solution)/shard_map/ppermute | solution.py:181
  38.6 2.1 %collective-permute-done.h1 = f32[3,1,512]{2,1,0:T(1,128)S(1)} collective-permute-done((f32[3,1,512]{2,1,0:T(1,128)S(1)}, f32[3,1,512]{2,1,0:T(1,128)S(1)}, u32[]{:S(2)}, u32[]{:S(2)}) %collective-permute-start) | collective-permute-done | bytes 6176 | tf_op jit(solution)/shard_map/ppermute | solution.py:181
  40.7 2.8 %collective-permute-start.1 = (f32[3,1,512]{2,1,0:T(1,128)S(1)}, f32[3,1,512]{2,1,0:T(1,128)S(1)}, u32[]{:S(2)}, u32[]{:S(2)}) collective-permute-start(f32[3,1,512]{2,1,0:T(1,128)S(1)} %collective-permute-done.h1), channel_id=1, source_target_pairs={{64,0},{128,64},{192,128},{0,192},{65,1},{129,65},{193,129},{1,193... | collective-permute-start | bytes 18440 | tf_op jit(solution)/shard_map/ppermute | solution.py:181
  43.4 1.3 %collective-permute-done.1.h2 = f32[3,1,512]{2,1,0:T(1,128)S(1)} collective-permute-done((f32[3,1,512]{2,1,0:T(1,128)S(1)}, f32[3,1,512]{2,1,0:T(1,128)S(1)}, u32[]{:S(2)}, u32[]{:S(2)}) %collective-permute-start.1) | collective-permute-done | bytes 6176 | tf_op jit(solution)/shard_map/ppermute | solution.py:181
  44.8 1.3 %shard_map.192 = (f32[3,2048]{1,0:T(4,128)S(1)}, f32[3,2048]{1,0:T(4,128)S(1)}, f32[3,2048]{1,0:T(4,128)S(1)}, f32[3,2048]{1,0:T(4,128)S(1)}) custom-call(s32[8,128]{1,0:T(8,128)S(1)} %get-tuple-element.32.info_ref, f32[3,1,512]{2,1,0:T(1,128)S(1)} %get-tuple-element.33.h0, f32[3,1,512]{2,1,0:T(1,128)S(1)} %collective-permute-done.h1, ...), custom_call_target="tpu_custom_call" | custom-call | flops 4194304 | tf_op jit(solution)/shard_map/pallas_call | solution.py:56
  46.2 4.9 %collective-permute-start.11 = (f32[3,2048]{1,0:T(4,128)S(1)}, f32[3,2048]{1,0:T(4,128)S(1)}, u32[]{:S(2)}, u32[]{:S(2)}) collective-permute-start(f32[3,2048]{1,0:T(4,128)S(1)} %get-tuple-element.37), channel_id=1, source_target_pairs={{128,0},{192,64},{0,128},{64,192},{129,1},{193,65},{1,129},{65,193... | collective-permute-start | bytes 73736 | tf_op jit(solution)/shard_map/ppermute | solution.py:181
  51.6 1.8 %collective-permute-done.11.m2 = f32[3,2048]{1,0:T(4,128)S(1)} collective-permute-done((f32[3,2048]{1,0:T(4,128)S(1)}, f32[3,2048]{1,0:T(4,128)S(1)}, u32[]{:S(2)}, u32[]{:S(2)}) %collective-permute-start.11) | collective-permute-done | bytes 24608 | tf_op jit(solution)/shard_map/ppermute | solution.py:181
  53.4 1.7 %collective-permute-done.12.m3 = f32[3,2048]{1,0:T(4,128)S(1)} collective-permute-done((f32[3,2048]{1,0:T(4,128)S(1)}, f32[3,2048]{1,0:T(4,128)S(1)}, u32[]{:S(2)}, u32[]{:S(2)}) %collective-permute-start.12) | collective-permute-done | bytes 24608 | tf_op jit(solution)/shard_map/ppermute | solution.py:181
  55.5 7.9 %shard_map.195 = (f32[1024,768]{1,0:T(8,128)S(1)}, f32[1024,768]{1,0:T(8,128)S(1)}, f32[768,1024]{1,0:T(8,128)S(1)}, f32[16,128]{1,0:T(8,128)S(1)}) custom-call(f32[512,1024]{1,0:T(8,128)S(1)} %get-tuple-element.39.own_ref, f32[512,1024]{1,0:T(8,128)} %collective-permute-done.14.recv_ref, bf16[512,1024]{1,0:T(8,128)(2,1)S(1)} %bitcast.36, ...), custom_call_target="tpu_custom_call" | custom-call | flops 3221225472 | tf_op jit(solution)/shard_map/pallas_call | solution.py:56
  64.8 12.7 %shard_map.196 = (bf16[1024,768]{1,0:T(8,128)(2,1)}, bf16[1024,768]{1,0:T(8,128)(2,1)}, bf16[768,1024]{1,0:T(8,128)(2,1)}, f32[3,1,512]{2,1,0:T(1,128)S(1)}, f32...) custom-call(s32[8,128]{1,0:T(8,128)S(1)} %get-tuple-element.32.info_, ...), custom_call_target="tpu_custom_call" | custom-call | flops 2415919104 | tf_op jit(solution)/shard_map/pallas_call | solution.py:56
  77.9 2.3 %shard_map.197.keep_ref = f32[256,1024]{1,0:T(8,128)S(1)} custom-call(s32[8,128]{1,0:T(8,128)S(1)} %get-tuple-element.32.info_ref, bf16[512,1024]{1,0:T(8,128)(2,1)S(1)} %bitcast.23, bf16[1024,768]{1,0:T(8,128)(2,1)S(1)} %get-tuple-element.54.new_g, bf16[1024,768]{1,0:T(8,128)(2,1)S(1)} %get-tuple-element.55.new_u, bf16[768,1024]{1,0:T(8,128)(2,1)S(1)} %get-tuple-element.56.new_d), custom_call_target="tpu_custom_call" | custom-call | flops 1073741824 | tf_op jit(solution)/shard_map/pallas_call | solution.py:56
  81.2 0.8 collective-permute-done.17.theirs_ref
  82.7 8.1 %all-to-all-start = ((f32[128,1,1]{2,1,0:T(1,128)}), f32[128,1,1]{2,1,0:T(1,128)S(1)}, u32[]{:S(2)}, u32[]{:S(2)}) async-start(f32[128,1,1]{2,1,0:T(1,128)} %shard_map.199), calls=%async_computation | async-start | bytes 131072 | tf_op jit(solution)/shard_map/all_to_all | solution.py:489
  92.0 10.0 %all-to-all-done = f32[128,1,1]{2,1,0:T(1,128)S(1)} async-done(((f32[128,1,1]{2,1,0:T(1,128)}), f32[128,1,1]{2,1,0:T(1,128)S(1)}, u32[]{:S(2)}, u32[]{:S(2)}) %all-to-all-start) | async-done | bytes 544 | tf_op jit(solution)/shard_map/all_to_all | solution.py:489
  (64 shorter events, 7.0 us)
Async XLA Ops:
  0.6 25.6 %collective-permute-start.4 = (f32[4,2048]{1,0:T(4,128)}, f32[4,2048]{1,0:T(4,128)S(1)}, u32[]{:S(2)}, u32[]{:S(2)}) collective-permute-start(f32[4,2048]{1,0:T(4,128)} %weight_hbm.1), channel_id=1, source_target_pairs={{4,0},{6,2},{8,4},{10,6},{12,8},{14,10},{0,12},{2,14},{15,1},{1,3}... | collective-permute-start | bytes 98312 | tf_op jit(solution)/shard_map/ppermute | solution.py:197
  6.1 20.1 %collective-permute-start.3 = (f32[4,2048]{1,0:T(4,128)}, f32[4,2048]{1,0:T(4,128)S(1)}, u32[]{:S(2)}, u32[]{:S(2)}) collective-permute-start(f32[4,2048]{1,0:T(4,128)} %weight_hbm.1), channel_id=1, source_target_pairs={{3,1},{5,3},{7,5},{9,7},{11,9},{13,11},{15,13},{1,15},{19,17},{21,... | collective-permute-start | bytes 98312 | tf_op jit(solution)/shard_map/ppermute | solution.py:197
  6.8 19.5 %collective-permute-start.6 = (f32[4,2048]{1,0:T(4,128)}, f32[4,2048]{1,0:T(4,128)S(1)}, u32[]{:S(2)}, u32[]{:S(2)}) collective-permute-start(f32[4,2048]{1,0:T(4,128)} %weight_hbm.1), channel_id=1, source_target_pairs={{8,0},{10,2},{12,4},{14,6},{0,8},{2,10},{4,12},{6,14},{11,1},{13,3... | collective-permute-start | bytes 98312 | tf_op jit(solution)/shard_map/ppermute | solution.py:197
  8.3 17.9 %collective-permute-start.5 = (f32[4,2048]{1,0:T(4,128)}, f32[4,2048]{1,0:T(4,128)S(1)}, u32[]{:S(2)}, u32[]{:S(2)}) collective-permute-start(f32[4,2048]{1,0:T(4,128)} %weight_hbm.1), channel_id=1, source_target_pairs={{6,0},{8,2},{10,4},{12,6},{14,8},{0,10},{2,12},{4,14},{13,1},{15,3... | collective-permute-start | bytes 98312 | tf_op jit(solution)/shard_map/ppermute | solution.py:197
  22.2 33.1 %collective-permute-start.14 = (f32[512,1024]{1,0:T(8,128)S(1)}, f32[512,1024]{1,0:T(8,128)}, u32[]{:S(2)}, u32[]{:S(2)}) collective-permute-start(f32[512,1024]{1,0:T(8,128)S(1)} %get-tuple-element.39.own_ref), channel_id=1, source_target_pairs={{0,1},{1,0},{2,3},{3,2},{4,5},{5,4},{6,7},{7,6},{8,9},{9,8},{10,11... | collective-permute-start | bytes 6291464 | tf_op jit(solution)/shard_map/ppermute | solution.py:185
  24.5 30.8 %copy-start.6 = (bf16[1,768,1024]{2,1,0:T(8,128)(2,1)S(1)}, bf16[1,768,1024]{2,1,0:T(8,128)(2,1)}, u32[]{:S(2)}) copy-start(bf16[1,768,1024]{2,1,0:T(8,128)(2,1)} %param.21) | copy-start | bytes 4718596
  24.5 30.8 %copy-start.14 = (bf16[1,512,1024]{2,1,0:T(8,128)(2,1)S(1)}, bf16[1,512,1024]{2,1,0:T(8,128)(2,1)}, u32[]{:S(2)}) copy-start(bf16[1,512,1024]{2,1,0:T(8,128)(2,1)} %param.16) | copy-start | bytes 3145732
  24.5 30.8 %copy-start.16 = (f32[512,768]{1,0:T(8,128)S(1)}, f32[512,768]{1,0:T(8,128)}, u32[]{:S(2)}) copy-start(f32[512,768]{1,0:T(8,128)} %copy-done.15) | copy-start | bytes 4718596
  24.6 30.8 %copy-start.18 = (f32[512,768]{1,0:T(8,128)S(1)}, f32[512,768]{1,0:T(8,128)}, u32[]{:S(2)}) copy-start(f32[512,768]{1,0:T(8,128)} %copy-done.17) | copy-start | bytes 4718596
  24.6 30.8 %copy-start.20 = (bf16[768,512]{1,0:T(8,128)(2,1)S(1)}, bf16[768,512]{1,0:T(8,128)(2,1)}, u32[]{:S(2)}) copy-start(bf16[768,512]{1,0:T(8,128)(2,1)} %copy-done.19) | copy-start | bytes 2359300
  26.3 18.5 %collective-permute-start.9 = (f32[16,2048]{1,0:T(8,128)S(1)}, f32[16,2048]{1,0:T(8,128)S(1)}, u32[]{:S(2)}, u32[]{:S(2)}) collective-permute-start(f32[16,2048]{1,0:T(8,128)S(1)} %shard_map.191.r0), channel_id=1, source_target_pairs={{48,0},{0,16},{16,32},{32,48},{49,1},{1,17},{17,33},{33,49},{50,2}... | collective-permute-start | bytes 393224 | tf_op jit(solution)/shard_map/ppermute | solution.py:181
  27.9 16.8 %collective-permute-start.8 = (f32[16,2048]{1,0:T(8,128)S(1)}, f32[16,2048]{1,0:T(8,128)S(1)}, u32[]{:S(2)}, u32[]{:S(2)}) collective-permute-start(f32[16,2048]{1,0:T(8,128)S(1)} %shard_map.191.r0), channel_id=1, source_target_pairs={{32,0},{48,16},{0,32},{16,48},{33,1},{49,17},{1,33},{17,49},{34,2}... | collective-permute-start | bytes 393224 | tf_op jit(solution)/shard_map/ppermute | solution.py:181
  30.8 13.9 %collective-permute-start.7 = (f32[16,2048]{1,0:T(8,128)S(1)}, f32[16,2048]{1,0:T(8,128)S(1)}, u32[]{:S(2)}, u32[]{:S(2)}) collective-permute-start(f32[16,2048]{1,0:T(8,128)S(1)} %shard_map.191.r0), channel_id=1, source_target_pairs={{16,0},{32,16},{48,32},{0,48},{17,1},{33,17},{49,33},{1,49},{18,2}... | collective-permute-start | bytes 393224 | tf_op jit(solution)/shard_map/ppermute | solution.py:181
  32.2 4.8 %collective-permute-start.2 = (f32[3,1,512]{2,1,0:T(1,128)S(1)}, f32[3,1,512]{2,1,0:T(1,128)S(1)}, u32[]{:S(2)}, u32[]{:S(2)}) collective-permute-start(f32[3,1,512]{2,1,0:T(1,128)S(1)} %bitcast.41), channel_id=1, source_target_pairs={{192,0},{0,64},{64,128},{128,192},{193,1},{1,65},{65,129},{129,193... | collective-permute-start | bytes 18440 | tf_op jit(solution)/shard_map/ppermute | solution.py:181
  37.0 3.6 %collective-permute-start = (f32[3,1,512]{2,1,0:T(1,128)S(1)}, f32[3,1,512]{2,1,0:T(1,128)S(1)}, u32[]{:S(2)}, u32[]{:S(2)}) collective-permute-start(f32[3,1,512]{2,1,0:T(1,128)S(1)} %bitcast.42), channel_id=1, source_target_pairs={{64,0},{128,64},{192,128},{0,192},{65,1},{129,65},{193,129},{1,193... | collective-permute-start | bytes 18440 | tf_op jit(solution)/shard_map/ppermute | solution.py:181
  40.7 4.1 %collective-permute-start.1 = (f32[3,1,512]{2,1,0:T(1,128)S(1)}, f32[3,1,512]{2,1,0:T(1,128)S(1)}, u32[]{:S(2)}, u32[]{:S(2)}) collective-permute-start(f32[3,1,512]{2,1,0:T(1,128)S(1)} %collective-permute-done.h1), channel_id=1, source_target_pairs={{64,0},{128,64},{192,128},{0,192},{65,1},{129,65},{193,129},{1,193... | collective-permute-start | bytes 18440 | tf_op jit(solution)/shard_map/ppermute | solution.py:181
  46.1 5.4 %collective-permute-start.10 = (f32[3,2048]{1,0:T(4,128)S(1)}, f32[3,2048]{1,0:T(4,128)S(1)}, u32[]{:S(2)}, u32[]{:S(2)}) collective-permute-start(f32[3,2048]{1,0:T(4,128)S(1)} %get-tuple-element.36), channel_id=1, source_target_pairs={{192,0},{0,64},{64,128},{128,192},{193,1},{1,65},{65,129},{129,193... | collective-permute-start | bytes 73736 | tf_op jit(solution)/shard_map/ppermute | solution.py:181
  46.2 7.2 %collective-permute-start.11 = (f32[3,2048]{1,0:T(4,128)S(1)}, f32[3,2048]{1,0:T(4,128)S(1)}, u32[]{:S(2)}, u32[]{:S(2)}) collective-permute-start(f32[3,2048]{1,0:T(4,128)S(1)} %get-tuple-element.37), channel_id=1, source_target_pairs={{128,0},{192,64},{0,128},{64,192},{129,1},{193,65},{1,129},{65,193... | collective-permute-start | bytes 73736 | tf_op jit(solution)/shard_map/ppermute | solution.py:181
  51.1 3.9 %collective-permute-start.12 = (f32[3,2048]{1,0:T(4,128)S(1)}, f32[3,2048]{1,0:T(4,128)S(1)}, u32[]{:S(2)}, u32[]{:S(2)}) collective-permute-start(f32[3,2048]{1,0:T(4,128)S(1)} %get-tuple-element.38), channel_id=1, source_target_pairs={{64,0},{128,64},{192,128},{0,192},{65,1},{129,65},{193,129},{1,193... | collective-permute-start | bytes 73736 | tf_op jit(solution)/shard_map/ppermute | solution.py:181
  55.1 8.9 %collective-permute-start.13 = (f32[3,2048]{1,0:T(4,128)S(1)}, f32[3,2048]{1,0:T(4,128)S(1)}, u32[]{:S(2)}, u32[]{:S(2)}) collective-permute-start(f32[3,2048]{1,0:T(4,128)S(1)} %shard_map.193.mine_ref), channel_id=1, source_target_pairs={{0,1},{1,0},{2,3},{3,2},{4,5},{5,4},{6,7},{7,6},{8,9},{9,8},{10,11... | collective-permute-start | bytes 73736 | tf_op jit(solution)/shard_map/ppermute | solution.py:185
  55.4 9.4 %copy-start = (bf16[1,512,1024]{2,1,0:T(8,128)(2,1)S(1)}, bf16[1,512,1024]{2,1,0:T(8,128)(2,1)}, u32[]{:S(2)}) copy-start(bf16[1,512,1024]{2,1,0:T(8,128)(2,1)} %param.17) | copy-start | bytes 3145732
  55.4 9.4 %copy-start.2 = (bf16[1,1024,768]{2,1,0:T(8,128)(2,1)S(1)}, bf16[1,1024,768]{2,1,0:T(8,128)(2,1)}, u32[]{:S(2)}) copy-start(bf16[1,1024,768]{2,1,0:T(8,128)(2,1)} %param.19) | copy-start | bytes 4718596
  55.4 9.3 %copy-start.4 = (bf16[1,1024,768]{2,1,0:T(8,128)(2,1)S(1)}, bf16[1,1024,768]{2,1,0:T(8,128)(2,1)}, u32[]{:S(2)}) copy-start(bf16[1,1024,768]{2,1,0:T(8,128)(2,1)} %param.20) | copy-start | bytes 4718596
  55.4 9.3 %copy-start.8 = (f32[3,2048]{1,0:T(4,128)S(1)}, f32[3,2048]{1,0:T(4,128)}, u32[]{:S(2)}) copy-start(f32[3,2048]{1,0:T(4,128)} %in_w_ref.1) | copy-start | bytes 73732
  55.4 9.3 %copy-start.9 = (f32[512,5]{0,1:T(8,128)S(1)}, f32[512,5]{0,1:T(8,128)}, u32[]{:S(2)}) copy-start(f32[512,5]{0,1:T(8,128)} %param.28) | copy-start | bytes 30724
  55.5 9.3 %copy-start.10 = (f32[2048]{0:T(1024)S(1)}, f32[2048]{0:T(1024)}, u32[]{:S(2)}) copy-start(f32[2048]{0:T(1024)} %param.27) | copy-start | bytes 24580
  55.5 9.3 %copy-start.11 = (f32[1,3,512]{2,0,1:T(1,128)S(1)}, f32[1,3,512]{2,0,1:T(1,128)}, u32[]{:S(2)}) copy-start(f32[1,3,512]{2,0,1:T(1,128)} %param.24) | copy-start | bytes 18436
  55.5 9.3 %copy-start.12 = (f32[3,4]{1,0:T(4,128)S(1)}, f32[3,4]{1,0:T(4,128)}, u32[]{:S(2)}) copy-start(f32[3,4]{1,0:T(4,128)} %mlp_ref.1) | copy-start | bytes 148
  63.4 1.4 %collective-permute-start.15 = (f32[16,128]{1,0:T(8,128)S(1)}, f32[16,128]{1,0:T(8,128)S(1)}, u32[]{:S(2)}, u32[]{:S(2)}) collective-permute-start(f32[16,128]{1,0:T(8,128)S(1)} %get-tuple-element.45.sq_ref), channel_id=1, source_target_pairs={{0,1},{1,0},{2,3},{3,2},{4,5},{5,4},{6,7},{7,6},{8,9},{9,8},{10,11... | collective-permute-start | bytes 24584 | tf_op jit(solution)/shard_map/ppermute | solution.py:185
  77.5 2.8 %collective-permute-start.16 = (f32[256,1024]{1,0:T(8,128)S(1)}, f32[256,1024]{1,0:T(8,128)S(1)}, u32[]{:S(2)}, u32[]{:S(2)}) collective-permute-start(f32[256,1024]{1,0:T(8,128)S(1)} %get-tuple-element.57), channel_id=1, source_target_pairs={{0,1},{1,0},{2,3},{3,2},{4,5},{5,4},{6,7},{7,6},{8,9},{9,8},{10,11... | collective-permute-start | bytes 3145736 | tf_op jit(solution)/shard_map/ppermute | solution.py:185
  80.8 1.2 %collective-permute-start.17 = (f32[1,128]{1,0:T(1,128)S(1)}, f32[1,128]{1,0:T(1,128)S(1)}, u32[]{:S(2)}, u32[]{:S(2)}) collective-permute-start(f32[1,128]{1,0:T(1,128)S(1)} %shard_map.198.mine_ref), channel_id=1, source_target_pairs={{0,1},{1,0},{2,3},{3,2},{4,5},{5,4},{6,7},{7,6},{8,9},{9,8},{10,11... | collective-permute-start | bytes 1544 | tf_op jit(solution)/shard_map/ppermute | solution.py:185
  82.7 19.3 %all-to-all-start = ((f32[128,1,1]{2,1,0:T(1,128)}), f32[128,1,1]{2,1,0:T(1,128)S(1)}, u32[]{:S(2)}, u32[]{:S(2)}) async-start(f32[128,1,1]{2,1,0:T(1,128)} %shard_map.199), calls=%async_computation | async-start | bytes 131072 | tf_op jit(solution)/shard_map/all_to_all | solution.py:489
  (9 other events, 18.6 us)

commit v6 on v5

--- a/solution.py
+++ b/solution.py
@@ -197,28 +197,16 @@
     return lax.ppermute(array, (Z, SHARD), pairs)
 
 
-def first_kernel(place_ref, hidden_hbm, weight_hbm, hidden_ref, weight_ref, info_ref, sems):
-    copies = (
-        pltpu.make_async_copy(weight_hbm, weight_ref, sems.at[0]),
-        pltpu.make_async_copy(hidden_hbm, hidden_ref, sems.at[1]),
-    )
-    for copy in copies:
-        copy.start()
+def first_kernel(place_ref, info_ref):
     row = lax.broadcasted_iota(jnp.int32, info_ref.shape, 0)
     info = jnp.zeros(info_ref.shape, jnp.int32)
     for k in range(5):
         info = jnp.where(row == k, place_ref[k], info)
     info_ref[...] = info
-    for copy in copies:
-        copy.wait()
-
-
-def brought(place, hidden, weight):
-    return call(
-        first_kernel, (place, hidden, weight), [IN_SMEM] + [IN_HBM] * 2,
-        vmem((hidden.shape, f32), (weight.shape, f32), ((8, 128), jnp.int32)),
-        [IN_VMEM] * 3, [pltpu.SemaphoreType.DMA((2,))], 1, 100_000_000_000,
-    )
+
+
+def first(place):
+    return call(first_kernel, (place,), [IN_SMEM], vmem(((8, 128), jnp.int32)), [IN_VMEM], (), 1, 100_000_000_000)[0]
 
 
 def line_kernel(info_ref, own, r0, r1, r2, r3, out_ref):
@@ -227,12 +215,17 @@
         out_ref[4 * k + 4 : 4 * k + 8, :] = r_ref[...]
 
 
-def sum_kernel(own, m1, m2, m3, out_ref):
-    out_ref[...] = (own[...] + m1[...]) + (m2[...] + m3[...])
-
-
-def recurrent_line(held, weight, info):
-    others = [from_along_z(held, amounts) for amounts in HOPS]
+def sum_kernel(own, m1, m2, m3, sq_ref, out_ref):
+    rows = own.shape[0]
+    out_ref[0:rows, :] = (own[...] + m1[...]) + (m2[...] + m3[...])
+    out_ref[rows : rows + 1, :] = jnp.zeros_like(out_ref[rows : rows + 1, :])
+    for k in range(3):
+        out_ref[rows : rows + 1, 128 * k : 128 * k + 128] = sq_ref[k : k + 1, :]
+        out_ref[rows : rows + 1, 128 * (k + 3) : 128 * (k + 4)] = sq_ref[8 + k : 9 + k, :]
+
+
+def recurrent_line(weight, info):
+    others = [from_along_z(weight, amounts) for amounts in HOPS]
     shape = (4 * weight.shape[0], weight.shape[1])
     return call(line_kernel, (info, weight, *others), [IN_VMEM] * 6, vmem((shape, f32)), [IN_VMEM], (), 1, 1 << 16)[0]
 
@@ -244,8 +237,12 @@
         recurrent_kernel, (info, *hids, *plane), [IN_VMEM] * 9,
         vmem(*[(out, f32)] * 4), [IN_VMEM] * 4, [pltpu.VMEM((32, hids[0].shape[2]), f32)], 4, 1 << 22,
     )
-    moved = [shifted(parts[k], X, -k) for k in (1, 2, 3)]
-    return call(sum_kernel, (parts[0], *moved), [IN_VMEM] * 4, vmem((out, f32)), [IN_VMEM], (), 1, 1 << 16)[0]
+    return [parts[0]] + [shifted(parts[k], X, -k) for k in (1, 2, 3)]
+
+
+def sent_across(parts, sums):
+    shape = (parts[0].shape[0] + 1, parts[0].shape[1])
+    return call(sum_kernel, (*parts, sums), [IN_VMEM] * 5, vmem((shape, f32)), [IN_VMEM], (), 1, 1 << 16)[0]
 
 
 def meta_piece(j, meta, new_g, new_u, new_d, acc):
@@ -285,17 +282,20 @@
 
 def update_kernel(
     info_ref,
-    mine_ref, theirs_ref, sq_ref, sq_recv_ref, in_w_ref, bias_ref, cell_ref, ctx_w_ref, mlp_ref,
+    mine_ref, theirs_ref, in_w_ref, bias_ref, cell_ref, ctx_w_ref, mlp_ref,
     wg_ref, wu_ref, wd_ref, gg_ref, gu_ref, gd_ref, meta_ref,
     up_g_hbm, up_u_hbm, up_d_hbm, hidden_ref, new_cell_ref, send_ref, new_g, new_u, new_d,
-    cell_old, table, table_s, order, sem, sem_out, out_g, out_u, out_d, theirs,
+    squared, cell_old, table, table_s, order, sem, sem_out, out_g, out_u, out_d, theirs,
 ):
     count = wg_ref.shape[1] // CHUNK
     units = mlp_ref.shape[1]
     entries = 2.0 * wg_ref.shape[0] * wg_ref.shape[1]
 
-    sums = sq_ref[...] + sq_recv_ref[...]
-    total = jnp.sum(sums, axis=1, keepdims=True)
+    both = mine_ref[...] + theirs_ref[...]
+    for k in range(3):
+        squared[k : k + 1, :] = both[3:4, 128 * k : 128 * k + 128]
+        squared[8 + k : 9 + k, :] = both[3:4, 128 * (k + 3) : 128 * (k + 4)]
+    total = jnp.sum(squared[...], axis=1, keepdims=True)
     rms = jnp.sqrt(total / entries + epsilon)
     rms_g, rms_p = rms[0:3], rms[8:11]
     logs = jnp.log(rms)
@@ -303,7 +303,7 @@
     in_w = in_w_ref[...]
     lstm_in = (
         (logs[0:3] * in_w[0:1] + logs[8:11] * in_w[1:2] + fraction * in_w[2:3])
-        + (mine_ref[...] + theirs_ref[...])
+        + both[0:3]
         + bias_ref[...]
     )
     width = cell_ref.shape[2]
@@ -406,16 +406,17 @@
             copy.wait()
 
 
-STRIP = 64
-
-
-def update(info, mine, theirs, sums, sums_recv, in_w, bias, cell, ctx_w, mlp, wg, wu, wd, gg, gu, gd, meta):
+STRIP = 256
+
+
+def update(info, mine, theirs, in_w, bias, cell, ctx_w, mlp, wg, wu, wd, gg, gu, gd, meta):
     tok, width = meta.shape
     hid = wg.shape[1]
     outs = [pltpu.HBM(wg.shape, bf16), pltpu.HBM(wu.shape, bf16), pltpu.HBM(wd.shape, bf16)]
     outs += vmem((cell.shape, f32), (cell.shape, f32), ((tok // 2, width), f32))
     outs += vmem((wg.shape, bf16), (wu.shape, bf16), (wd.shape, bf16))
     scratch = [
+        pltpu.VMEM((16, 128), f32),
         pltpu.VMEM((8, cell.shape[2]), f32),
         pltpu.VMEM((48, 128), f32),
         pltpu.SMEM((48, 128), f32),
@@ -427,9 +428,9 @@
         pltpu.VMEM(wd.shape, bf16),
         pltpu.VMEM((tok // 2, width), bf16),
     ]
-    operands = (info, mine, theirs, sums, sums_recv, in_w, bias, cell, ctx_w, mlp, wg, wu, wd, gg, gu, gd, meta)
+    operands = (info, mine, theirs, in_w, bias, cell, ctx_w, mlp, wg, wu, wd, gg, gu, gd, meta)
     return call(
-        update_kernel, operands, [IN_VMEM] * 17,
+        update_kernel, operands, [IN_VMEM] * 15,
         outs, [IN_HBM] * 3 + [IN_VMEM] * 6, scratch, 12, 6 * tok * width * hid,
     )
 
@@ -466,20 +467,18 @@
 ):
     core = lax.axis_index(SHARD)
     place = jnp.stack([lax.axis_index(X), lax.axis_index(Y), lax.axis_index(Z), core, task_step[0]]).astype(jnp.int32)
-    hidden, weight, info = brought(place, hidden_state.transpose(1, 0, 2), recurrent_weight)
-    state = hidden_state.transpose(1, 0, 2)
-    above = shifted(state, X, 1)
-    below = shifted(state, X, 3)
-    far = shifted(above, X, 1)
-    line = recurrent_line(recurrent_weight, weight, info)
-    hids = (hidden, above, far, below)
+    info = first(place)
+    hidden = hidden_state.transpose(1, 0, 2)
+    line = recurrent_line(recurrent_weight, info)
+    hids = [hidden] + [shifted(hidden, X, k) for k in (1, 2, 3)]
     wg, wu, wd = gate_weight[0], up_weight[0], down_weight[0]
     own, p, q, act_t, x_t, param_sq = forward(tokens[0], wg, wu, wd)
     recv = swapped(own)
-    mine = recurrent(hids, line, info)
+    parts = recurrent(hids, line, info)
     gg, gu, gd, sums = backward(own, recv, targets[0], wd, p, q, act_t, x_t, param_sq)
+    mine = sent_across(parts, sums)
     up_g, up_u, up_d, new_hidden, new_cell, send, new_g, new_u, new_d = update(
-        info, mine, swapped(mine), sums, swapped(sums), input_weight, lstm_bias[None], cell_state.transpose(1, 0, 2),
+        info, mine, swapped(mine), input_weight, lstm_bias[None], cell_state.transpose(1, 0, 2),
         context_weight.T, mlp_weight, wg, wu, wd, gg, gu, gd, meta_tokens[0],
     )
     count = lax.axis_size(TASK)

time: 104 us -> 98.9 us (0.951)
  starting transfers between devices: 36.6 us -> 34.4 us
  Pallas kernels: 31.5 us -> 29.7 us
  waiting for transfers between devices: 22.3 us -> 21.1 us
    ppermute x9, waiting for transfers between devices: 10.7 us -> 8.76 us  [shifted(): lax.ppermute(array, axis, [((i + shift) % size, i) for i in range(size)])]
    pallas_call x10, Pallas kernels: 31.5 us -> 29.7 us  [call(): pl.pallas_call(body, in_specs=specs, out_specs=out_specs, out_shape=outs,...]
    ppermute x9, starting transfers between devices: 16.7 us -> 15.2 us  [shifted(): lax.ppermute(array, axis, [((i + shift) % size, i) for i in range(size)])]
    ppermute x5 -> x4, waiting for transfers between devices: 1.68 us -> 2.34 us  [swapped(): return lax.ppermute(array, SHARD, [(0, 1), (1, 0)])]
    ppermute x5 -> x4, starting transfers between devices: 3.18 us -> 3.3 us  [swapped(): return lax.ppermute(array, SHARD, [(0, 1), (1, 0)])]
    unnamed x46 -> x48, local copies, waits for them, and re-layouts: 9.87 us -> 9.99 us
  transfers between devices with their start and end apart: 19 -> 18, of which waited for: 9 -> 7; matrix products, arithmetic and copies ran while one was open for 1% -> 1% of each run, Pallas kernels for 17% -> 17%
where the time goes in v6:
time: 98.9 us; the launch traced here: 97.6 us
  starting transfers between devices  34.4 us (35%)
  Pallas kernels  29.7 us (30%)
  waiting for transfers between devices  21.1 us (21%)
  local copies, waits for them, and re-layouts  10.1 us (10%)
  between operations  1.62 us (2%)
    pallas_call x10, Pallas kernels, call(): pl.pallas_call(body, in_specs=specs, out_specs=out_specs, out_shape=outs,...  29.7 us
    ppermute x9, starting transfers between devices, shifted(): lax.ppermute(array, axis, [((i + shift) % size, i) for i in range(size)])  15.2 us
    unnamed x48, local copies, waits for them, and re-layouts  9.99 us
    all_to_all x1, waiting for transfers between devices, local(): everyone = lax.all_to_all(spread(part, count), TASK, 0, 0, tiled=True)  9.99 us
    ppermute x9, waiting for transfers between devices, shifted(): lax.ppermute(array, axis, [((i + shift) % size, i) for i in range(size)])  8.76 us
    ppermute x4, starting transfers between devices, from_along_z(): return lax.ppermute(array, (Z, SHARD), pairs)  8.55 us
    all_to_all x1, starting transfers between devices, local(): everyone = lax.all_to_all(spread(part, count), TASK, 0, 0, tiled=True)  7.27 us
    ppermute x4, starting transfers between devices, swapped(): return lax.ppermute(array, SHARD, [(0, 1), (1, 0)])  3.3 us
  transfers between devices with their start and end apart: 18, of which 7 were waited for; matrix products, arithmetic and copies ran while one was open for 1% of the time, Pallas kernels for 17%

profile of v6, /device:TPU:32, one launch (start us, length us, event | category | flops | bytes accessed | tf_op | source)
XLA Modules:
  0.0 97.6 jit_solution(2977742008290379402)
XLA Ops:
  0.6 5.9 %collective-permute-start.5 = (f32[4,2048]{1,0:T(4,128)}, f32[4,2048]{1,0:T(4,128)S(1)}, u32[]{:S(2)}, u32[]{:S(2)}) collective-permute-start(f32[4,2048]{1,0:T(4,128)} %own.1), channel_id=1, source_target_pairs={{6,0},{8,2},{10,4},{12,6},{14,8},{0,10},{2,12},{4,14},{13,1},{15,3... | collective-permute-start | bytes 98312 | tf_op jit(solution)/shard_map/ppermute | solution.py:197
  6.6 1.5 %collective-permute-start.4 = (f32[4,2048]{1,0:T(4,128)}, f32[4,2048]{1,0:T(4,128)S(1)}, u32[]{:S(2)}, u32[]{:S(2)}) collective-permute-start(f32[4,2048]{1,0:T(4,128)} %own.1), channel_id=1, source_target_pairs={{4,0},{6,2},{8,4},{10,6},{12,8},{14,10},{0,12},{2,14},{15,1},{1,3}... | collective-permute-start | bytes 98312 | tf_op jit(solution)/shard_map/ppermute | solution.py:197
  8.0 0.7 collective-permute-start.3
  9.2 1.4 %copy-done.1 = bf16[1,1024,768]{2,1,0:T(8,128)(2,1)S(1)} copy-done((bf16[1,1024,768]{2,1,0:T(8,128)(2,1)S(1)}, bf16[1,1024,768]{2,1,0:T(8,128)(2,1)}, u32[]{:S(2)}) %copy-start.1) | copy-done | bytes 1572888
  10.6 1.4 %copy-done.3 = bf16[1,1024,768]{2,1,0:T(8,128)(2,1)S(1)} copy-done((bf16[1,1024,768]{2,1,0:T(8,128)(2,1)S(1)}, bf16[1,1024,768]{2,1,0:T(8,128)(2,1)}, u32[]{:S(2)}) %copy-start.3) | copy-done | bytes 1572888
  12.0 1.4 %copy-done.5 = bf16[1,768,1024]{2,1,0:T(8,128)(2,1)S(1)} copy-done((bf16[1,768,1024]{2,1,0:T(8,128)(2,1)S(1)}, bf16[1,768,1024]{2,1,0:T(8,128)(2,1)}, u32[]{:S(2)}) %copy-start.5) | copy-done | bytes 1572888
  13.4 1.2 %copy-done.15 = bf16[1,512,1024]{2,1,0:T(8,128)(2,1)S(1)} copy-done((bf16[1,512,1024]{2,1,0:T(8,128)(2,1)S(1)}, bf16[1,512,1024]{2,1,0:T(8,128)(2,1)}, u32[]{:S(2)}) %copy-start.15) | copy-done | bytes 1048600
  14.6 4.4 %shard_map.193 = (f32[512,1024]{1,0:T(8,128)S(1)}, f32[512,768]{1,0:T(8,128)S(1)}, f32[512,768]{1,0:T(8,128)S(1)}, bf16[768,512]{1,0:T(8,128)(2,1)S(1)}, bf16[10...) custom-call(bf16[512,1024]{1,0:T(8,128)(2,1)S(1)} %bitcast.39, bf16[1024,768]{1,0:T(8,128)(2,1)S(1)} %bitcast.24, ...), custom_call_target="tpu_custom_call" | custom-call | flops 2415919104 | tf_op jit(solution)/shard_map/pallas_call | solution.py:56
  19.1 1.1 %copy-done.17 = f32[512,768]{1,0:T(8,128)} copy-done((f32[512,768]{1,0:T(8,128)}, f32[512,768]{1,0:T(8,128)S(1)}, u32[]{:S(2)}) %copy-start.17) | copy-done | bytes 1572888
  20.2 1.1 %copy-done.19 = f32[512,768]{1,0:T(8,128)} copy-done((f32[512,768]{1,0:T(8,128)}, f32[512,768]{1,0:T(8,128)S(1)}, u32[]{:S(2)}) %copy-start.19) | copy-done | bytes 1572888
  21.4 0.9 copy-done.21
  22.2 2.8 %collective-permute-start.13 = (f32[512,1024]{1,0:T(8,128)S(1)}, f32[512,1024]{1,0:T(8,128)}, u32[]{:S(2)}, u32[]{:S(2)}) collective-permute-start(f32[512,1024]{1,0:T(8,128)S(1)} %get-tuple-element.33.own_ref), channel_id=1, source_target_pairs={{0,1},{1,0},{2,3},{3,2},{4,5},{5,4},{6,7},{7,6},{8,9},{9,8},{10,11... | collective-permute-start | bytes 6291464 | tf_op jit(solution)/shard_map/ppermute | solution.py:185
  26.5 1.7 %collective-permute-start.9 = (f32[16,2048]{1,0:T(8,128)S(1)}, f32[16,2048]{1,0:T(8,128)S(1)}, u32[]{:S(2)}, u32[]{:S(2)}) collective-permute-start(f32[16,2048]{1,0:T(8,128)S(1)} %shard_map.191.r0), channel_id=1, source_target_pairs={{48,0},{0,16},{16,32},{32,48},{49,1},{1,17},{17,33},{33,49},{50,2}... | collective-permute-start | bytes 393224 | tf_op jit(solution)/shard_map/ppermute | solution.py:181
  28.2 2.9 %collective-permute-start.8 = (f32[16,2048]{1,0:T(8,128)S(1)}, f32[16,2048]{1,0:T(8,128)S(1)}, u32[]{:S(2)}, u32[]{:S(2)}) collective-permute-start(f32[16,2048]{1,0:T(8,128)S(1)} %shard_map.191.r0), channel_id=1, source_target_pairs={{32,0},{48,16},{0,32},{16,48},{33,1},{49,17},{1,33},{17,49},{34,2}... | collective-permute-start | bytes 393224 | tf_op jit(solution)/shard_map/ppermute | solution.py:181
  31.1 1.3 %collective-permute-start.7 = (f32[16,2048]{1,0:T(8,128)S(1)}, f32[16,2048]{1,0:T(8,128)S(1)}, u32[]{:S(2)}, u32[]{:S(2)}) collective-permute-start(f32[16,2048]{1,0:T(8,128)S(1)} %shard_map.191.r0), channel_id=1, source_target_pairs={{16,0},{32,16},{48,32},{0,48},{17,1},{33,17},{49,33},{1,49},{18,2}... | collective-permute-start | bytes 393224 | tf_op jit(solution)/shard_map/ppermute | solution.py:181
  32.4 1.5 %collective-permute-start.2 = (f32[3,1,512]{2,1,0:T(1,128)S(1)}, f32[3,1,512]{2,1,0:T(1,128)S(1)}, u32[]{:S(2)}, u32[]{:S(2)}) collective-permute-start(f32[3,1,512]{2,1,0:T(1,128)S(1)} %bitcast.34), channel_id=1, source_target_pairs={{192,0},{0,64},{64,128},{128,192},{193,1},{1,65},{65,129},{129,193... | collective-permute-start | bytes 18440 | tf_op jit(solution)/shard_map/ppermute | solution.py:181
  33.9 3.3 %collective-permute-done.2.h3 = f32[3,1,512]{2,1,0:T(1,128)S(1)} collective-permute-done((f32[3,1,512]{2,1,0:T(1,128)S(1)}, f32[3,1,512]{2,1,0:T(1,128)S(1)}, u32[]{:S(2)}, u32[]{:S(2)}) %collective-permute-start.2) | collective-permute-done | bytes 6176 | tf_op jit(solution)/shard_map/ppermute | solution.py:181
  37.3 1.8 %collective-permute-start.1 = (f32[3,1,512]{2,1,0:T(1,128)S(1)}, f32[3,1,512]{2,1,0:T(1,128)S(1)}, u32[]{:S(2)}, u32[]{:S(2)}) collective-permute-start(f32[3,1,512]{2,1,0:T(1,128)S(1)} %bitcast.35), channel_id=1, source_target_pairs={{128,0},{192,64},{0,128},{64,192},{129,1},{193,65},{1,129},{65,193... | collective-permute-start | bytes 18440 | tf_op jit(solution)/shard_map/ppermute | solution.py:181
  39.1 3.3 %collective-permute-done.1.h2 = f32[3,1,512]{2,1,0:T(1,128)S(1)} collective-permute-done((f32[3,1,512]{2,1,0:T(1,128)S(1)}, f32[3,1,512]{2,1,0:T(1,128)S(1)}, u32[]{:S(2)}, u32[]{:S(2)}) %collective-permute-start.1) | collective-permute-done | bytes 6176 | tf_op jit(solution)/shard_map/ppermute | solution.py:181
  42.4 1.5 %collective-permute-start = (f32[3,1,512]{2,1,0:T(1,128)S(1)}, f32[3,1,512]{2,1,0:T(1,128)S(1)}, u32[]{:S(2)}, u32[]{:S(2)}) collective-permute-start(f32[3,1,512]{2,1,0:T(1,128)S(1)} %bitcast.36), channel_id=1, source_target_pairs={{64,0},{128,64},{192,128},{0,192},{65,1},{129,65},{193,129},{1,193... | collective-permute-start | bytes 18440 | tf_op jit(solution)/shard_map/ppermute | solution.py:181
  44.0 2.1 %collective-permute-done.h1 = f32[3,1,512]{2,1,0:T(1,128)S(1)} collective-permute-done((f32[3,1,512]{2,1,0:T(1,128)S(1)}, f32[3,1,512]{2,1,0:T(1,128)S(1)}, u32[]{:S(2)}, u32[]{:S(2)}) %collective-permute-start) | collective-permute-done | bytes 6176 | tf_op jit(solution)/shard_map/ppermute | solution.py:181
  46.1 1.3 %shard_map.192 = (f32[3,2048]{1,0:T(4,128)S(1)}, f32[3,2048]{1,0:T(4,128)S(1)}, f32[3,2048]{1,0:T(4,128)S(1)}, f32[3,2048]{1,0:T(4,128)S(1)}) custom-call(s32[8,128]{1,0:T(8,128)S(1)} %shard_map.190.info_ref, f32[3,1,512]{2,1,0:T(1,128)S(1)} %bitcast.37, f32[3,1,512]{2,1,0:T(1,128)S(1)} %collective-permute-done.h1, ...), custom_call_target="tpu_custom_call" | custom-call | flops 4194304 | tf_op jit(solution)/shard_map/pallas_call | solution.py:56
  47.7 4.0 %collective-permute-start.11 = (f32[3,2048]{1,0:T(4,128)S(1)}, f32[3,2048]{1,0:T(4,128)S(1)}, u32[]{:S(2)}, u32[]{:S(2)}) collective-permute-start(f32[3,2048]{1,0:T(4,128)S(1)} %get-tuple-element.31), channel_id=1, source_target_pairs={{128,0},{192,64},{0,128},{64,192},{129,1},{193,65},{1,129},{65,193... | collective-permute-start | bytes 73736 | tf_op jit(solution)/shard_map/ppermute | solution.py:181
  52.0 7.8 %shard_map.194 = (f32[1024,768]{1,0:T(8,128)S(1)}, f32[1024,768]{1,0:T(8,128)S(1)}, f32[768,1024]{1,0:T(8,128)S(1)}, f32[16,128]{1,0:T(8,128)S(1)}) custom-call(f32[512,1024]{1,0:T(8,128)S(1)} %get-tuple-element.33.own_ref, f32[512,1024]{1,0:T(8,128)} %collective-permute-done.13.recv_ref, bf16[512,1024]{1,0:T(8,128)(2,1)S(1)} %bitcast.40, ...), custom_call_target="tpu_custom_call" | custom-call | flops 3221225472 | tf_op jit(solution)/shard_map/pallas_call | solution.py:56
  60.0 1.2 %collective-permute-done.14.theirs_ref = f32[4,2048]{1,0:T(4,128)S(1)} collective-permute-done((f32[4,2048]{1,0:T(4,128)S(1)}, f32[4,2048]{1,0:T(4,128)S(1)}, u32[]{:S(2)}, u32[]{:S(2)}) %collective-permute-start.14) | collective-permute-done | bytes 32800 | tf_op jit(solution)/shard_map/ppermute | solution.py:185
  61.3 12.0 %shard_map.196 = (bf16[1024,768]{1,0:T(8,128)(2,1)}, bf16[1024,768]{1,0:T(8,128)(2,1)}, bf16[768,1024]{1,0:T(8,128)(2,1)}, f32[3,1,512]{2,1,0:T(1,128)S(1)}, f32...) custom-call(s32[8,128]{1,0:T(8,128)S(1)} %shard_map.190.info_ref, ...), custom_call_target="tpu_custom_call" | custom-call | flops 2415919104 | tf_op jit(solution)/shard_map/pallas_call | solution.py:56
  73.5 2.3 %shard_map.197.keep_ref = f32[256,1024]{1,0:T(8,128)S(1)} custom-call(s32[8,128]{1,0:T(8,128)S(1)} %shard_map.190.info_ref, bf16[512,1024]{1,0:T(8,128)(2,1)S(1)} %bitcast.23, bf16[1024,768]{1,0:T(8,128)(2,1)S(1)} %get-tuple-element.48.new_g, bf16[1024,768]{1,0:T(8,128)(2,1)S(1)} %get-tuple-element.49.new_u, bf16[768,1024]{1,0:T(8,128)(2,1)S(1)} %get-tuple-element.50.new_d), custom_call_target="tpu_custom_call" | custom-call | flops 1073741824 | tf_op jit(solution)/shard_map/pallas_call | solution.py:56
  76.8 1.0 collective-permute-done.16.theirs_ref
  77.7 0.7 shard_map.199
  78.4 7.3 %all-to-all-start = ((f32[128,1,1]{2,1,0:T(1,128)}), f32[128,1,1]{2,1,0:T(1,128)S(1)}, u32[]{:S(2)}, u32[]{:S(2)}) async-start(f32[128,1,1]{2,1,0:T(1,128)} %shard_map.199), calls=%async_computation | async-start | bytes 131072 | tf_op jit(solution)/shard_map/all_to_all | solution.py:488
  86.8 10.0 %all-to-all-done = f32[128,1,1]{2,1,0:T(1,128)S(1)} async-done(((f32[128,1,1]{2,1,0:T(1,128)}), f32[128,1,1]{2,1,0:T(1,128)S(1)}, u32[]{:S(2)}, u32[]{:S(2)}) %all-to-all-start) | async-done | bytes 544 | tf_op jit(solution)/shard_map/all_to_all | solution.py:488
  96.8 0.7 reduce_sum.9
  (64 shorter events, 4.4 us)
Async XLA Ops:
  0.6 25.7 %collective-permute-start.5 = (f32[4,2048]{1,0:T(4,128)}, f32[4,2048]{1,0:T(4,128)S(1)}, u32[]{:S(2)}, u32[]{:S(2)}) collective-permute-start(f32[4,2048]{1,0:T(4,128)} %own.1), channel_id=1, source_target_pairs={{6,0},{8,2},{10,4},{12,6},{14,8},{0,10},{2,12},{4,14},{13,1},{15,3... | collective-permute-start | bytes 98312 | tf_op jit(solution)/shard_map/ppermute | solution.py:197
  6.6 19.8 %collective-permute-start.4 = (f32[4,2048]{1,0:T(4,128)}, f32[4,2048]{1,0:T(4,128)S(1)}, u32[]{:S(2)}, u32[]{:S(2)}) collective-permute-start(f32[4,2048]{1,0:T(4,128)} %own.1), channel_id=1, source_target_pairs={{4,0},{6,2},{8,4},{10,6},{12,8},{14,10},{0,12},{2,14},{15,1},{1,3}... | collective-permute-start | bytes 98312 | tf_op jit(solution)/shard_map/ppermute | solution.py:197
  8.0 18.3 %collective-permute-start.3 = (f32[4,2048]{1,0:T(4,128)}, f32[4,2048]{1,0:T(4,128)S(1)}, u32[]{:S(2)}, u32[]{:S(2)}) collective-permute-start(f32[4,2048]{1,0:T(4,128)} %own.1), channel_id=1, source_target_pairs={{3,1},{5,3},{7,5},{9,7},{11,9},{13,11},{15,13},{1,15},{19,17},{21,... | collective-permute-start | bytes 98312 | tf_op jit(solution)/shard_map/ppermute | solution.py:197
  8.7 17.7 %collective-permute-start.6 = (f32[4,2048]{1,0:T(4,128)}, f32[4,2048]{1,0:T(4,128)S(1)}, u32[]{:S(2)}, u32[]{:S(2)}) collective-permute-start(f32[4,2048]{1,0:T(4,128)} %own.1), channel_id=1, source_target_pairs={{8,0},{10,2},{12,4},{14,6},{0,8},{2,10},{4,12},{6,14},{11,1},{13,3... | collective-permute-start | bytes 98312 | tf_op jit(solution)/shard_map/ppermute | solution.py:197
  22.2 29.7 %collective-permute-start.13 = (f32[512,1024]{1,0:T(8,128)S(1)}, f32[512,1024]{1,0:T(8,128)}, u32[]{:S(2)}, u32[]{:S(2)}) collective-permute-start(f32[512,1024]{1,0:T(8,128)S(1)} %get-tuple-element.33.own_ref), channel_id=1, source_target_pairs={{0,1},{1,0},{2,3},{3,2},{4,5},{5,4},{6,7},{7,6},{8,9},{9,8},{10,11... | collective-permute-start | bytes 6291464 | tf_op jit(solution)/shard_map/ppermute | solution.py:185
  25.7 6.7 %copy-start.12 = (f32[1,3,512]{2,0,1:T(1,128)S(1)}, f32[1,3,512]{2,0,1:T(1,128)}, u32[]{:S(2)}) copy-start(f32[1,3,512]{2,0,1:T(1,128)} %param.23) | copy-start | bytes 18436
  25.7 26.2 %copy-start.6 = (bf16[1,768,1024]{2,1,0:T(8,128)(2,1)S(1)}, bf16[1,768,1024]{2,1,0:T(8,128)(2,1)}, u32[]{:S(2)}) copy-start(bf16[1,768,1024]{2,1,0:T(8,128)(2,1)} %param.21) | copy-start | bytes 4718596
  25.7 26.2 %copy-start.16 = (bf16[1,512,1024]{2,1,0:T(8,128)(2,1)S(1)}, bf16[1,512,1024]{2,1,0:T(8,128)(2,1)}, u32[]{:S(2)}) copy-start(bf16[1,512,1024]{2,1,0:T(8,128)(2,1)} %param.16) | copy-start | bytes 3145732
  25.7 26.2 %copy-start.18 = (f32[512,768]{1,0:T(8,128)S(1)}, f32[512,768]{1,0:T(8,128)}, u32[]{:S(2)}) copy-start(f32[512,768]{1,0:T(8,128)} %copy-done.17) | copy-start | bytes 4718596
  25.8 26.2 %copy-start.20 = (f32[512,768]{1,0:T(8,128)S(1)}, f32[512,768]{1,0:T(8,128)}, u32[]{:S(2)}) copy-start(f32[512,768]{1,0:T(8,128)} %copy-done.19) | copy-start | bytes 4718596
  25.8 26.2 %copy-start.22 = (bf16[768,512]{1,0:T(8,128)(2,1)S(1)}, bf16[768,512]{1,0:T(8,128)(2,1)}, u32[]{:S(2)}) copy-start(bf16[768,512]{1,0:T(8,128)(2,1)} %copy-done.21) | copy-start | bytes 2359300
  26.5 19.5 %collective-permute-start.9 = (f32[16,2048]{1,0:T(8,128)S(1)}, f32[16,2048]{1,0:T(8,128)S(1)}, u32[]{:S(2)}, u32[]{:S(2)}) collective-permute-start(f32[16,2048]{1,0:T(8,128)S(1)} %shard_map.191.r0), channel_id=1, source_target_pairs={{48,0},{0,16},{16,32},{32,48},{49,1},{1,17},{17,33},{33,49},{50,2}... | collective-permute-start | bytes 393224 | tf_op jit(solution)/shard_map/ppermute | solution.py:181
  28.2 17.9 %collective-permute-start.8 = (f32[16,2048]{1,0:T(8,128)S(1)}, f32[16,2048]{1,0:T(8,128)S(1)}, u32[]{:S(2)}, u32[]{:S(2)}) collective-permute-start(f32[16,2048]{1,0:T(8,128)S(1)} %shard_map.191.r0), channel_id=1, source_target_pairs={{32,0},{48,16},{0,32},{16,48},{33,1},{49,17},{1,33},{17,49},{34,2}... | collective-permute-start | bytes 393224 | tf_op jit(solution)/shard_map/ppermute | solution.py:181
  31.1 15.0 %collective-permute-start.7 = (f32[16,2048]{1,0:T(8,128)S(1)}, f32[16,2048]{1,0:T(8,128)S(1)}, u32[]{:S(2)}, u32[]{:S(2)}) collective-permute-start(f32[16,2048]{1,0:T(8,128)S(1)} %shard_map.191.r0), channel_id=1, source_target_pairs={{16,0},{32,16},{48,32},{0,48},{17,1},{33,17},{49,33},{1,49},{18,2}... | collective-permute-start | bytes 393224 | tf_op jit(solution)/shard_map/ppermute | solution.py:181
  32.4 4.8 %collective-permute-start.2 = (f32[3,1,512]{2,1,0:T(1,128)S(1)}, f32[3,1,512]{2,1,0:T(1,128)S(1)}, u32[]{:S(2)}, u32[]{:S(2)}) collective-permute-start(f32[3,1,512]{2,1,0:T(1,128)S(1)} %bitcast.34), channel_id=1, source_target_pairs={{192,0},{0,64},{64,128},{128,192},{193,1},{1,65},{65,129},{129,193... | collective-permute-start | bytes 18440 | tf_op jit(solution)/shard_map/ppermute | solution.py:181
  37.3 5.1 %collective-permute-start.1 = (f32[3,1,512]{2,1,0:T(1,128)S(1)}, f32[3,1,512]{2,1,0:T(1,128)S(1)}, u32[]{:S(2)}, u32[]{:S(2)}) collective-permute-start(f32[3,1,512]{2,1,0:T(1,128)S(1)} %bitcast.35), channel_id=1, source_target_pairs={{128,0},{192,64},{0,128},{64,192},{129,1},{193,65},{1,129},{65,193... | collective-permute-start | bytes 18440 | tf_op jit(solution)/shard_map/ppermute | solution.py:181
  42.4 3.6 %collective-permute-start = (f32[3,1,512]{2,1,0:T(1,128)S(1)}, f32[3,1,512]{2,1,0:T(1,128)S(1)}, u32[]{:S(2)}, u32[]{:S(2)}) collective-permute-start(f32[3,1,512]{2,1,0:T(1,128)S(1)} %bitcast.36), channel_id=1, source_target_pairs={{64,0},{128,64},{192,128},{0,192},{65,1},{129,65},{193,129},{1,193... | collective-permute-start | bytes 18440 | tf_op jit(solution)/shard_map/ppermute | solution.py:181
  47.4 12.5 %collective-permute-start.10 = (f32[3,2048]{1,0:T(4,128)S(1)}, f32[3,2048]{1,0:T(4,128)S(1)}, u32[]{:S(2)}, u32[]{:S(2)}) collective-permute-start(f32[3,2048]{1,0:T(4,128)S(1)} %get-tuple-element.30), channel_id=1, source_target_pairs={{192,0},{0,64},{64,128},{128,192},{193,1},{1,65},{65,129},{129,193... | collective-permute-start | bytes 73736 | tf_op jit(solution)/shard_map/ppermute | solution.py:181
  47.7 12.2 %collective-permute-start.11 = (f32[3,2048]{1,0:T(4,128)S(1)}, f32[3,2048]{1,0:T(4,128)S(1)}, u32[]{:S(2)}, u32[]{:S(2)}) collective-permute-start(f32[3,2048]{1,0:T(4,128)S(1)} %get-tuple-element.31), channel_id=1, source_target_pairs={{128,0},{192,64},{0,128},{64,192},{129,1},{193,65},{1,129},{65,193... | collective-permute-start | bytes 73736 | tf_op jit(solution)/shard_map/ppermute | solution.py:181
  51.7 8.2 %collective-permute-start.12 = (f32[3,2048]{1,0:T(4,128)S(1)}, f32[3,2048]{1,0:T(4,128)S(1)}, u32[]{:S(2)}, u32[]{:S(2)}) collective-permute-start(f32[3,2048]{1,0:T(4,128)S(1)} %get-tuple-element.32), channel_id=1, source_target_pairs={{64,0},{128,64},{192,128},{0,192},{65,1},{129,65},{193,129},{1,193... | collective-permute-start | bytes 73736 | tf_op jit(solution)/shard_map/ppermute | solution.py:181
  51.9 9.3 %copy-start = (bf16[1,512,1024]{2,1,0:T(8,128)(2,1)S(1)}, bf16[1,512,1024]{2,1,0:T(8,128)(2,1)}, u32[]{:S(2)}) copy-start(bf16[1,512,1024]{2,1,0:T(8,128)(2,1)} %param.17) | copy-start | bytes 3145732
  51.9 9.3 %copy-start.2 = (bf16[1,1024,768]{2,1,0:T(8,128)(2,1)S(1)}, bf16[1,1024,768]{2,1,0:T(8,128)(2,1)}, u32[]{:S(2)}) copy-start(bf16[1,1024,768]{2,1,0:T(8,128)(2,1)} %param.19) | copy-start | bytes 4718596
  52.0 9.3 %copy-start.4 = (bf16[1,1024,768]{2,1,0:T(8,128)(2,1)S(1)}, bf16[1,1024,768]{2,1,0:T(8,128)(2,1)}, u32[]{:S(2)}) copy-start(bf16[1,1024,768]{2,1,0:T(8,128)(2,1)} %param.20) | copy-start | bytes 4718596
  52.0 9.3 %copy-start.8 = (f32[3,2048]{1,0:T(4,128)S(1)}, f32[3,2048]{1,0:T(4,128)}, u32[]{:S(2)}) copy-start(f32[3,2048]{1,0:T(4,128)} %in_w_ref.1) | copy-start | bytes 73732
  52.0 9.3 %copy-start.10 = (f32[512,5]{0,1:T(8,128)S(1)}, f32[512,5]{0,1:T(8,128)}, u32[]{:S(2)}) copy-start(f32[512,5]{0,1:T(8,128)} %param.28) | copy-start | bytes 30724
  52.0 9.3 %copy-start.11 = (f32[2048]{0:T(1024)S(1)}, f32[2048]{0:T(1024)}, u32[]{:S(2)}) copy-start(f32[2048]{0:T(1024)} %param.27) | copy-start | bytes 24580
  52.0 9.3 %copy-start.13 = (f32[1,3,512]{2,0,1:T(1,128)S(1)}, f32[1,3,512]{2,0,1:T(1,128)}, u32[]{:S(2)}) copy-start(f32[1,3,512]{2,0,1:T(1,128)} %param.24) | copy-start | bytes 18436
  52.0 9.3 %copy-start.14 = (f32[3,4]{1,0:T(4,128)S(1)}, f32[3,4]{1,0:T(4,128)}, u32[]{:S(2)}) copy-start(f32[3,4]{1,0:T(4,128)} %mlp_ref.1) | copy-start | bytes 148
  59.9 1.3 %collective-permute-start.14 = (f32[4,2048]{1,0:T(4,128)S(1)}, f32[4,2048]{1,0:T(4,128)S(1)}, u32[]{:S(2)}, u32[]{:S(2)}) collective-permute-start(f32[4,2048]{1,0:T(4,128)S(1)} %shard_map.195.mine_ref), channel_id=1, source_target_pairs={{0,1},{1,0},{2,3},{3,2},{4,5},{5,4},{6,7},{7,6},{8,9},{9,8},{10,11... | collective-permute-start | bytes 98312 | tf_op jit(solution)/shard_map/ppermute | solution.py:185
  73.2 2.7 %collective-permute-start.15 = (f32[256,1024]{1,0:T(8,128)S(1)}, f32[256,1024]{1,0:T(8,128)S(1)}, u32[]{:S(2)}, u32[]{:S(2)}) collective-permute-start(f32[256,1024]{1,0:T(8,128)S(1)} %get-tuple-element.51), channel_id=1, source_target_pairs={{0,1},{1,0},{2,3},{3,2},{4,5},{5,4},{6,7},{7,6},{8,9},{9,8},{10,11... | collective-permute-start | bytes 3145736 | tf_op jit(solution)/shard_map/ppermute | solution.py:185
  76.5 1.2 %collective-permute-start.16 = (f32[1,128]{1,0:T(1,128)S(1)}, f32[1,128]{1,0:T(1,128)S(1)}, u32[]{:S(2)}, u32[]{:S(2)}) collective-permute-start(f32[1,128]{1,0:T(1,128)S(1)} %shard_map.198.mine_ref), channel_id=1, source_target_pairs={{0,1},{1,0},{2,3},{3,2},{4,5},{5,4},{6,7},{7,6},{8,9},{9,8},{10,11... | collective-permute-start | bytes 1544 | tf_op jit(solution)/shard_map/ppermute | solution.py:185
  78.4 18.5 %all-to-all-start = ((f32[128,1,1]{2,1,0:T(1,128)}), f32[128,1,1]{2,1,0:T(1,128)S(1)}, u32[]{:S(2)}, u32[]{:S(2)}) async-start(f32[128,1,1]{2,1,0:T(1,128)} %shard_map.199), calls=%async_computation | async-start | bytes 131072 | tf_op jit(solution)/shard_map/all_to_all | solution.py:488
  (9 other events, 11.9 us)

commit v7 on v6

--- a/solution.py
+++ b/solution.py
@@ -231,7 +231,9 @@
 
 
 def recurrent(hids, line, info):
-    plane = [line] + [shifted(line, Y, k) for k in (1, 2, 3)]
+    plane = [line]
+    for k in (1, 2, 3):
+        plane.append(shifted(line, Y, k))
     out = (hids[0].shape[0], line.shape[1])
     parts = call(
         recurrent_kernel, (info, *hids, *plane), [IN_VMEM] * 9,
@@ -331,6 +333,8 @@
     table[40:41, :units] = out_w
     copy = pltpu.make_async_copy(table, table_s, sem)
     copy.start()
+    half = theirs.shape[0]
+    theirs[...] = jnp.where(info_ref[3:4, 0:1] == 0, meta_ref[half:], meta_ref[:half])
     copy.wait()
 
     positive = jnp.int32(0)
@@ -385,9 +389,6 @@
             pltpu.make_async_copy(out_u.at[:, at], up_u_hbm.at[:, at], sem_out.at[1, j]),
             pltpu.make_async_copy(out_d.at[at, :], up_d_hbm.at[at, :], sem_out.at[2, j]),
         )
-
-    half = theirs.shape[0]
-    theirs[...] = jnp.where(info_ref[3:4, 0:1] == 0, meta_ref[half:], meta_ref[:half])
 
     def body(j, carry):
         copies = results(j)
@@ -470,7 +471,9 @@
     info = first(place)
     hidden = hidden_state.transpose(1, 0, 2)
     line = recurrent_line(recurrent_weight, info)
-    hids = [hidden] + [shifted(hidden, X, k) for k in (1, 2, 3)]
+    hids = [hidden]
+    for k in (1, 2, 3):
+        hids.append(shifted(hidden, X, k))
     wg, wu, wd = gate_weight[0], up_weight[0], down_weight[0]
     own, p, q, act_t, x_t, param_sq = forward(tokens[0], wg, wu, wd)
     recv = swapped(own)

time: 98.9 us -> 98.9 us (level)
  no operation moved by 1% of the time
where the time goes in v7:
time: 98.9 us; the launch traced here: 97.5 us
  starting transfers between devices  34.4 us (35%)
  Pallas kernels  29.6 us (30%)
  waiting for transfers between devices  21.1 us (21%)
  local copies, waits for them, and re-layouts  10.1 us (10%)
  between operations  1.62 us (2%)
    pallas_call x10, Pallas kernels, call(): pl.pallas_call(body, in_specs=specs, out_specs=out_specs, out_shape=outs,...  29.6 us
    ppermute x9, starting transfers between devices, shifted(): lax.ppermute(array, axis, [((i + shift) % size, i) for i in range(size)])  15.2 us
    unnamed x48, local copies, waits for them, and re-layouts  9.99 us
    all_to_all x1, waiting for transfers between devices, local(): everyone = lax.all_to_all(spread(part, count), TASK, 0, 0, tiled=True)  9.99 us
    ppermute x9, waiting for transfers between devices, shifted(): lax.ppermute(array, axis, [((i + shift) % size, i) for i in range(size)])  8.76 us
    ppermute x4, starting transfers between devices, from_along_z(): return lax.ppermute(array, (Z, SHARD), pairs)  8.55 us
    all_to_all x1, starting transfers between devices, local(): everyone = lax.all_to_all(spread(part, count), TASK, 0, 0, tiled=True)  7.27 us
    ppermute x4, starting transfers between devices, swapped(): return lax.ppermute(array, SHARD, [(0, 1), (1, 0)])  3.31 us
  transfers between devices with their start and end apart: 18, of which 7 were waited for; matrix products, arithmetic and copies ran while one was open for 1% of the time, Pallas kernels for 17%

profile of v7, /device:TPU:32, one launch (start us, length us, event | category | flops | bytes accessed | tf_op | source)
XLA Modules:
  0.0 97.5 jit_solution(1573424553384588873)
XLA Ops:
  0.6 5.9 %collective-permute-start.5 = (f32[4,2048]{1,0:T(4,128)}, f32[4,2048]{1,0:T(4,128)S(1)}, u32[]{:S(2)}, u32[]{:S(2)}) collective-permute-start(f32[4,2048]{1,0:T(4,128)} %own.1), channel_id=1, source_target_pairs={{6,0},{8,2},{10,4},{12,6},{14,8},{0,10},{2,12},{4,14},{13,1},{15,3... | collective-permute-start | bytes 98312 | tf_op jit(solution)/shard_map/ppermute | solution.py:197
  6.6 1.5 %collective-permute-start.4 = (f32[4,2048]{1,0:T(4,128)}, f32[4,2048]{1,0:T(4,128)S(1)}, u32[]{:S(2)}, u32[]{:S(2)}) collective-permute-start(f32[4,2048]{1,0:T(4,128)} %own.1), channel_id=1, source_target_pairs={{4,0},{6,2},{8,4},{10,6},{12,8},{14,10},{0,12},{2,14},{15,1},{1,3}... | collective-permute-start | bytes 98312 | tf_op jit(solution)/shard_map/ppermute | solution.py:197
  8.0 0.7 collective-permute-start.3
  9.2 1.4 %copy-done.1 = bf16[1,1024,768]{2,1,0:T(8,128)(2,1)S(1)} copy-done((bf16[1,1024,768]{2,1,0:T(8,128)(2,1)S(1)}, bf16[1,1024,768]{2,1,0:T(8,128)(2,1)}, u32[]{:S(2)}) %copy-start.1) | copy-done | bytes 1572888
  10.6 1.4 %copy-done.3 = bf16[1,1024,768]{2,1,0:T(8,128)(2,1)S(1)} copy-done((bf16[1,1024,768]{2,1,0:T(8,128)(2,1)S(1)}, bf16[1,1024,768]{2,1,0:T(8,128)(2,1)}, u32[]{:S(2)}) %copy-start.3) | copy-done | bytes 1572888
  12.0 1.4 %copy-done.5 = bf16[1,768,1024]{2,1,0:T(8,128)(2,1)S(1)} copy-done((bf16[1,768,1024]{2,1,0:T(8,128)(2,1)S(1)}, bf16[1,768,1024]{2,1,0:T(8,128)(2,1)}, u32[]{:S(2)}) %copy-start.5) | copy-done | bytes 1572888
  13.4 1.2 %copy-done.15 = bf16[1,512,1024]{2,1,0:T(8,128)(2,1)S(1)} copy-done((bf16[1,512,1024]{2,1,0:T(8,128)(2,1)S(1)}, bf16[1,512,1024]{2,1,0:T(8,128)(2,1)}, u32[]{:S(2)}) %copy-start.15) | copy-done | bytes 1048600
  14.6 4.4 %shard_map.193 = (f32[512,1024]{1,0:T(8,128)S(1)}, f32[512,768]{1,0:T(8,128)S(1)}, f32[512,768]{1,0:T(8,128)S(1)}, bf16[768,512]{1,0:T(8,128)(2,1)S(1)}, bf16[10...) custom-call(bf16[512,1024]{1,0:T(8,128)(2,1)S(1)} %bitcast.39, bf16[1024,768]{1,0:T(8,128)(2,1)S(1)} %bitcast.24, ...), custom_call_target="tpu_custom_call" | custom-call | flops 2415919104 | tf_op jit(solution)/shard_map/pallas_call | solution.py:56
  19.1 1.1 %copy-done.17 = f32[512,768]{1,0:T(8,128)} copy-done((f32[512,768]{1,0:T(8,128)}, f32[512,768]{1,0:T(8,128)S(1)}, u32[]{:S(2)}) %copy-start.17) | copy-done | bytes 1572888
  20.2 1.1 %copy-done.19 = f32[512,768]{1,0:T(8,128)} copy-done((f32[512,768]{1,0:T(8,128)}, f32[512,768]{1,0:T(8,128)S(1)}, u32[]{:S(2)}) %copy-start.19) | copy-done | bytes 1572888
  21.4 0.9 copy-done.21
  22.2 2.8 %collective-permute-start.13 = (f32[512,1024]{1,0:T(8,128)S(1)}, f32[512,1024]{1,0:T(8,128)}, u32[]{:S(2)}, u32[]{:S(2)}) collective-permute-start(f32[512,1024]{1,0:T(8,128)S(1)} %get-tuple-element.33.own_ref), channel_id=1, source_target_pairs={{0,1},{1,0},{2,3},{3,2},{4,5},{5,4},{6,7},{7,6},{8,9},{9,8},{10,11... | collective-permute-start | bytes 6291464 | tf_op jit(solution)/shard_map/ppermute | solution.py:185
  26.5 1.7 %collective-permute-start.9 = (f32[16,2048]{1,0:T(8,128)S(1)}, f32[16,2048]{1,0:T(8,128)S(1)}, u32[]{:S(2)}, u32[]{:S(2)}) collective-permute-start(f32[16,2048]{1,0:T(8,128)S(1)} %shard_map.191.r0), channel_id=1, source_target_pairs={{48,0},{0,16},{16,32},{32,48},{49,1},{1,17},{17,33},{33,49},{50,2}... | collective-permute-start | bytes 393224 | tf_op jit(solution)/shard_map/ppermute | solution.py:181
  28.2 2.9 %collective-permute-start.8 = (f32[16,2048]{1,0:T(8,128)S(1)}, f32[16,2048]{1,0:T(8,128)S(1)}, u32[]{:S(2)}, u32[]{:S(2)}) collective-permute-start(f32[16,2048]{1,0:T(8,128)S(1)} %shard_map.191.r0), channel_id=1, source_target_pairs={{32,0},{48,16},{0,32},{16,48},{33,1},{49,17},{1,33},{17,49},{34,2}... | collective-permute-start | bytes 393224 | tf_op jit(solution)/shard_map/ppermute | solution.py:181
  31.1 1.3 %collective-permute-start.7 = (f32[16,2048]{1,0:T(8,128)S(1)}, f32[16,2048]{1,0:T(8,128)S(1)}, u32[]{:S(2)}, u32[]{:S(2)}) collective-permute-start(f32[16,2048]{1,0:T(8,128)S(1)} %shard_map.191.r0), channel_id=1, source_target_pairs={{16,0},{32,16},{48,32},{0,48},{17,1},{33,17},{49,33},{1,49},{18,2}... | collective-permute-start | bytes 393224 | tf_op jit(solution)/shard_map/ppermute | solution.py:181
  32.4 1.5 %collective-permute-start.2 = (f32[3,1,512]{2,1,0:T(1,128)S(1)}, f32[3,1,512]{2,1,0:T(1,128)S(1)}, u32[]{:S(2)}, u32[]{:S(2)}) collective-permute-start(f32[3,1,512]{2,1,0:T(1,128)S(1)} %bitcast.34), channel_id=1, source_target_pairs={{192,0},{0,64},{64,128},{128,192},{193,1},{1,65},{65,129},{129,193... | collective-permute-start | bytes 18440 | tf_op jit(solution)/shard_map/ppermute | solution.py:181
  33.9 3.3 %collective-permute-done.2.h3 = f32[3,1,512]{2,1,0:T(1,128)S(1)} collective-permute-done((f32[3,1,512]{2,1,0:T(1,128)S(1)}, f32[3,1,512]{2,1,0:T(1,128)S(1)}, u32[]{:S(2)}, u32[]{:S(2)}) %collective-permute-start.2) | collective-permute-done | bytes 6176 | tf_op jit(solution)/shard_map/ppermute | solution.py:181
  37.3 1.8 %collective-permute-start.1 = (f32[3,1,512]{2,1,0:T(1,128)S(1)}, f32[3,1,512]{2,1,0:T(1,128)S(1)}, u32[]{:S(2)}, u32[]{:S(2)}) collective-permute-start(f32[3,1,512]{2,1,0:T(1,128)S(1)} %bitcast.35), channel_id=1, source_target_pairs={{128,0},{192,64},{0,128},{64,192},{129,1},{193,65},{1,129},{65,193... | collective-permute-start | bytes 18440 | tf_op jit(solution)/shard_map/ppermute | solution.py:181
  39.1 3.3 %collective-permute-done.1.h2 = f32[3,1,512]{2,1,0:T(1,128)S(1)} collective-permute-done((f32[3,1,512]{2,1,0:T(1,128)S(1)}, f32[3,1,512]{2,1,0:T(1,128)S(1)}, u32[]{:S(2)}, u32[]{:S(2)}) %collective-permute-start.1) | collective-permute-done | bytes 6176 | tf_op jit(solution)/shard_map/ppermute | solution.py:181
  42.4 1.5 %collective-permute-start = (f32[3,1,512]{2,1,0:T(1,128)S(1)}, f32[3,1,512]{2,1,0:T(1,128)S(1)}, u32[]{:S(2)}, u32[]{:S(2)}) collective-permute-start(f32[3,1,512]{2,1,0:T(1,128)S(1)} %bitcast.36), channel_id=1, source_target_pairs={{64,0},{128,64},{192,128},{0,192},{65,1},{129,65},{193,129},{1,193... | collective-permute-start | bytes 18440 | tf_op jit(solution)/shard_map/ppermute | solution.py:181
  44.0 2.1 %collective-permute-done.h1 = f32[3,1,512]{2,1,0:T(1,128)S(1)} collective-permute-done((f32[3,1,512]{2,1,0:T(1,128)S(1)}, f32[3,1,512]{2,1,0:T(1,128)S(1)}, u32[]{:S(2)}, u32[]{:S(2)}) %collective-permute-start) | collective-permute-done | bytes 6176 | tf_op jit(solution)/shard_map/ppermute | solution.py:181
  46.1 1.3 %shard_map.192 = (f32[3,2048]{1,0:T(4,128)S(1)}, f32[3,2048]{1,0:T(4,128)S(1)}, f32[3,2048]{1,0:T(4,128)S(1)}, f32[3,2048]{1,0:T(4,128)S(1)}) custom-call(s32[8,128]{1,0:T(8,128)S(1)} %shard_map.190.info_ref, f32[3,1,512]{2,1,0:T(1,128)S(1)} %bitcast.37, f32[3,1,512]{2,1,0:T(1,128)S(1)} %collective-permute-done.h1, ...), custom_call_target="tpu_custom_call" | custom-call | flops 4194304 | tf_op jit(solution)/shard_map/pallas_call | solution.py:56
  47.7 4.0 %collective-permute-start.11 = (f32[3,2048]{1,0:T(4,128)S(1)}, f32[3,2048]{1,0:T(4,128)S(1)}, u32[]{:S(2)}, u32[]{:S(2)}) collective-permute-start(f32[3,2048]{1,0:T(4,128)S(1)} %get-tuple-element.31), channel_id=1, source_target_pairs={{128,0},{192,64},{0,128},{64,192},{129,1},{193,65},{1,129},{65,193... | collective-permute-start | bytes 73736 | tf_op jit(solution)/shard_map/ppermute | solution.py:181
  52.0 7.8 %shard_map.194 = (f32[1024,768]{1,0:T(8,128)S(1)}, f32[1024,768]{1,0:T(8,128)S(1)}, f32[768,1024]{1,0:T(8,128)S(1)}, f32[16,128]{1,0:T(8,128)S(1)}) custom-call(f32[512,1024]{1,0:T(8,128)S(1)} %get-tuple-element.33.own_ref, f32[512,1024]{1,0:T(8,128)} %collective-permute-done.13.recv_ref, bf16[512,1024]{1,0:T(8,128)(2,1)S(1)} %bitcast.40, ...), custom_call_target="tpu_custom_call" | custom-call | flops 3221225472 | tf_op jit(solution)/shard_map/pallas_call | solution.py:56
  60.0 1.2 %collective-permute-done.14.theirs_ref = f32[4,2048]{1,0:T(4,128)S(1)} collective-permute-done((f32[4,2048]{1,0:T(4,128)S(1)}, f32[4,2048]{1,0:T(4,128)S(1)}, u32[]{:S(2)}, u32[]{:S(2)}) %collective-permute-start.14) | collective-permute-done | bytes 32800 | tf_op jit(solution)/shard_map/ppermute | solution.py:185
  61.3 11.9 %shard_map.196 = (bf16[1024,768]{1,0:T(8,128)(2,1)}, bf16[1024,768]{1,0:T(8,128)(2,1)}, bf16[768,1024]{1,0:T(8,128)(2,1)}, f32[3,1,512]{2,1,0:T(1,128)S(1)}, f32...) custom-call(s32[8,128]{1,0:T(8,128)S(1)} %shard_map.190.info_ref, ...), custom_call_target="tpu_custom_call" | custom-call | flops 2415919104 | tf_op jit(solution)/shard_map/pallas_call | solution.py:56
  73.4 2.3 %shard_map.197.keep_ref = f32[256,1024]{1,0:T(8,128)S(1)} custom-call(s32[8,128]{1,0:T(8,128)S(1)} %shard_map.190.info_ref, bf16[512,1024]{1,0:T(8,128)(2,1)S(1)} %bitcast.23, bf16[1024,768]{1,0:T(8,128)(2,1)S(1)} %get-tuple-element.48.new_g, bf16[1024,768]{1,0:T(8,128)(2,1)S(1)} %get-tuple-element.49.new_u, bf16[768,1024]{1,0:T(8,128)(2,1)S(1)} %get-tuple-element.50.new_d), custom_call_target="tpu_custom_call" | custom-call | flops 1073741824 | tf_op jit(solution)/shard_map/pallas_call | solution.py:56
  76.7 1.0 collective-permute-done.16.theirs_ref
  77.7 0.7 shard_map.199
  78.3 7.3 %all-to-all-start = ((f32[128,1,1]{2,1,0:T(1,128)}), f32[128,1,1]{2,1,0:T(1,128)S(1)}, u32[]{:S(2)}, u32[]{:S(2)}) async-start(f32[128,1,1]{2,1,0:T(1,128)} %shard_map.199), calls=%async_computation | async-start | bytes 131072 | tf_op jit(solution)/shard_map/all_to_all | solution.py:491
  86.8 10.0 %all-to-all-done = f32[128,1,1]{2,1,0:T(1,128)S(1)} async-done(((f32[128,1,1]{2,1,0:T(1,128)}), f32[128,1,1]{2,1,0:T(1,128)S(1)}, u32[]{:S(2)}, u32[]{:S(2)}) %all-to-all-start) | async-done | bytes 544 | tf_op jit(solution)/shard_map/all_to_all | solution.py:491
  96.8 0.7 reduce_sum.9
  (64 shorter events, 4.5 us)
Async XLA Ops:
  0.6 25.7 %collective-permute-start.5 = (f32[4,2048]{1,0:T(4,128)}, f32[4,2048]{1,0:T(4,128)S(1)}, u32[]{:S(2)}, u32[]{:S(2)}) collective-permute-start(f32[4,2048]{1,0:T(4,128)} %own.1), channel_id=1, source_target_pairs={{6,0},{8,2},{10,4},{12,6},{14,8},{0,10},{2,12},{4,14},{13,1},{15,3... | collective-permute-start | bytes 98312 | tf_op jit(solution)/shard_map/ppermute | solution.py:197
  6.6 19.8 %collective-permute-start.4 = (f32[4,2048]{1,0:T(4,128)}, f32[4,2048]{1,0:T(4,128)S(1)}, u32[]{:S(2)}, u32[]{:S(2)}) collective-permute-start(f32[4,2048]{1,0:T(4,128)} %own.1), channel_id=1, source_target_pairs={{4,0},{6,2},{8,4},{10,6},{12,8},{14,10},{0,12},{2,14},{15,1},{1,3}... | collective-permute-start | bytes 98312 | tf_op jit(solution)/shard_map/ppermute | solution.py:197
  8.0 18.3 %collective-permute-start.3 = (f32[4,2048]{1,0:T(4,128)}, f32[4,2048]{1,0:T(4,128)S(1)}, u32[]{:S(2)}, u32[]{:S(2)}) collective-permute-start(f32[4,2048]{1,0:T(4,128)} %own.1), channel_id=1, source_target_pairs={{3,1},{5,3},{7,5},{9,7},{11,9},{13,11},{15,13},{1,15},{19,17},{21,... | collective-permute-start | bytes 98312 | tf_op jit(solution)/shard_map/ppermute | solution.py:197
  8.7 17.7 %collective-permute-start.6 = (f32[4,2048]{1,0:T(4,128)}, f32[4,2048]{1,0:T(4,128)S(1)}, u32[]{:S(2)}, u32[]{:S(2)}) collective-permute-start(f32[4,2048]{1,0:T(4,128)} %own.1), channel_id=1, source_target_pairs={{8,0},{10,2},{12,4},{14,6},{0,8},{2,10},{4,12},{6,14},{11,1},{13,3... | collective-permute-start | bytes 98312 | tf_op jit(solution)/shard_map/ppermute | solution.py:197
  22.2 29.7 %collective-permute-start.13 = (f32[512,1024]{1,0:T(8,128)S(1)}, f32[512,1024]{1,0:T(8,128)}, u32[]{:S(2)}, u32[]{:S(2)}) collective-permute-start(f32[512,1024]{1,0:T(8,128)S(1)} %get-tuple-element.33.own_ref), channel_id=1, source_target_pairs={{0,1},{1,0},{2,3},{3,2},{4,5},{5,4},{6,7},{7,6},{8,9},{9,8},{10,11... | collective-permute-start | bytes 6291464 | tf_op jit(solution)/shard_map/ppermute | solution.py:185
  25.7 6.7 %copy-start.12 = (f32[1,3,512]{2,0,1:T(1,128)S(1)}, f32[1,3,512]{2,0,1:T(1,128)}, u32[]{:S(2)}) copy-start(f32[1,3,512]{2,0,1:T(1,128)} %param.23) | copy-start | bytes 18436
  25.7 26.2 %copy-start.6 = (bf16[1,768,1024]{2,1,0:T(8,128)(2,1)S(1)}, bf16[1,768,1024]{2,1,0:T(8,128)(2,1)}, u32[]{:S(2)}) copy-start(bf16[1,768,1024]{2,1,0:T(8,128)(2,1)} %param.21) | copy-start | bytes 4718596
  25.7 26.2 %copy-start.16 = (bf16[1,512,1024]{2,1,0:T(8,128)(2,1)S(1)}, bf16[1,512,1024]{2,1,0:T(8,128)(2,1)}, u32[]{:S(2)}) copy-start(bf16[1,512,1024]{2,1,0:T(8,128)(2,1)} %param.16) | copy-start | bytes 3145732
  25.7 26.2 %copy-start.18 = (f32[512,768]{1,0:T(8,128)S(1)}, f32[512,768]{1,0:T(8,128)}, u32[]{:S(2)}) copy-start(f32[512,768]{1,0:T(8,128)} %copy-done.17) | copy-start | bytes 4718596
  25.8 26.2 %copy-start.20 = (f32[512,768]{1,0:T(8,128)S(1)}, f32[512,768]{1,0:T(8,128)}, u32[]{:S(2)}) copy-start(f32[512,768]{1,0:T(8,128)} %copy-done.19) | copy-start | bytes 4718596
  25.8 26.2 %copy-start.22 = (bf16[768,512]{1,0:T(8,128)(2,1)S(1)}, bf16[768,512]{1,0:T(8,128)(2,1)}, u32[]{:S(2)}) copy-start(bf16[768,512]{1,0:T(8,128)(2,1)} %copy-done.21) | copy-start | bytes 2359300
  26.5 19.5 %collective-permute-start.9 = (f32[16,2048]{1,0:T(8,128)S(1)}, f32[16,2048]{1,0:T(8,128)S(1)}, u32[]{:S(2)}, u32[]{:S(2)}) collective-permute-start(f32[16,2048]{1,0:T(8,128)S(1)} %shard_map.191.r0), channel_id=1, source_target_pairs={{48,0},{0,16},{16,32},{32,48},{49,1},{1,17},{17,33},{33,49},{50,2}... | collective-permute-start | bytes 393224 | tf_op jit(solution)/shard_map/ppermute | solution.py:181
  28.2 17.9 %collective-permute-start.8 = (f32[16,2048]{1,0:T(8,128)S(1)}, f32[16,2048]{1,0:T(8,128)S(1)}, u32[]{:S(2)}, u32[]{:S(2)}) collective-permute-start(f32[16,2048]{1,0:T(8,128)S(1)} %shard_map.191.r0), channel_id=1, source_target_pairs={{32,0},{48,16},{0,32},{16,48},{33,1},{49,17},{1,33},{17,49},{34,2}... | collective-permute-start | bytes 393224 | tf_op jit(solution)/shard_map/ppermute | solution.py:181
  31.1 15.0 %collective-permute-start.7 = (f32[16,2048]{1,0:T(8,128)S(1)}, f32[16,2048]{1,0:T(8,128)S(1)}, u32[]{:S(2)}, u32[]{:S(2)}) collective-permute-start(f32[16,2048]{1,0:T(8,128)S(1)} %shard_map.191.r0), channel_id=1, source_target_pairs={{16,0},{32,16},{48,32},{0,48},{17,1},{33,17},{49,33},{1,49},{18,2}... | collective-permute-start | bytes 393224 | tf_op jit(solution)/shard_map/ppermute | solution.py:181
  32.4 4.8 %collective-permute-start.2 = (f32[3,1,512]{2,1,0:T(1,128)S(1)}, f32[3,1,512]{2,1,0:T(1,128)S(1)}, u32[]{:S(2)}, u32[]{:S(2)}) collective-permute-start(f32[3,1,512]{2,1,0:T(1,128)S(1)} %bitcast.34), channel_id=1, source_target_pairs={{192,0},{0,64},{64,128},{128,192},{193,1},{1,65},{65,129},{129,193... | collective-permute-start | bytes 18440 | tf_op jit(solution)/shard_map/ppermute | solution.py:181
  37.3 5.1 %collective-permute-start.1 = (f32[3,1,512]{2,1,0:T(1,128)S(1)}, f32[3,1,512]{2,1,0:T(1,128)S(1)}, u32[]{:S(2)}, u32[]{:S(2)}) collective-permute-start(f32[3,1,512]{2,1,0:T(1,128)S(1)} %bitcast.35), channel_id=1, source_target_pairs={{128,0},{192,64},{0,128},{64,192},{129,1},{193,65},{1,129},{65,193... | collective-permute-start | bytes 18440 | tf_op jit(solution)/shard_map/ppermute | solution.py:181
  42.4 3.6 %collective-permute-start = (f32[3,1,512]{2,1,0:T(1,128)S(1)}, f32[3,1,512]{2,1,0:T(1,128)S(1)}, u32[]{:S(2)}, u32[]{:S(2)}) collective-permute-start(f32[3,1,512]{2,1,0:T(1,128)S(1)} %bitcast.36), channel_id=1, source_target_pairs={{64,0},{128,64},{192,128},{0,192},{65,1},{129,65},{193,129},{1,193... | collective-permute-start | bytes 18440 | tf_op jit(solution)/shard_map/ppermute | solution.py:181
  47.4 12.5 %collective-permute-start.10 = (f32[3,2048]{1,0:T(4,128)S(1)}, f32[3,2048]{1,0:T(4,128)S(1)}, u32[]{:S(2)}, u32[]{:S(2)}) collective-permute-start(f32[3,2048]{1,0:T(4,128)S(1)} %get-tuple-element.30), channel_id=1, source_target_pairs={{192,0},{0,64},{64,128},{128,192},{193,1},{1,65},{65,129},{129,193... | collective-permute-start | bytes 73736 | tf_op jit(solution)/shard_map/ppermute | solution.py:181
  47.7 12.2 %collective-permute-start.11 = (f32[3,2048]{1,0:T(4,128)S(1)}, f32[3,2048]{1,0:T(4,128)S(1)}, u32[]{:S(2)}, u32[]{:S(2)}) collective-permute-start(f32[3,2048]{1,0:T(4,128)S(1)} %get-tuple-element.31), channel_id=1, source_target_pairs={{128,0},{192,64},{0,128},{64,192},{129,1},{193,65},{1,129},{65,193... | collective-permute-start | bytes 73736 | tf_op jit(solution)/shard_map/ppermute | solution.py:181
  51.7 8.2 %collective-permute-start.12 = (f32[3,2048]{1,0:T(4,128)S(1)}, f32[3,2048]{1,0:T(4,128)S(1)}, u32[]{:S(2)}, u32[]{:S(2)}) collective-permute-start(f32[3,2048]{1,0:T(4,128)S(1)} %get-tuple-element.32), channel_id=1, source_target_pairs={{64,0},{128,64},{192,128},{0,192},{65,1},{129,65},{193,129},{1,193... | collective-permute-start | bytes 73736 | tf_op jit(solution)/shard_map/ppermute | solution.py:181
  51.9 9.3 %copy-start = (bf16[1,512,1024]{2,1,0:T(8,128)(2,1)S(1)}, bf16[1,512,1024]{2,1,0:T(8,128)(2,1)}, u32[]{:S(2)}) copy-start(bf16[1,512,1024]{2,1,0:T(8,128)(2,1)} %param.17) | copy-start | bytes 3145732
  51.9 9.3 %copy-start.2 = (bf16[1,1024,768]{2,1,0:T(8,128)(2,1)S(1)}, bf16[1,1024,768]{2,1,0:T(8,128)(2,1)}, u32[]{:S(2)}) copy-start(bf16[1,1024,768]{2,1,0:T(8,128)(2,1)} %param.19) | copy-start | bytes 4718596
  52.0 9.3 %copy-start.4 = (bf16[1,1024,768]{2,1,0:T(8,128)(2,1)S(1)}, bf16[1,1024,768]{2,1,0:T(8,128)(2,1)}, u32[]{:S(2)}) copy-start(bf16[1,1024,768]{2,1,0:T(8,128)(2,1)} %param.20) | copy-start | bytes 4718596
  52.0 9.3 %copy-start.8 = (f32[3,2048]{1,0:T(4,128)S(1)}, f32[3,2048]{1,0:T(4,128)}, u32[]{:S(2)}) copy-start(f32[3,2048]{1,0:T(4,128)} %in_w_ref.1) | copy-start | bytes 73732
  52.0 9.3 %copy-start.10 = (f32[512,5]{0,1:T(8,128)S(1)}, f32[512,5]{0,1:T(8,128)}, u32[]{:S(2)}) copy-start(f32[512,5]{0,1:T(8,128)} %param.28) | copy-start | bytes 30724
  52.0 9.3 %copy-start.11 = (f32[2048]{0:T(1024)S(1)}, f32[2048]{0:T(1024)}, u32[]{:S(2)}) copy-start(f32[2048]{0:T(1024)} %param.27) | copy-start | bytes 24580
  52.0 9.3 %copy-start.13 = (f32[1,3,512]{2,0,1:T(1,128)S(1)}, f32[1,3,512]{2,0,1:T(1,128)}, u32[]{:S(2)}) copy-start(f32[1,3,512]{2,0,1:T(1,128)} %param.24) | copy-start | bytes 18436
  52.0 9.3 %copy-start.14 = (f32[3,4]{1,0:T(4,128)S(1)}, f32[3,4]{1,0:T(4,128)}, u32[]{:S(2)}) copy-start(f32[3,4]{1,0:T(4,128)} %mlp_ref.1) | copy-start | bytes 148
  59.9 1.3 %collective-permute-start.14 = (f32[4,2048]{1,0:T(4,128)S(1)}, f32[4,2048]{1,0:T(4,128)S(1)}, u32[]{:S(2)}, u32[]{:S(2)}) collective-permute-start(f32[4,2048]{1,0:T(4,128)S(1)} %shard_map.195.mine_ref), channel_id=1, source_target_pairs={{0,1},{1,0},{2,3},{3,2},{4,5},{5,4},{6,7},{7,6},{8,9},{9,8},{10,11... | collective-permute-start | bytes 98312 | tf_op jit(solution)/shard_map/ppermute | solution.py:185
  73.2 2.7 %collective-permute-start.15 = (f32[256,1024]{1,0:T(8,128)S(1)}, f32[256,1024]{1,0:T(8,128)S(1)}, u32[]{:S(2)}, u32[]{:S(2)}) collective-permute-start(f32[256,1024]{1,0:T(8,128)S(1)} %get-tuple-element.51), channel_id=1, source_target_pairs={{0,1},{1,0},{2,3},{3,2},{4,5},{5,4},{6,7},{7,6},{8,9},{9,8},{10,11... | collective-permute-start | bytes 3145736 | tf_op jit(solution)/shard_map/ppermute | solution.py:185
  76.5 1.2 %collective-permute-start.16 = (f32[1,128]{1,0:T(1,128)S(1)}, f32[1,128]{1,0:T(1,128)S(1)}, u32[]{:S(2)}, u32[]{:S(2)}) collective-permute-start(f32[1,128]{1,0:T(1,128)S(1)} %shard_map.198.mine_ref), channel_id=1, source_target_pairs={{0,1},{1,0},{2,3},{3,2},{4,5},{5,4},{6,7},{7,6},{8,9},{9,8},{10,11... | collective-permute-start | bytes 1544 | tf_op jit(solution)/shard_map/ppermute | solution.py:185
  78.3 18.5 %all-to-all-start = ((f32[128,1,1]{2,1,0:T(1,128)}), f32[128,1,1]{2,1,0:T(1,128)S(1)}, u32[]{:S(2)}, u32[]{:S(2)}) async-start(f32[128,1,1]{2,1,0:T(1,128)} %shard_map.199), calls=%async_computation | async-start | bytes 131072 | tf_op jit(solution)/shard_map/all_to_all | solution.py:491
  (9 other events, 11.9 us)
